TPU v7x, 32 devices: a whole 2x2x4 slice. The times are simulated.
32 devices in a mesh: dp: 8 (over z, x), mp: 4 (over y, core).
Axes of the slice: x: 2, y: 2, z: 4, core: 2. Of those that a mesh axis runs over, the one named last changes fastest.
Arguments:
- hidden_in: bfloat16 [8192, 1024], P(('dp', 'mp')), may hold values from -6 to 6
- seg_lengths: int32 [8, 8], P('dp'), may hold values from 1 to 256, 1024 in all within a row
- partner: int32 [8, 8], P('dp'), may hold values from 0 to 7, as said below
- qkv_weight: float32 [2, 1024, 3, 1024], P(None, 'dp', None, 'mp'), may hold values from -0.1875 to 0.1875
- out_weight: float32 [2, 1024, 1024], P(None, 'mp', 'dp'), may hold values from -2 to 2
- up_weight: float32 [2, 1024, 4096], P(None, 'dp', 'mp'), may hold values from -0.1875 to 0.1875
- down_weight: float32 [2, 4096, 1024], P(None, 'mp', 'dp'), may hold values from -0.09375 to 0.09375
- norm_params: float32 [2, 2, 2, 1024], P(None, None, None, 'dp'), may hold values from -0.6 to 1.15, as said below
- emb_weight: float32 [1024, 128], P('dp'), may hold values from -0.1875 to 0.1875
- log_scale: float32 [1], replicated, may hold values from 2.5 to 3.2
- qkv_moments: float32 [2, 2, 1024, 3, 1024], P(None, None, 'dp', None, 'mp'), as said below
- out_moments: float32 [2, 2, 1024, 1024], P(None, None, 'mp', 'dp'), as said below
- up_moments: float32 [2, 2, 1024, 4096], P(None, None, 'dp', 'mp'), as said below
- down_moments: float32 [2, 2, 4096, 1024], P(None, None, 'mp', 'dp'), as said below
- norm_moments: float32 [2, 2, 2, 2, 1024], P(None, None, None, None, 'dp'), as said below
- emb_moments: float32 [2, 1024, 128], P(None, 'dp'), as said below
- scale_moments: float32 [2, 1], replicated, as said below
Outputs:
- hidden_out: float32 [8192, 1024], P(('dp', 'mp'))
- hidden_grad: float32 [8192, 1024], P(('dp', 'mp'))
- loss: float32 [1], replicated
- clip_norm: float32 [1], replicated
- qkv_new: float32 [2, 1024, 3, 1024], P(None, 'dp', None, 'mp')
- qkv_first: float32 [2, 1024, 3, 1024], P(None, 'dp', None, 'mp')
- qkv_second: float32 [2, 1024, 3, 1024], P(None, 'dp', None, 'mp')
- out_new: float32 [2, 1024, 1024], P(None, 'mp', 'dp')
- out_first: float32 [2, 1024, 1024], P(None, 'mp', 'dp')
- out_second: float32 [2, 1024, 1024], P(None, 'mp', 'dp')
- up_new: float32 [2, 1024, 4096], P(None, 'dp', 'mp')
- up_first: float32 [2, 1024, 4096], P(None, 'dp', 'mp')
- up_second: float32 [2, 1024, 4096], P(None, 'dp', 'mp')
- down_new: float32 [2, 4096, 1024], P(None, 'mp', 'dp')
- down_first: float32 [2, 4096, 1024], P(None, 'mp', 'dp')
- down_second: float32 [2, 4096, 1024], P(None, 'mp', 'dp')
- norm_new: float32 [2, 2, 2, 1024], P(None, None, None, 'dp')
- norm_first: float32 [2, 2, 2, 1024], P(None, None, None, 'dp')
- norm_second: float32 [2, 2, 2, 1024], P(None, None, None, 'dp')
- emb_new: float32 [1024, 128], P('dp')
- emb_first: float32 [1024, 128], P('dp')
- emb_second: float32 [1024, 128], P('dp')
- scale_new: float32 [1], replicated
- scale_first: float32 [1], replicated
- scale_second: float32 [1], replicated
Inputs may be any that keep to these rules, and one draw needn't show every extreme that they name: `seg_lengths`: the 8 lengths of a row sum to 1024. The segments of a row come in pairs: partner of s is never s, and the partner of the partner of s is s. `norm_params`: gains near 1 at index 0 of the third dimension, biases of both signs at index 1. `qkv_moments`: index 0 holds first moments of both signs, index 1 positive second moments. `out_moments`: index 0 holds first moments of both signs, index 1 positive second moments. `up_moments`: index 0 holds first moments of both signs, index 1 positive second moments. `down_moments`: index 0 holds first moments of both signs, index 1 positive second moments. `norm_moments`: index 0 holds first moments of both signs, index 1 positive second moments. `emb_moments`: index 0 holds first moments of both signs, index 1 positive second moments. `scale_moments`: index 0 holds the first moment, index 1 the positive second moment.
All inputs are finite; a program needn't handle non-finite values.
Results may differ from a plain program's by a relative error of at most 0.018.
Values may be sent and summed in bfloat16 or wider, within the bound.
No kernel may reach another device: no remote copies, remote signals or barrier semaphores. Data moves between devices by JAX's collectives and lax.ppermute only.
A program may use at most 192 MiB of HBM per device.

v0:
```python
import math

import jax
import jax.numpy as jnp
from jax import lax
from jax.sharding import PartitionSpec as P

D = 1024
HEAD_DIM = 64
FF = 4096
EMB = 128
LAYERS = 2
STEP = 5
ROW_LEN = 1024
SEGS = 8


sharpness = 0.05
clip_limit = 1.0
best = lax.Precision.HIGHEST


def plain_dot(left, right):
    return jnp.dot(left, right, preferred_element_type=jnp.float32)


def inner_dot(left, right):
    return lax.dot_general(
        left, right, (((0,), (0,)), ((), ())), preferred_element_type=jnp.float32
    )


def outer_dot(left, right):
    return lax.dot_general(
        left, right, (((1,), (1,)), ((), ())), preferred_element_type=jnp.float32
    )


def layer_norm(values, gain, bias):
    centered = values - jnp.mean(values, axis=-1, keepdims=True)
    spread = jnp.mean(centered * centered, axis=-1, keepdims=True)
    return centered * lax.rsqrt(spread + 1e-05) * gain + bias


def row_layout(lengths):
    ends = jnp.cumsum(lengths)
    places = jnp.arange(ROW_LEN, dtype=jnp.int32)
    after = places[:, None] >= ends[None, :]
    segment = jnp.sum(after.astype(jnp.int32), axis=1)
    starts = jnp.sum(jnp.where(after, lengths[None, :], 0), axis=1)
    return (segment, places - starts)


def rotary_tables(offsets):
    frequency = jnp.exp(
        jnp.arange(HEAD_DIM // 2, dtype=jnp.float32) * (-2.0 * math.log(10000.0) / HEAD_DIM)
    )
    angles = offsets.astype(jnp.float32)[..., None] * frequency
    return (jnp.cos(angles), jnp.sin(angles))


def rotate(values, cosines, sines):
    half_dim = values.shape[-1] // 2
    leading = values[..., :half_dim]
    trailing = values[..., half_dim:]
    return jnp.concatenate(
        [leading * cosines - trailing * sines, trailing * cosines + leading * sines], axis=-1
    )


def row_loss(embedded, log_scale, segment, lengths, partner):
    segment_count = lengths.shape[0]
    labels = jnp.arange(segment_count, dtype=jnp.int32)
    member = (segment[:, None] == labels[None, :]).astype(jnp.float32)
    scaling = jnp.exp(log_scale[0])
    columns = jnp.arange(embedded.shape[1], dtype=jnp.int32)
    allowed = labels[:, None] != labels[None, :]
    chosen = partner[:, None] == labels[None, :]
    counts_f = lengths.astype(jnp.float32)[:, None]
    result = jnp.zeros((), jnp.float32)
    for width_now in (EMB, EMB * 3 // 4, EMB // 2):
        keep_cols = (columns < width_now).astype(jnp.float32)
        masked = embedded * keep_cols[None, :]
        unit_rows = masked * lax.rsqrt(jnp.sum(masked * masked, axis=1, keepdims=True) + 1e-06)
        similar = jnp.dot(unit_rows, unit_rows.T, precision=best)
        soft_max = (
            sharpness
            * jnp.log(jnp.dot(jnp.exp((similar - 1.0) / sharpness), member, precision=best))
            + 1.0
        )
        scores = jnp.dot(member.T, soft_max, precision=best) / counts_f
        logits = jnp.where(allowed, scaling * scores, -1e30)
        highest = jnp.max(logits, axis=1, keepdims=True)
        log_total = highest[:, 0] + jnp.log(jnp.sum(jnp.exp(logits - highest), axis=1))
        picked = jnp.sum(jnp.where(chosen, logits, 0.0), axis=1)
        result = result + jnp.sum(log_total - picked)
    return result


def adamw_update(master, moments, grad, factor, rate, step_f):
    scaled = grad * factor
    moment_one = 0.9 * moments[0] + 0.1 * scaled
    moment_two = 0.95 * moments[1] + 0.05 * scaled * scaled
    one_hat = moment_one / (1.0 - jnp.power(0.9, step_f))
    two_hat = moment_two / (1.0 - jnp.power(0.95, step_f))
    updated = master - rate * (one_hat / (jnp.sqrt(two_hat) + 1e-08) + 0.01 * master)
    return (updated, moment_one, moment_two)


def attend_forward(queries, key_rows, value_rows, segment):
    block_rows = min(512, ROW_LEN)
    block_count = queries.shape[0] // block_rows
    scaling = HEAD_DIM ** (-0.5)

    def one_block(block_at):
        begin_row = block_at * block_rows
        rows_here = lax.dynamic_slice_in_dim(queries, begin_row, block_rows, 0)
        own_segment = lax.dynamic_slice_in_dim(segment, begin_row, block_rows, 0)
        scores = (
            jnp.einsum("qhd,khd->hqk", rows_here, key_rows, preferred_element_type=jnp.float32)
            * scaling
        )
        scores = jnp.where((own_segment[:, None] == segment[None, :])[None], scores, -1e30)
        highest = jnp.max(scores, axis=-1, keepdims=True)
        weights_exp = jnp.exp(scores - highest)
        totals = jnp.sum(weights_exp, axis=-1, keepdims=True)
        probs = (weights_exp / totals).astype(jnp.bfloat16)
        mixture = jnp.einsum("hqk,khd->qhd", probs, value_rows, preferred_element_type=jnp.float32)
        return (mixture, (highest + jnp.log(totals))[..., 0])

    mixture, log_totals = lax.map(one_block, jnp.arange(block_count, dtype=jnp.int32))
    return (mixture.reshape(queries.shape[0], queries.shape[1], queries.shape[2]), log_totals)


def attend_backward(queries, key_rows, value_rows, segment, log_totals, grad_out):
    block_rows = min(512, ROW_LEN)
    block_count = queries.shape[0] // block_rows
    scaling = HEAD_DIM ** (-0.5)

    def one_block(carry, block_at):
        key_acc, value_acc = carry
        begin_row = block_at * block_rows
        rows_here = lax.dynamic_slice_in_dim(queries, begin_row, block_rows, 0)
        grads_here = lax.dynamic_slice_in_dim(grad_out, begin_row, block_rows, 0)
        own_segment = lax.dynamic_slice_in_dim(segment, begin_row, block_rows, 0)
        scores = (
            jnp.einsum("qhd,khd->hqk", rows_here, key_rows, preferred_element_type=jnp.float32)
            * scaling
        )
        scores = jnp.where((own_segment[:, None] == segment[None, :])[None], scores, -1e30)
        probs = jnp.exp(scores - log_totals[block_at][..., None])
        grad_probs = jnp.einsum(
            "qhd,khd->hqk", grads_here, value_rows, preferred_element_type=jnp.float32
        )
        grad_scores = (
            probs * (grad_probs - jnp.sum(grad_probs * probs, axis=-1, keepdims=True))
        ).astype(jnp.bfloat16)
        grad_query = (
            jnp.einsum("hqk,khd->qhd", grad_scores, key_rows, preferred_element_type=jnp.float32)
            * scaling
        )
        key_part = (
            jnp.einsum("hqk,qhd->khd", grad_scores, rows_here, preferred_element_type=jnp.float32)
            * scaling
        )
        value_part = jnp.einsum(
            "hqk,qhd->khd",
            probs.astype(jnp.bfloat16),
            grads_here,
            preferred_element_type=jnp.float32,
        )
        key_acc = key_acc + key_part
        value_acc = value_acc + value_part
        return ((key_acc, value_acc), grad_query)

    zeros_rows = jnp.zeros(key_rows.shape, jnp.float32)
    (grad_keys, grad_values), grad_queries = lax.scan(
        one_block, (zeros_rows, zeros_rows), jnp.arange(block_count, dtype=jnp.int32)
    )
    return (grad_queries.reshape(queries.shape), grad_keys, grad_values)


def body(
    hidden_in,
    seg_lengths,
    partner,
    qkv_weight,
    out_weight,
    up_weight,
    down_weight,
    norm_params,
    emb_weight,
    log_scale,
    qkv_moments,
    out_moments,
    up_moments,
    down_moments,
    norm_moments,
    emb_moments,
    scale_moments,
):
    shard_rows = hidden_in.shape[0]
    mp_count = lax.axis_size("mp")
    row_start = lax.axis_index("mp") * shard_rows
    packed_here = seg_lengths.shape[0]
    local_tokens = packed_here * ROW_LEN
    width_here = qkv_weight.shape[3]
    heads_here = width_here // HEAD_DIM
    qkv_all, out_all, up_all, down_all, norm_low, emb_all = (
        lax.all_gather(qkv_weight.astype(jnp.bfloat16), "dp", axis=1, tiled=True),
        lax.all_gather(out_weight.astype(jnp.bfloat16), "dp", axis=2, tiled=True),
        lax.all_gather(up_weight.astype(jnp.bfloat16), "dp", axis=1, tiled=True),
        lax.all_gather(down_weight.astype(jnp.bfloat16), "dp", axis=2, tiled=True),
        lax.all_gather(norm_params.astype(jnp.bfloat16), "dp", axis=3, tiled=True),
        lax.all_gather(emb_weight.astype(jnp.bfloat16), "dp", axis=0, tiled=True),
    )
    norm_all = norm_low.astype(jnp.float32)
    segment_rows, offset_rows = jax.vmap(row_layout)(seg_lengths)
    row_labels = (jnp.arange(packed_here, dtype=jnp.int32) * SEGS)[:, None]
    segment = (segment_rows + row_labels).reshape(local_tokens)
    cosines, sines = rotary_tables(offset_rows.reshape(local_tokens))
    cosines = cosines[:, None, :]
    sines = sines[:, None, :]
    stream = hidden_in.astype(jnp.float32)
    kept = []
    for layer_at in range(LAYERS):
        joint = qkv_all[layer_at].reshape(D, 3 * width_here)
        stream_rows = lax.all_gather(stream.astype(jnp.bfloat16), "mp", axis=0, tiled=True)
        mixture = plain_dot(stream_rows, joint).reshape(local_tokens, 3, heads_here, HEAD_DIM)
        queries = rotate(mixture[:, 0], cosines, sines).astype(jnp.bfloat16)
        key_rows = rotate(mixture[:, 1], cosines, sines).astype(jnp.bfloat16)
        value_rows = mixture[:, 2].astype(jnp.bfloat16)
        attended, log_totals = attend_forward(queries, key_rows, value_rows, segment)
        attended_low = attended.reshape(local_tokens, width_here).astype(jnp.bfloat16)
        out_here = out_all[layer_at]
        attn_out = lax.psum_scatter(
            plain_dot(attended_low, out_here).astype(jnp.bfloat16),
            "mp",
            scatter_dimension=0,
            tiled=True,
        ).astype(jnp.float32)
        attn_sum = stream + attn_out
        normed = layer_norm(attn_sum, norm_all[layer_at, 0, 0], norm_all[layer_at, 0, 1])
        normed_rows = lax.all_gather(normed.astype(jnp.bfloat16), "mp", axis=0, tiled=True)
        pre_act = plain_dot(normed_rows, up_all[layer_at])
        activated = jax.nn.gelu(pre_act, approximate=False).astype(jnp.bfloat16)
        down_here = down_all[layer_at]
        ffn_out = lax.psum_scatter(
            plain_dot(activated, down_here).astype(jnp.bfloat16),
            "mp",
            scatter_dimension=0,
            tiled=True,
        ).astype(jnp.float32)
        ffn_sum = normed + ffn_out
        kept.append(
            (
                stream_rows,
                queries,
                key_rows,
                value_rows,
                log_totals,
                attended_low,
                attn_sum,
                normed_rows,
                pre_act,
                activated,
                ffn_sum,
            )
        )
        stream = layer_norm(ffn_sum, norm_all[layer_at, 1, 0], norm_all[layer_at, 1, 1])
    stream_low = stream.astype(jnp.bfloat16)
    embed_low = plain_dot(stream_low, emb_all).astype(jnp.bfloat16)
    embed_rows = lax.all_gather(embed_low, "mp", axis=0, tiled=True)

    def loss_of(embedded, scale_log):
        per_row = jax.vmap(
            lambda one_emb, one_seg, one_len, one_partner: row_loss(
                one_emb, scale_log, one_seg, one_len, one_partner
            )
        )(embedded.reshape(packed_here, ROW_LEN, EMB), segment_rows, seg_lengths, partner)
        return jnp.sum(per_row)

    loss_value, loss_back = jax.vjp(loss_of, embed_rows.astype(jnp.float32), log_scale)
    grad_embed_rows, grad_scale = loss_back(jnp.ones((), jnp.float32))
    grad_embed = lax.dynamic_slice_in_dim(grad_embed_rows, row_start, shard_rows, 0).astype(
        jnp.bfloat16
    )
    emb_grad_t = inner_dot(grad_embed, stream_low)
    grad_stream = outer_dot(grad_embed, emb_all)
    collected = [None] * LAYERS
    for layer_at in reversed(range(LAYERS)):
        (
            stream_rows,
            queries,
            key_rows,
            value_rows,
            log_totals,
            attended_low,
            attn_sum,
            normed_rows,
            pre_act,
            activated,
            ffn_sum,
        ) = kept[layer_at]
        _, norm_back_ffn = jax.vjp(
            layer_norm, ffn_sum, norm_all[layer_at, 1, 0], norm_all[layer_at, 1, 1]
        )
        grad_ffn_sum, gain_grad_ffn, bias_grad_ffn = norm_back_ffn(grad_stream)
        grad_ffn_rows = lax.all_gather(grad_ffn_sum.astype(jnp.bfloat16), "mp", axis=0, tiled=True)
        g_down = inner_dot(activated, grad_ffn_rows)
        grad_act = outer_dot(grad_ffn_rows, down_all[layer_at])
        _, gelu_back = jax.vjp(lambda values: jax.nn.gelu(values, approximate=False), pre_act)
        grad_pre = gelu_back(grad_act)[0].astype(jnp.bfloat16)
        g_up = inner_dot(normed_rows, grad_pre)
        up_here = up_all[layer_at]
        grad_normed = grad_ffn_sum + lax.psum_scatter(
            outer_dot(grad_pre, up_here).astype(jnp.bfloat16), "mp", scatter_dimension=0, tiled=True
        ).astype(jnp.float32)
        _, norm_back_attn = jax.vjp(
            layer_norm, attn_sum, norm_all[layer_at, 0, 0], norm_all[layer_at, 0, 1]
        )
        grad_attn_sum, gain_grad_attn, bias_grad_attn = norm_back_attn(grad_normed)
        grad_attn_rows = lax.all_gather(
            grad_attn_sum.astype(jnp.bfloat16), "mp", axis=0, tiled=True
        )
        g_out = inner_dot(attended_low, grad_attn_rows)
        grad_attended = (
            outer_dot(grad_attn_rows, out_all[layer_at])
            .astype(jnp.bfloat16)
            .reshape(local_tokens, heads_here, HEAD_DIM)
        )
        grad_queries, grad_keys, grad_values = attend_backward(
            queries, key_rows, value_rows, segment, log_totals, grad_attended
        )
        grad_queries = rotate(grad_queries, cosines, -sines).astype(jnp.bfloat16)
        grad_keys = rotate(grad_keys, cosines, -sines).astype(jnp.bfloat16)
        grad_mixture = jnp.stack(
            [grad_queries, grad_keys, grad_values.astype(jnp.bfloat16)], axis=1
        ).reshape(local_tokens, 3 * width_here)
        g_qkv = inner_dot(stream_rows, grad_mixture).reshape(D, 3, width_here)
        joint = qkv_all[layer_at].reshape(D, 3 * width_here)
        grad_stream = grad_attn_sum + lax.psum_scatter(
            outer_dot(grad_mixture, joint).astype(jnp.bfloat16),
            "mp",
            scatter_dimension=0,
            tiled=True,
        ).astype(jnp.float32)
        g_norm_rows = jnp.stack([gain_grad_attn, bias_grad_attn, gain_grad_ffn, bias_grad_ffn])
        collected[layer_at] = (g_qkv, g_out, g_up, g_down, g_norm_rows)
    small_rows = jnp.concatenate(
        [collected[layer_at][4] for layer_at in range(LAYERS)] + [emb_grad_t], axis=0
    )
    r_qkv, r_out, r_up, r_down, r_small = (
        lax.psum_scatter(
            jnp.stack([collected[layer_at][0] for layer_at in range(LAYERS)]),
            "dp",
            scatter_dimension=1,
            tiled=True,
        ),
        lax.psum_scatter(
            jnp.stack([collected[layer_at][1] for layer_at in range(LAYERS)]),
            "dp",
            scatter_dimension=2,
            tiled=True,
        ),
        lax.psum_scatter(
            jnp.stack([collected[layer_at][2] for layer_at in range(LAYERS)]),
            "dp",
            scatter_dimension=1,
            tiled=True,
        ),
        lax.psum_scatter(
            jnp.stack([collected[layer_at][3] for layer_at in range(LAYERS)]),
            "dp",
            scatter_dimension=2,
            tiled=True,
        ),
        lax.psum_scatter(small_rows, "dp", scatter_dimension=1, tiled=True),
    )
    small_full = lax.psum(r_small, "mp")
    norm_grad = small_full[: 4 * LAYERS].reshape(LAYERS, 2, 2, small_full.shape[1])
    emb_grad = small_full[4 * LAYERS :].T
    squares = (
        jnp.sum(r_qkv * r_qkv)
        + jnp.sum(r_out * r_out)
        + jnp.sum(r_up * r_up)
        + jnp.sum(r_down * r_down)
    )
    squares = squares + jnp.sum(small_full * small_full) / mp_count
    total_squares, scale_grad, loss_total = lax.psum(
        (squares, grad_scale / mp_count, loss_value / mp_count), ("dp", "mp")
    )
    norm_value = jnp.sqrt(total_squares + scale_grad[0] * scale_grad[0] + 1e-06)
    factor = clip_limit / jnp.maximum(norm_value, clip_limit)
    step_f = jnp.asarray(STEP, jnp.float32)
    qkv_new, qkv_first, qkv_second = adamw_update(
        qkv_weight, qkv_moments, r_qkv, factor, D ** (-0.5), step_f
    )
    out_new, out_first, out_second = adamw_update(
        out_weight, out_moments, r_out, factor, (D * SEGS // ROW_LEN) ** (-0.5), step_f
    )
    up_new, up_first, up_second = adamw_update(
        up_weight, up_moments, r_up, factor, D ** (-0.5), step_f
    )
    down_new, down_first, down_second = adamw_update(
        down_weight, down_moments, r_down, factor, FF ** (-0.5), step_f
    )
    norm_new, norm_first, norm_second = adamw_update(
        norm_params, norm_moments, norm_grad, factor, 0.5, step_f
    )
    emb_new, emb_first, emb_second = adamw_update(
        emb_weight, emb_moments, emb_grad, factor, D ** (-0.5), step_f
    )
    scale_new, scale_first, scale_second = adamw_update(
        log_scale, scale_moments, scale_grad, factor, 1.0, step_f
    )
    return (
        stream,
        grad_stream,
        loss_total.reshape(1),
        norm_value.reshape(1),
        qkv_new,
        qkv_first,
        qkv_second,
        out_new,
        out_first,
        out_second,
        up_new,
        up_first,
        up_second,
        down_new,
        down_first,
        down_second,
        norm_new,
        norm_first,
        norm_second,
        emb_new,
        emb_first,
        emb_second,
        scale_new,
        scale_first,
        scale_second,
    )


def solution(mesh):
    placed = (
        P(("dp", "mp"), None),
        P("dp", None),
        P("dp", None),
        P(None, "dp", None, "mp"),
        P(None, "mp", "dp"),
        P(None, "dp", "mp"),
        P(None, "mp", "dp"),
        P(None, None, None, "dp"),
        P("dp", None),
        P(),
        P(None, None, "dp", None, "mp"),
        P(None, None, "mp", "dp"),
        P(None, None, "dp", "mp"),
        P(None, None, "mp", "dp"),
        P(None, None, None, None, "dp"),
        P(None, "dp", None),
        P(),
    )
    return jax.shard_map(
        body,
        mesh=mesh,
        in_specs=placed,
        out_specs=(
            P(("dp", "mp"), None),
            P(("dp", "mp"), None),
            P(),
            P(),
            P(None, "dp", None, "mp"),
            P(None, "dp", None, "mp"),
            P(None, "dp", None, "mp"),
            P(None, "mp", "dp"),
            P(None, "mp", "dp"),
            P(None, "mp", "dp"),
            P(None, "dp", "mp"),
            P(None, "dp", "mp"),
            P(None, "dp", "mp"),
            P(None, "mp", "dp"),
            P(None, "mp", "dp"),
            P(None, "mp", "dp"),
            P(None, None, None, "dp"),
            P(None, None, None, "dp"),
            P(None, None, None, "dp"),
            P("dp", None),
            P("dp", None),
            P("dp", None),
            P(),
            P(),
            P(),
        ),
        check_vma=False,
    )
```

profile of v0, /device:TPU:0, one launch (start us, length us, event | category | flops | bytes accessed | tf_op | source)
XLA Modules:
  0.0 1638.0 jit_solution(16357508865796174734)
XLA Ops:
  14.6 61.9 %all-gather.15.cloned.1.call-done = bf16[2,1024,3,256]{1,3,2,0:T(8,128)(2,1)} async-done(((bf16[2,128,3,256]{1,3,2,0:T(8,128)(2,1)}), bf16[2,1024,3,256]{1,3,2,0:T(8,128)(2,1)}) %all-gather.15.cloned.1.call-update) | async-done | bytes 3145744 | tf_op jit(solution)/shard_map/all_gather | solution.py:210
  80.0 18.8 %all-gather.13.cloned.1.call-done = bf16[1024,1024]{1,0:T(8,128)(2,1)} async-done(((bf16[256,1024]{1,0:T(8,128)(2,1)}), bf16[1024,1024]{1,0:T(8,128)(2,1)}) %all-gather.13.cloned.1.call-update) | async-done | bytes 2097168 | tf_op jit(solution)/shard_map/all_gather | solution.py:228
  103.1 17.6 %while.54 = (s32[]{:T(128)}, bf16[2,512,4,64]{1,3,2,0:T(8,128)(2,1)S(1)}, f32[2,4,512]{2,1,0:T(4,128)S(1)}, s32[2]{0:T(128)S(1)}, s32[1024]{0:T(1024)S(1)}, /*in...) while((s32[]{:T(128)}, ...), condition=%wide.region_6.7_spmd, body=%wide.region_3.6_spmd.sunk | while | flops 562558976 | bytes 29173960 | solution.py:131
  121.4 19.7 %all-gather.17.cloned.1.call-done = bf16[2,256,1024]{2,1,0:T(8,128)(2,1)} async-done(((bf16[2,256,128]{2,1,0:T(8,128)(2,1)}), bf16[2,256,1024]{2,1,0:T(8,128)(2,1)}) %all-gather.17.cloned.1.call-update) | async-done | bytes 1048592 | tf_op jit(solution)/shard_map/all_gather | solution.py:211
  146.5 18.7 %all_gather.48 = bf16[2,2,2,1024]{3,2,1,0:T(2,128)(2,1)S(1)} all-gather(bf16[2,2,2,128]{3,2,1,0:T(2,128)(2,1)S(1)} %convert_element_type.277), channel_id=1, replica_groups=mesh['dp'=8,'mp'=4] {'dp'}, dimensions={3}, use_global_device_ids=true | all-gather | bytes 18432 | tf_op jit(solution)/shard_map/all_gather | solution.py:214
  165.8 8.9 reduce-scatter.14.cloned.1.call-done
  180.6 70.3 %all-gather.21.cloned.1.call-done = bf16[2,1024,1024]{2,1,0:T(8,128)(2,1)} async-done(((bf16[2,128,1024]{2,1,0:T(8,128)(2,1)}), bf16[2,1024,1024]{2,1,0:T(8,128)(2,1)}) %all-gather.21.cloned.1.call-update) | async-done | bytes 4194320 | tf_op jit(solution)/shard_map/all_gather | solution.py:212
  250.9 23.0 %all-gather.19.cloned.1.call-done = bf16[1024,1024]{1,0:T(8,128)(2,1)} async-done(((bf16[256,1024]{1,0:T(8,128)(2,1)}), bf16[1024,1024]{1,0:T(8,128)(2,1)}) %all-gather.19.cloned.1.call-update) | async-done | bytes 2097168 | tf_op jit(solution)/shard_map/all_gather | solution.py:244
  273.9 15.1 multiply_convert_fusion.3
  289.0 62.8 %all-gather.23.cloned.1.call-done = bf16[2,1024,1024]{2,1,0:T(8,128)(2,1)} async-done(((bf16[2,1024,128]{2,1,0:T(8,128)(2,1)}), bf16[2,1024,1024]{2,1,0:T(8,128)(2,1)}) %all-gather.23.cloned.1.call-update) | async-done | bytes 4194320 | tf_op jit(solution)/shard_map/all_gather | solution.py:213
  351.8 5.9 convolution_convert_fusion.4
  357.7 29.7 %reduce-scatter.16.cloned.1.call-done = bf16[256,1024]{1,0:T(8,128)(2,1)} async-done(((bf16[1024,1024]{1,0:T(8,128)(2,1)}), bf16[256,1024]{1,0:T(8,128)(2,1)}) %reduce-scatter.16.cloned.1.call-update) | async-done | bytes 524304 | tf_op jit(solution)/shard_map/reduce_scatter | solution.py:248
  390.6 22.5 %all-gather.25.cloned.1.call-done = bf16[1024,1024]{1,0:T(8,128)(2,1)} async-done(((bf16[256,1024]{1,0:T(8,128)(2,1)}), bf16[1024,1024]{1,0:T(8,128)(2,1)}) %all-gather.25.cloned.1.call-update) | async-done | bytes 2097168 | tf_op jit(solution)/shard_map/all_gather | solution.py:228
  417.8 17.6 %while.55 = (s32[]{:T(128)}, bf16[2,512,4,64]{1,3,2,0:T(8,128)(2,1)S(1)}, f32[2,4,512]{2,1,0:T(4,128)S(1)}, s32[2]{0:T(128)S(1)}, s32[1024]{0:T(1024)S(1)}, /*in...) while((s32[]{:T(128)}, ...), condition=%wide.region_16.17_spmd, body=%wide.region_13.16_spmd.sunk | while | flops 562558976 | bytes 29173960 | solution.py:131
  439.4 31.5 %reduce-scatter.18.cloned.1.call-done = bf16[256,1024]{1,0:T(8,128)(2,1)} async-done(((bf16[1024,1024]{1,0:T(8,128)(2,1)}), bf16[256,1024]{1,0:T(8,128)(2,1)}) %reduce-scatter.18.cloned.1.call-update) | async-done | bytes 524304 | tf_op jit(solution)/shard_map/reduce_scatter | solution.py:236
  474.2 22.3 %all-gather.27.cloned.1.call-done = bf16[1024,1024]{1,0:T(8,128)(2,1)} async-done(((bf16[256,1024]{1,0:T(8,128)(2,1)}), bf16[1024,1024]{1,0:T(8,128)(2,1)}) %all-gather.27.cloned.1.call-update) | async-done | bytes 2097168 | tf_op jit(solution)/shard_map/all_gather | solution.py:244
  496.5 14.8 multiply_convert_fusion.2
  517.1 30.8 %all_gather.54 = bf16[1024,128]{1,0:T(8,128)(2,1)S(1)} all-gather(bf16[128,128]{1,0:T(8,128)(2,1)S(1)} %convert_element_type.296), channel_id=1, replica_groups=mesh['dp'=8,'mp'=4] {'dp'}, dimensions={0}, use_global_device_ids=true | all-gather | bytes 294912 | tf_op jit(solution)/shard_map/all_gather | solution.py:215
  551.2 6.0 all_gather.55
  570.9 7.5 multiply_reduce_fusion.21
  607.0 7.2 convolution_add_fusion
  614.2 7.3 multiply_reduce_fusion.19
  624.9 22.3 %all-gather.29.cloned.1.call-done = bf16[1024,1024]{1,0:T(8,128)(2,1)} async-done(((bf16[256,1024]{1,0:T(8,128)(2,1)}), bf16[1024,1024]{1,0:T(8,128)(2,1)}) %all-gather.29.cloned.1.call-update) | async-done | bytes 2097168 | tf_op jit(solution)/shard_map/all_gather | solution.py:309
  647.2 8.2 add_convert_fusion.1
  660.5 31.5 %reduce-scatter.22.cloned.1.call-done = bf16[256,1024]{1,0:T(8,128)(2,1)} async-done(((bf16[1024,1024]{1,0:T(8,128)(2,1)}), bf16[256,1024]{1,0:T(8,128)(2,1)}) %reduce-scatter.22.cloned.1.call-update) | async-done | bytes 524304 | tf_op jit(solution)/shard_map/reduce_scatter | solution.py:316
  697.2 22.7 %all-gather.31.cloned.1.call-done = bf16[1024,1024]{1,0:T(8,128)(2,1)} async-done(((bf16[256,1024]{1,0:T(8,128)(2,1)}), bf16[1024,1024]{1,0:T(8,128)(2,1)}) %all-gather.31.cloned.1.call-update) | async-done | bytes 2097168 | tf_op jit(solution)/shard_map/all_gather | solution.py:323
  724.4 79.8 %while.56 = (s32[]{:T(128)}, f32[1024,4,64]{0,2,1:T(8,128)S(1)}, f32[1024,4,64]{0,2,1:T(8,128)}, f32[2,512,4,64]{1,0,3,2:T(2,128)}, s32[2]{0:T(128)S(1)}, /*inde...) while((s32[]{:T(128)}, f32[1024,4,64]{0,2,1:T(8,128)S(1)}, ...), condition=%wide.region_48.49_spmd.clone, body=%wide.region_46.48_spmd.clone.sunk | while | flops 1375598592 | bytes 120654256 | solution.py:177
  732.4 5.8 multiply_reduce_fusion.33
  744.8 10.4 dynamic_update_slice.36
  758.4 5.8 fusion.401
  784.4 10.4 dynamic_update_slice.36
  798.1 6.1 fusion.401
  812.9 31.3 %reduce-scatter.24.cloned.1.call-done = bf16[256,1024]{1,0:T(8,128)(2,1)} async-done(((bf16[1024,1024]{1,0:T(8,128)(2,1)}), bf16[256,1024]{1,0:T(8,128)(2,1)}) %reduce-scatter.24.cloned.1.call-update) | async-done | bytes 524304 | tf_op jit(solution)/shard_map/reduce_scatter | solution.py:342
  848.4 22.7 %all-gather.33.cloned.1.call-done = bf16[1024,1024]{1,0:T(8,128)(2,1)} async-done(((bf16[256,1024]{1,0:T(8,128)(2,1)}), bf16[1024,1024]{1,0:T(8,128)(2,1)}) %all-gather.33.cloned.1.call-update) | async-done | bytes 2097168 | tf_op jit(solution)/shard_map/all_gather | solution.py:309
  871.1 8.2 add_convert_fusion
  885.6 30.5 %reduce-scatter.26.cloned.1.call-done = bf16[256,1024]{1,0:T(8,128)(2,1)} async-done(((bf16[1024,1024]{1,0:T(8,128)(2,1)}), bf16[256,1024]{1,0:T(8,128)(2,1)}) %reduce-scatter.26.cloned.1.call-update) | async-done | bytes 524304 | tf_op jit(solution)/shard_map/reduce_scatter | solution.py:316
  925.6 51.0 %reduce-scatter.38.cloned.1.call-done = f32[136,128]{1,0:T(8,128)} async-done(((f32[136,1024]{1,0:T(8,128)}), f32[136,128]{1,0:T(8,128)}) %reduce-scatter.38.cloned.1.call-update) | async-done | bytes 69648 | tf_op jit(solution)/shard_map/reduce_scatter | solution.py:378
  976.7 23.7 %all-gather.35.cloned.1.call-done = bf16[1024,1024]{1,0:T(8,128)(2,1)} async-done(((bf16[256,1024]{1,0:T(8,128)(2,1)}), bf16[1024,1024]{1,0:T(8,128)(2,1)}) %all-gather.35.cloned.1.call-update) | async-done | bytes 2097168 | tf_op jit(solution)/shard_map/all_gather | solution.py:323
  1008.9 81.2 %while.57 = (s32[]{:T(128)}, f32[1024,4,64]{0,2,1:T(8,128)S(1)}, f32[1024,4,64]{0,2,1:T(8,128)}, f32[2,512,4,64]{1,0,3,2:T(2,128)}, s32[2]{0:T(128)S(1)}, /*inde...) while((s32[]{:T(128)}, f32[1024,4,64]{0,2,1:T(8,128)S(1)}, ...), condition=%wide.region_57.58_spmd.clone, body=%wide.region_55.57_spmd.clone.sunk | while | flops 1375598592 | bytes 120654256 | solution.py:177
  1029.9 10.4 dynamic_update_slice.37
  1043.5 6.0 fusion.414
  1057.8 5.9 multiply_reduce_fusion.34
  1070.3 10.4 dynamic_update_slice.37
  1083.9 6.2 fusion.414
  1154.5 137.7 %reduce-scatter.36.cloned.1.call-done = f32[2,1024,128]{2,1,0:T(8,128)} async-done(((f32[2,1024,1024]{2,1,0:T(8,128)}), f32[2,1024,128]{2,1,0:T(8,128)}) %reduce-scatter.36.cloned.1.call-update) | async-done | bytes 1048592 | tf_op jit(solution)/shard_map/reduce_scatter | solution.py:372
  1294.3 149.5 %reduce-scatter.34.cloned.1.call-done = f32[2,128,1024]{2,1,0:T(8,128)} async-done(((f32[2,1024,1024]{2,1,0:T(8,128)}), f32[2,128,1024]{2,1,0:T(8,128)}) %reduce-scatter.34.cloned.1.call-update) | async-done | bytes 1048592 | tf_op jit(solution)/shard_map/reduce_scatter | solution.py:366
  1446.0 119.2 %reduce-scatter.30.cloned.1.call-done = f32[2,128,3,256]{3,1,2,0:T(8,128)} async-done(((f32[2,1024,3,256]{3,1,2,0:T(8,128)}), f32[2,128,3,256]{3,1,2,0:T(8,128)}) %reduce-scatter.30.cloned.1.call-update) | async-done | bytes 786448 | tf_op jit(solution)/shard_map/reduce_scatter | solution.py:354
  1569.8 40.6 %all-reduce = (f32[1]{0:T(128)}, f32[]{:T(128)}, f32[1]{0:T(128)}) all-reduce(f32[1]{0:T(128)} %bitcast.74, f32[]{:T(128)S(6)} %add.497, f32[1]{0:T(128)} %bitcast.95), channel_id=1, replica_groups=mesh['dp'=8,'mp'=4] {'dp','mp'}, use_global_device_ids=true, to_apply=%region_65.66 | all-reduce | flops 3 | bytes 24 | tf_op jit(solution)/shard_map/psum | solution.py:390
  (601 shorter events, 331.0 us)
Async XLA Ops:
  7.2 69.3 %all-gather.15.cloned.1.call-start = ((), (), s32[]{:S(2)}) async-start(), calls=%async_computation.14 | async-start | bytes 3538944 | tf_op jit(solution)/shard_map/all_gather | solution.py:210
  9.3 89.5 %all-gather.13.cloned.1.call-start = ((), (), s32[]{:S(2)}) async-start(), calls=%async_computation.13 | async-start | bytes 2621440 | tf_op jit(solution)/shard_map/all_gather | solution.py:228
  10.1 131.0 %all-gather.17.cloned.1.call-start = ((), (), s32[]{:S(2)}) async-start(), calls=%async_computation.15 | async-start | bytes 1179648 | tf_op jit(solution)/shard_map/all_gather | solution.py:211
  11.8 162.9 %reduce-scatter.14.cloned.1.call-start = ((), (), s32[]{:S(2)}) async-start(), calls=%async_computation.16 | async-start | bytes 2621440 | tf_op jit(solution)/shard_map/reduce_scatter | solution.py:236
  14.6 402.7 %copy-start.34 = (f32[1024,32]{0,1:T(8,128)}, f32[1024,32]{0,1:T(8,128)S(1)}, u32[]{:S(2)}) copy-start(f32[1024,32]{0,1:T(8,128)S(1)} %get-tuple-element.624) | copy-start | bytes 393220
  121.3 53.4 %copy-start.8 = (bf16[256,1024]{1,0:T(8,128)(2,1)S(1)}, bf16[256,1024]{1,0:T(8,128)(2,1)}, u32[]{:S(2)}) copy-start(bf16[256,1024]{1,0:T(8,128)(2,1)} %param.25) | copy-start | bytes 1572868
  121.4 54.5 %copy-start.24 = (bf16[32,8,2,512]{3,1,2,0:T(8,128)(2,1)}, bf16[32,8,2,512]{3,1,2,0:T(8,128)(2,1)S(1)}, u32[]{:S(2)}) copy-start(bf16[32,8,2,512]{3,1,2,0:T(8,128)(2,1)S(1)} %copy.168) | copy-start | bytes 1572868
  144.2 106.7 %all-gather.21.cloned.1.call-start = ((), (), s32[]{:S(2)}) async-start(), calls=%async_computation.18 | async-start | bytes 4718592 | tf_op jit(solution)/shard_map/all_gather | solution.py:212
  146.4 127.5 %all-gather.19.cloned.1.call-start = ((), (), s32[]{:S(2)}) async-start(), calls=%async_computation.17 | async-start | bytes 2621440 | tf_op jit(solution)/shard_map/all_gather | solution.py:244
  165.8 221.7 %copy-start.59 = (f32[1,1,1,1024]{3,2,1,0:T(1,128)}, f32[1,1,1,1024]{3,2,1,0:T(1,128)S(1)}, u32[]{:S(2)}) copy-start(f32[1,1,1,1024]{3,2,1,0:T(1,128)S(1)} %get-tuple-element.620) | copy-start | bytes 12292
  165.8 305.2 %copy-start.61 = (f32[1,1,1,1024]{3,2,1,0:T(1,128)}, f32[1,1,1,1024]{3,2,1,0:T(1,128)S(1)}, u32[]{:S(2)}) copy-start(f32[1,1,1,1024]{3,2,1,0:T(1,128)S(1)} %get-tuple-element.618) | copy-start | bytes 12292
  176.0 211.5 %copy-start.70 = (f32[256]{0:T(256)}, f32[256]{0:T(256)S(1)}, u32[]{:S(2)}) copy-start(f32[256]{0:T(256)S(1)} %broadcast_multiply_fusion.3) | copy-start | bytes 3076
  177.3 111.7 %copy-start.85 = (f32[256]{0:T(256)}, f32[256]{0:T(256)S(1)}, u32[]{:S(2)}) copy-start(f32[256]{0:T(256)S(1)} %multiply_reduce_fusion.15) | copy-start | bytes 3076
  177.3 210.1 %copy-start.74 = (f32[256]{0:T(256)}, f32[256]{0:T(256)S(1)}, u32[]{:S(2)}) copy-start(f32[256]{0:T(256)S(1)} %fusion.230) | copy-start | bytes 3076
  179.5 172.3 %all-gather.23.cloned.1.call-start = ((), (), s32[]{:S(2)}) async-start(), calls=%async_computation.19 | async-start | bytes 4718592 | tf_op jit(solution)/shard_map/all_gather | solution.py:213
  180.4 207.0 %reduce-scatter.16.cloned.1.call-start = ((), (), s32[]{:S(2)}) async-start(), calls=%async_computation.20 | async-start | bytes 2621440 | tf_op jit(solution)/shard_map/reduce_scatter | solution.py:248
  357.7 55.4 %all-gather.25.cloned.1.call-start = ((), (), s32[]{:S(2)}) async-start(), calls=%async_computation.21 | async-start | bytes 2621440 | tf_op jit(solution)/shard_map/all_gather | solution.py:228
  389.0 81.9 %copy-start.6 = (f32[256,1024]{1,0:T(8,128)}, f32[256,1024]{1,0:T(8,128)S(1)}, u32[]{:S(2)}) copy-start(f32[256,1024]{1,0:T(8,128)S(1)} %get-tuple-element.567) | copy-start | bytes 3145732
  389.0 81.9 %copy-start.72 = (f32[256]{0:T(256)}, f32[256]{0:T(256)S(1)}, u32[]{:S(2)}) copy-start(f32[256]{0:T(256)S(1)} %broadcast_multiply_fusion.2) | copy-start | bytes 3076
  389.3 81.6 %copy-start.76 = (f32[256]{0:T(256)}, f32[256]{0:T(256)S(1)}, u32[]{:S(2)}) copy-start(f32[256]{0:T(256)S(1)} %fusion.231) | copy-start | bytes 3076
  390.4 80.5 %reduce-scatter.18.cloned.1.call-start = ((), (), s32[]{:S(2)}) async-start(), calls=%async_computation.22 | async-start | bytes 2621440 | tf_op jit(solution)/shard_map/reduce_scatter | solution.py:236
  439.4 57.1 %all-gather.27.cloned.1.call-start = ((), (), s32[]{:S(2)}) async-start(), calls=%async_computation.23 | async-start | bytes 2621440 | tf_op jit(solution)/shard_map/all_gather | solution.py:244
  473.8 74.2 %reduce-scatter.20.cloned.1.call-start = ((), (), s32[]{:S(2)}) async-start(), calls=%async_computation.24 | async-start | bytes 2621440 | tf_op jit(solution)/shard_map/reduce_scatter | solution.py:248
  516.3 130.9 %all-gather.29.cloned.1.call-start = ((), (), s32[]{:S(2)}) async-start(), calls=%async_computation.25 | async-start | bytes 2621440 | tf_op jit(solution)/shard_map/all_gather | solution.py:309
  624.5 67.6 %reduce-scatter.22.cloned.1.call-start = ((), (), s32[]{:S(2)}) async-start(), calls=%async_computation.26 | async-start | bytes 2621440 | tf_op jit(solution)/shard_map/reduce_scatter | solution.py:316
  660.5 59.5 %all-gather.31.cloned.1.call-start = ((), (), s32[]{:S(2)}) async-start(), calls=%async_computation.27 | async-start | bytes 2621440 | tf_op jit(solution)/shard_map/all_gather | solution.py:323
  697.2 147.0 %reduce-scatter.24.cloned.1.call-start = ((), (), s32[]{:S(2)}) async-start(), calls=%async_computation.28 | async-start | bytes 2621440 | tf_op jit(solution)/shard_map/reduce_scatter | solution.py:342
  724.4 83.4 %copy-start.35 = (f32[1024,32]{0,1:T(8,128)S(1)}, f32[1024,32]{0,1:T(8,128)}, u32[]{:S(2)}) copy-start(f32[1024,32]{0,1:T(8,128)} %copy-done.34) | copy-start | bytes 393220
  724.4 83.4 %copy-start.47 = (f32[1024,32]{0,1:T(8,128)S(1)}, f32[1024,32]{0,1:T(8,128)}, u32[]{:S(2)}) copy-start(f32[1024,32]{0,1:T(8,128)} %get-tuple-element.622) | copy-start | bytes 393220
  812.6 58.5 %all-gather.33.cloned.1.call-start = ((), (), s32[]{:S(2)}) async-start(), calls=%async_computation.29 | async-start | bytes 2621440 | tf_op jit(solution)/shard_map/all_gather | solution.py:309
  848.4 67.7 %reduce-scatter.26.cloned.1.call-start = ((), (), s32[]{:S(2)}) async-start(), calls=%async_computation.30 | async-start | bytes 2621440 | tf_op jit(solution)/shard_map/reduce_scatter | solution.py:316
  884.5 35.8 %copy-start.86 = (f32[256]{0:T(256)S(1)}, f32[256]{0:T(256)}, u32[]{:S(2)}) copy-start(f32[256]{0:T(256)} %copy-done.85) | copy-start | bytes 3076
  884.5 92.1 %reduce-scatter.38.cloned.1.call-start = ((), (), s32[]{:S(2)}) async-start(), calls=%async_computation.37 | async-start | bytes 626688 | tf_op jit(solution)/shard_map/reduce_scatter | solution.py:378
  920.2 80.2 %all-gather.35.cloned.1.call-start = ((), (), s32[]{:S(2)}) async-start(), calls=%async_computation.31 | async-start | bytes 2621440 | tf_op jit(solution)/shard_map/all_gather | solution.py:323
  922.0 78.4 %copy-start.25 = (bf16[32,8,2,512]{3,1,2,0:T(8,128)(2,1)S(1)}, bf16[32,8,2,512]{3,1,2,0:T(8,128)(2,1)}, u32[]{:S(2)}) copy-start(bf16[32,8,2,512]{3,1,2,0:T(8,128)(2,1)} %copy-done.24) | copy-start | bytes 1572868
  922.0 80.7 %copy-start.83 = (f32[256]{0:T(256)}, f32[256]{0:T(256)S(1)}, u32[]{:S(2)}) copy-start(f32[256]{0:T(256)S(1)} %negate_multiply_fusion.2) | copy-start | bytes 3076
  923.1 225.3 %all-reduce.3.cloned.1.call-start = ((), (), s32[]{:S(2)}) async-start(), calls=%async_computation.38 | async-start | bytes 139264 | tf_op jit(solution)/shard_map/psum | solution.py:380
  976.6 174.0 %reduce-scatter.32.cloned.1.call-start = ((), (), s32[]{:S(2)}) async-start(), calls=%async_computation.34 | async-start | bytes 2359296 | tf_op jit(solution)/shard_map/reduce_scatter | solution.py:360
  1004.3 148.0 %reduce-scatter.28.cloned.1.call-start = ((), (), s32[]{:S(2)}) async-start(), calls=%async_computation.32 | async-start | bytes 2621440 | tf_op jit(solution)/shard_map/reduce_scatter | solution.py:342
  1098.4 193.7 %reduce-scatter.36.cloned.1.call-start = ((), (), s32[]{:S(2)}) async-start(), calls=%async_computation.36 | async-start | bytes 9437184 | tf_op jit(solution)/shard_map/reduce_scatter | solution.py:372
  1109.5 334.3 %reduce-scatter.34.cloned.1.call-start = ((), (), s32[]{:S(2)}) async-start(), calls=%async_computation.35 | async-start | bytes 9437184 | tf_op jit(solution)/shard_map/reduce_scatter | solution.py:366
  1121.0 444.1 %reduce-scatter.30.cloned.1.call-start = ((), (), s32[]{:S(2)}) async-start(), calls=%async_computation.33 | async-start | bytes 7077888 | tf_op jit(solution)/shard_map/reduce_scatter | solution.py:354
  1139.6 477.3 %copy-start.82 = (f32[2,2,2,128]{3,2,1,0:T(2,128)S(1)}, f32[2,2,2,128]{3,2,1,0:T(2,128)}, u32[]{:S(2)}) copy-start(f32[2,2,2,128]{3,2,1,0:T(2,128)} %param.32) | copy-start | bytes 12292
  1139.6 477.3 %copy-start.89 = (f32[2,2,2,2,128]{4,3,2,1,0:T(2,128)S(1)}, f32[2,2,2,2,128]{4,3,2,1,0:T(2,128)}, u32[]{:S(2)}) copy-start(f32[2,2,2,2,128]{4,3,2,1,0:T(2,128)} %param.39) | copy-start | bytes 24580
  1139.6 477.9 %copy-start.28 = (f32[2,1024,128]{2,1,0:T(8,128)S(1)}, f32[2,1024,128]{2,1,0:T(8,128)}, u32[]{:S(2)}) copy-start(f32[2,1024,128]{2,1,0:T(8,128)} %param.31) | copy-start | bytes 3145732
  1148.4 464.8 %copy-start.53 = (f32[136,128]{1,0:T(8,128)S(1)}, f32[136,128]{1,0:T(8,128)}, u32[]{:S(2)}) copy-start(f32[136,128]{1,0:T(8,128)} %all-reduce.3.cloned.1.call-done) | copy-start | bytes 208900
  1292.2 325.4 %copy-start.30 = (f32[2,1024,128]{2,1,0:T(8,128)S(1)}, f32[2,1024,128]{2,1,0:T(8,128)}, u32[]{:S(2)}) copy-start(f32[2,1024,128]{2,1,0:T(8,128)} %reduce-scatter.36.cloned.1.call-done) | copy-start | bytes 3145732
  1567.1 54.5 %copy-start.29 = (f32[2,128,1024]{2,1,0:T(8,128)S(1)}, f32[2,128,1024]{2,1,0:T(8,128)}, u32[]{:S(2)}) copy-start(f32[2,128,1024]{2,1,0:T(8,128)} %param.30) | copy-start | bytes 3145732
  (122 other events, 1206.5 us)
Sparse Core Ops, SparseCore 0:
  10.7 65.7 all-gather.14
  78.1 20.7 all-gather.12
  101.5 39.5 all-gather.16
  144.3 30.2 reduce-scatter.13
  177.5 73.3 all-gather.20
  253.0 20.8 all-gather.18
  276.7 75.0 all-gather.22
  357.8 29.6 reduce-scatter.15
  390.5 22.5 all-gather.24
  439.5 31.4 reduce-scatter.17
  473.9 22.5 all-gather.26
  516.4 31.4 reduce-scatter.19
  624.6 22.5 all-gather.28
  660.6 31.4 reduce-scatter.21
  697.3 22.5 all-gather.30
  812.7 31.4 reduce-scatter.23
  848.5 22.5 all-gather.32
  884.6 31.4 reduce-scatter.25
  920.3 56.2 reduce-scatter.37
  978.7 21.6 all-gather.34
  1002.8 29.2 all-reduce.2
  1035.6 69.9 reduce-scatter.31
  1108.2 30.5 reduce-scatter.27
  1142.6 149.4 reduce-scatter.35
  1295.8 148.0 reduce-scatter.33
  1447.8 117.3 reduce-scatter.29
where the time goes:
time: 1650 us; the launch traced here: 1640 us
  waiting for transfers between devices  1010 us (61%)
  matrix products  285 us (17%)
  other arithmetic  99.9 us (6%)
  blocking collectives  96.1 us (6%)
  local copies, waits for them, and re-layouts  93.8 us (6%)
  between operations  32.8 us (2%)
    reduce_scatter x1, waiting for transfers between devices, body(): lax.psum_scatter(jnp.stack([collected[layer_at][2] for layer_at in range(...  150 us
    reduce_scatter x1, waiting for transfers between devices, body(): lax.psum_scatter(jnp.stack([collected[layer_at][3] for layer_at in range(...  138 us
    reduce_scatter x1, waiting for transfers between devices, body(): lax.psum_scatter(jnp.stack([collected[layer_at][0] for layer_at in range(...  119 us
    all_gather x1, waiting for transfers between devices, body(): lax.all_gather(up_weight.astype(jnp.bfloat16), 'dp', axis=1, tiled=True)  70.3 us
    all_gather x1, waiting for transfers between devices, body(): lax.all_gather(down_weight.astype(jnp.bfloat16), 'dp', axis=2, tiled=True)  62.8 us
    reduce_scatter x2, waiting for transfers between devices, body(): lax.psum_scatter(outer_dot(grad_pre, up_here).astype(jnp.bfloat16), 'mp',...  62 us
    all_gather x1, waiting for transfers between devices, body(): lax.all_gather(qkv_weight.astype(jnp.bfloat16), 'dp', axis=1, tiled=True)  61.9 us
    dot_general x9, matrix products, plain_dot(): return jnp.dot(left, right, preferred_element_type=jnp.float32)  53.4 us
  transfers between devices with their start and end apart: 26, of which 22 were waited for; matrix products, arithmetic and copies ran while one was open for 12% of the time, Pallas kernels for 0%

commit v1 on v0

v1 whole, which is shorter than its diff:
```python
import functools
import math

import jax
import jax.numpy as jnp
from jax import lax
from jax.experimental import pallas as pl
from jax.experimental.pallas import tpu as pltpu
from jax.sharding import PartitionSpec as P

D = 1024
HEAD_DIM = 64
FF = 4096
EMB = 128
LAYERS = 2
STEP = 5
ROW_LEN = 1024
SEGS = 8

BLK = 256
HALF = 512
WIDE = 256
HID = 1024
PAIR = 128
PAIRS = WIDE // PAIR
MIB = 1 << 20
COST = 1

f32 = jnp.float32
bf16 = jnp.bfloat16
best = lax.Precision.HIGHEST
sharpness = 0.05
clip_limit = 1.0

OUT_AT = 3 * WIDE


def dot_nn(left, right):
    return lax.dot_general(left, right, (((1,), (0,)), ((), ())), preferred_element_type=f32)


def dot_nt(left, right):
    return lax.dot_general(left, right, (((1,), (1,)), ((), ())), preferred_element_type=f32)


def dot_tn(left, right):
    return lax.dot_general(left, right, (((0,), (0,)), ((), ())), preferred_element_type=f32)


def whole(shape):
    return pl.BlockSpec(shape, lambda *_: (0,) * len(shape))


def call(kernel, args, in_specs, outs, out_specs=None, grid=(1,), scratch=(), flops=0, vmem=32, alias=None,
         keep=(), after=None, far=()):
    out_shape = [
        pltpu.HBM(s, d) if i in keep else jax.ShapeDtypeStruct(s, d) for i, (s, d) in enumerate(outs)
    ]
    if out_specs is None:
        out_specs = [whole(s) for s, _ in outs]
    args = [pltpu.with_memory_space_constraint(a, pltpu.HBM) if i in far else a for i, a in enumerate(args)]
    in_specs = list(in_specs)
    moved = sum(math.prod(a.shape) * a.dtype.itemsize for a in args if a.size < 3 * MIB)
    moved += sum(math.prod(s) * jnp.dtype(d).itemsize for s, d in outs)
    body_fn = kernel
    if after is not None:
        count = len(args)
        args = args + [after]
        in_specs = in_specs + [pl.BlockSpec(memory_space=pl.ANY)]

        def body_fn(*refs):
            kernel(*refs[:count], *refs[count + 1 :])

    return pl.pallas_call(
        body_fn,
        grid=grid,
        in_specs=in_specs,
        out_specs=out_specs,
        out_shape=out_shape,
        scratch_shapes=list(scratch),
        input_output_aliases=alias or {},
        compiler_params=pltpu.CompilerParams(
            dimension_semantics=("arbitrary",) * len(grid), vmem_limit_bytes=vmem * MIB
        ),
        cost_estimate=pl.CostEstimate(flops=int(flops * COST), bytes_accessed=int(moved * COST), transcendentals=0),
    )(*args)


def smem():
    return pl.BlockSpec(memory_space=pltpu.SMEM)


def halves(values):
    high = values.astype(bf16)
    return high, (values - high.astype(f32)).astype(bf16)


def norm_fwd_kernel(row, with_sums, *refs):
    if with_sums:
        x_ref, s_ref, r_ref, n_ref, h_ref, hb_ref, z_ref = refs
        v = x_ref[...].astype(f32) + (s_ref[...].astype(f32) + r_ref[...].astype(f32))
    else:
        x_ref, n_ref, h_ref, hb_ref, z_ref = refs
        v = x_ref[...].astype(f32)
    cen = v - jnp.mean(v, axis=1, keepdims=True)
    var = jnp.mean(cen * cen, axis=1, keepdims=True)
    rstd = lax.rsqrt(var + 1e-05)
    z = cen * rstd
    h = z * n_ref[row : row + 1, :] + n_ref[row + 1 : row + 2, :]
    h_ref[...] = h
    hb_ref[...] = h.astype(bf16)
    z_ref[:, 0:D] = z.astype(bf16)
    high, rest = halves(rstd)
    lane = lax.broadcasted_iota(jnp.int32, (BLK, PAIR), 1)
    z_ref[:, D:] = jnp.where(lane < 1, high.astype(f32), rest.astype(f32)).astype(bf16)


def norm_fwd(row, x, s, r, nrm):
    blk = whole((BLK, D))
    return call(
        functools.partial(norm_fwd_kernel, row, True),
        (x, s, r, nrm),
        [blk, blk, blk, whole(nrm.shape)],
        [((BLK, D), f32), ((BLK, D), bf16), ((BLK, D + PAIR), bf16)],
        flops=BLK * D * 10,
        keep=(2,),
    )


def norm_bwd_kernel(row, with_sums, *refs):
    if with_sums:
        d_ref, s_ref, r_ref, z_ref, n_ref, o_ref, ob_ref, g_ref = refs
        dy = d_ref[...] + (s_ref[...].astype(f32) + r_ref[...].astype(f32))
    else:
        d_ref, z_ref, n_ref, o_ref, ob_ref, g_ref = refs
        dy = d_ref[...]
    z = z_ref[:, 0:D].astype(f32)
    rstd = z_ref[:, D : D + 1].astype(f32) + z_ref[:, D + 1 : D + 2].astype(f32)
    dz = dy * n_ref[row : row + 1, :]
    m1 = jnp.mean(dz, axis=1, keepdims=True)
    m2 = jnp.mean(dz * z, axis=1, keepdims=True)
    dr = (dz - m1 - z * m2) * rstd
    o_ref[...] = dr
    ob_ref[...] = dr.astype(bf16)
    g_ref[...] = jnp.concatenate(
        [jnp.sum(dy * z, axis=0, keepdims=True), jnp.sum(dy, axis=0, keepdims=True), jnp.zeros((6, D), f32)],
        axis=0,
    )


def norm_bwd(row, d, sums, z, nrm):
    blk = whole((BLK, D))
    args = (d,) + tuple(sums) + (z, nrm)
    return call(
        functools.partial(norm_bwd_kernel, row, len(sums) > 0),
        args,
        [blk] * (1 + len(sums)) + [whole((BLK, D + PAIR)), whole(nrm.shape)],
        [((BLK, D), f32), ((BLK, D), bf16), ((8, D), f32)],
        flops=BLK * D * 14,
        far=(1 + len(sums),),
    )


def rope_lanes(values, cosines, sines):
    lane = lax.broadcasted_iota(jnp.int32, values.shape, 1)
    low = (lane & (HEAD_DIM - 1)) < HEAD_DIM // 2
    swapped = jnp.where(
        low, pltpu.roll(values, PAIR - HEAD_DIM // 2, 1), pltpu.roll(values, HEAD_DIM // 2, 1)
    )
    return values * cosines + swapped * sines


def qkv_kernel(xo_ref, xs_ref, w_ref, c_ref, s_ref, m_ref):
    for at, x_ref in enumerate((xo_ref, xs_ref)):
        rows = slice(at * BLK, (at + 1) * BLK)
        mix = dot_nn(x_ref[...], w_ref[...])
        cosines, sines = c_ref[rows, :], s_ref[rows, :]
        for p in range(PAIRS):
            lanes = slice(p * PAIR, (p + 1) * PAIR)
            q = rope_lanes(mix[:, p * PAIR : (p + 1) * PAIR], cosines, sines).astype(bf16)
            m_ref[rows, lanes] = q * HEAD_DIM ** (-0.5)
            lanes = slice(WIDE + p * PAIR, WIDE + (p + 1) * PAIR)
            m_ref[rows, lanes] = rope_lanes(mix[:, lanes], cosines, sines).astype(bf16)
        m_ref[rows, 2 * WIDE :] = mix[:, 2 * WIDE :].astype(bf16)


def qkv_project(x_own, x_sib, weights, cosines, sines, at):
    blk = whole((BLK, D))
    tab = pl.BlockSpec((HALF, PAIR), lambda *_: (at, 0))
    return call(
        qkv_kernel,
        (x_own, x_sib, weights, cosines, sines),
        [blk, blk, pl.BlockSpec((D, 3 * WIDE), lambda *_: (0, 0)), tab, tab],
        [((HALF, 3 * WIDE), bf16)],
        flops=2 * HALF * D * 3 * WIDE,
        keep=(0,),
    )[0]


def near_places(core, at):
    if at == 0:
        return 1 - core, core
    return core, 1 - core


def attend_kernel(at, core_ref, m_ref, mo_ref, sc_ref, sco_ref, sr_ref, w_ref, o_ref, l_ref, own_ref, send_ref):
    q_ref, k_ref, v_ref = [m_ref.at[:, i * WIDE : (i + 1) * WIDE] for i in range(3)]
    ko_ref, vo_ref = [mo_ref.at[:, i * WIDE : (i + 1) * WIDE] for i in (1, 2)]
    near, cross = near_places(core_ref[0], at)
    cross_rows = pl.ds(pl.multiple_of(cross * BLK, BLK), BLK)
    row_at = lax.broadcasted_iota(jnp.int32, (PAIR, BLK), 0)
    lane_at = lax.broadcasted_iota(jnp.int32, (BLK, PAIR), 1)
    seg_main = sc_ref[...]
    seg_main = jnp.concatenate([seg_main, seg_main], axis=1)
    seg_cross = sco_ref[cross_rows, :]
    seg_cross = jnp.concatenate([seg_cross, seg_cross], axis=1)
    l_ref[...] = jnp.zeros(l_ref.shape, f32)
    for is_near in (False, True):
        place = near if is_near else 1 - near
        start = pl.multiple_of(place * BLK, BLK)
        rows = pl.ds(start, BLK)
        seg_q = sr_ref[0:1, rows]
        bias = jnp.where(seg_main == seg_q, 0.0, -1e30)
        if is_near:
            bias_cross = jnp.where(seg_cross == seg_q, 0.0, -1e30)
        for p in range(PAIRS):
            lanes = slice(p * PAIR, (p + 1) * PAIR)
            keys = k_ref[:, lanes]
            values_t = v_ref[:, lanes].T
            queries = q_ref[rows, lanes]
            if is_near:
                keys_cross = ko_ref[cross_rows, lanes]
                values_cross_t = vo_ref[cross_rows, lanes].T
            parts = []
            for h in range(2):
                q = jnp.where((lane_at >= HEAD_DIM) == (h == 1), queries, jnp.zeros_like(queries))
                scores = dot_nt(keys, q) + bias
                top = jnp.max(scores, axis=0, keepdims=True)
                if is_near:
                    scores_cross = dot_nt(keys_cross, q) + bias_cross
                    top = jnp.maximum(top, jnp.max(scores_cross, axis=0, keepdims=True))
                e = jnp.exp(scores - top)
                total = jnp.sum(e, axis=0, keepdims=True)
                mixed = dot_nn(values_t, e.astype(bf16))
                if is_near:
                    e = jnp.exp(scores_cross - top)
                    total = total + jnp.sum(e, axis=0, keepdims=True)
                    mixed = mixed + dot_nn(values_cross_t, e.astype(bf16))
                parts.append(mixed / total)
                head = 2 * p + h
                l_ref[head : head + 1, rows] = top + jnp.log(total)
            both = jnp.where(row_at < HEAD_DIM, parts[0], parts[1])
            o_ref[rows, lanes] = both.T.astype(bf16)
    own_ref[...] = dot_nt(o_ref[0:BLK, :], w_ref[...]).astype(bf16)
    send_ref[...] = dot_nt(o_ref[BLK:HALF, :], w_ref[...]).astype(bf16)


def attend(at, core, qkv, qkv_other, seg_col, seg_row, weights, after):
    mix = whole((HALF, 3 * WIDE))
    return call(
        functools.partial(attend_kernel, at),
        (core, qkv, qkv_other, seg_col, seg_col, seg_row, weights),
        [
            smem(), mix, mix,
            pl.BlockSpec((HALF, PAIR), lambda *_: (at, 0)),
            pl.BlockSpec((HALF, PAIR), lambda *_: (1 - at, 0)),
            pl.BlockSpec((8, HALF), lambda *_: (0, at)),
            pl.BlockSpec((D, WIDE), lambda *_: (0, OUT_AT // WIDE)),
        ],
        [((HALF, WIDE), bf16), ((8, HALF), f32), ((BLK, D), bf16), ((BLK, D), bf16)],
        flops=4 * 4 * 5 * BLK * BLK * PAIR + 2 * HALF * WIDE * D,
        far=(1, 2),
        keep=(0, 1),
        after=after,
    )


def attend_back_kernel(core_ref, d0o, d0s, d1o, d1s, w_ref, mix0, mix1, o0, o1, l0, l1,
                       sc_ref, sr_ref, c_ref, s_ref, m0_ref, m1_ref,
                       dout_ref, dk_ref, dv_ref, dq_ref):
    for i, d in enumerate((d0o, d0s, d1o, d1s)):
        dout_ref[i // 2, (i % 2) * BLK : (i % 2 + 1) * BLK, :] = dot_nn(d[...], w_ref[...]).astype(bf16)
    dk_ref[...] = jnp.zeros(dk_ref.shape, f32)
    dv_ref[...] = jnp.zeros(dv_ref.shape, f32)
    row_at = lax.broadcasted_iota(jnp.int32, (PAIR, 1), 0)
    lane_at = lax.broadcasted_iota(jnp.int32, (1, PAIR), 1)
    scaling = HEAD_DIM ** (-0.5)
    q_refs, k_refs, v_refs = [
        [m.at[:, i * WIDE : (i + 1) * WIDE] for m in (mix0, mix1)] for i in range(3)
    ]
    o_refs, l_refs = (o0, o1), (l0, l1)
    for at in range(2):
        near, cross = near_places(core_ref[0], at)
        cross_rows = pl.ds(pl.multiple_of(cross * BLK, BLK), BLK)
        cross_full = pl.ds(pl.multiple_of((1 - at) * HALF + cross * BLK, BLK), BLK)
        seg_main = sc_ref[at * HALF : (at + 1) * HALF, :]
        seg_main = jnp.concatenate([seg_main, seg_main], axis=1)
        seg_cross = sc_ref[cross_full, :]
        seg_cross = jnp.concatenate([seg_cross, seg_cross], axis=1)
        for is_near in (False, True):
            place = near if is_near else 1 - near
            rows = pl.ds(pl.multiple_of(place * BLK, BLK), BLK)
            seg_q = sr_ref[0:1, pl.ds(pl.multiple_of(at * HALF + place * BLK, BLK), BLK)]
            bias = jnp.where(seg_main == seg_q, 0.0, -1e30)
            if is_near:
                bias_cross = jnp.where(seg_cross == seg_q, 0.0, -1e30)
            for p in range(PAIRS):
                lanes = slice(p * PAIR, (p + 1) * PAIR)
                keys, values = k_refs[at][:, lanes], v_refs[at][:, lanes]
                keys_t = keys.T
                queries, douts = q_refs[at][rows, lanes], dout_ref[at, rows, lanes]
                if is_near:
                    keys_cross = k_refs[1 - at][cross_rows, lanes]
                    values_cross = v_refs[1 - at][cross_rows, lanes]
                    keys_cross_t = keys_cross.T
                products = (douts.astype(f32) * o_refs[at][rows, lanes].astype(f32)).T
                dq_t = jnp.zeros((PAIR, BLK), f32)
                for h in range(2):
                    in_lanes = (lane_at >= HEAD_DIM) == (h == 1)
                    in_rows = (row_at >= HEAD_DIM) == (h == 1)
                    q = jnp.where(in_lanes, queries, jnp.zeros_like(queries))
                    d = jnp.where(in_lanes, douts, jnp.zeros_like(douts))
                    delta = jnp.sum(products[h * HEAD_DIM : (h + 1) * HEAD_DIM, :], axis=0, keepdims=True)
                    lse = l_refs[at][2 * p + h : 2 * p + h + 1, rows]
                    kt = jnp.where(in_rows, keys_t, jnp.zeros_like(keys_t))
                    probs = jnp.exp(dot_nt(keys, q) + bias - lse)
                    dscores = (probs * (dot_nt(values, d) - delta)).astype(bf16)
                    dv_ref[at, :, lanes] += dot_nn(probs.astype(bf16), d)
                    dk_ref[at, :, lanes] += dot_nn(dscores, q)
                    dq_t = dq_t + dot_nn(kt, dscores)
                    if is_near:
                        kt = jnp.where(in_rows, keys_cross_t, jnp.zeros_like(keys_cross_t))
                        probs = jnp.exp(dot_nt(keys_cross, q) + bias_cross - lse)
                        dscores = (probs * (dot_nt(values_cross, d) - delta)).astype(bf16)
                        dv_ref[1 - at, cross_rows, lanes] += dot_nn(probs.astype(bf16), d)
                        dk_ref[1 - at, cross_rows, lanes] += dot_nn(dscores, q)
                        dq_t = dq_t + dot_nn(kt, dscores)
                dq_ref[at, rows, lanes] = dq_t.T * scaling
    for at, m_ref in enumerate((m0_ref, m1_ref)):
        rows = slice(at * HALF, (at + 1) * HALF)
        cosines, sines = c_ref[rows, :], -s_ref[rows, :]
        for p in range(PAIRS):
            lanes = slice(p * PAIR, (p + 1) * PAIR)
            m_ref[:, p * PAIR : (p + 1) * PAIR] = rope_lanes(dq_ref[at, :, lanes], cosines, sines).astype(bf16)
            m_ref[:, WIDE + p * PAIR : WIDE + (p + 1) * PAIR] = rope_lanes(
                dk_ref[at, :, lanes], cosines, sines
            ).astype(bf16)
        m_ref[:, 2 * WIDE :] = dv_ref[at].astype(bf16)


def attend_back(core, dblocks, weights, qkv_a, qkv_b, o_a, o_b, l_a, l_b, seg_col, seg_row, cosines, sines):
    blk, half, low, mix = whole((BLK, D)), whole((HALF, WIDE)), whole((8, HALF)), whole((HALF, 3 * WIDE))
    tab = whole((ROW_LEN, PAIR))
    return call(
        attend_back_kernel,
        (core, *dblocks, weights, qkv_a, qkv_b, o_a, o_b, l_a, l_b, seg_col, seg_row, cosines, sines),
        [smem(), blk, blk, blk, blk, pl.BlockSpec((D, WIDE), lambda *_: (0, OUT_AT // WIDE))]
        + [mix, mix, half, half]
        + [low, low, tab, whole((8, ROW_LEN)), tab, tab],
        [((HALF, 3 * WIDE), bf16)] * 2,
        scratch=[
            pltpu.VMEM((2, HALF, WIDE), bf16),
            pltpu.VMEM((2, HALF, WIDE), f32),
            pltpu.VMEM((2, HALF, WIDE), f32),
            pltpu.VMEM((2, HALF, WIDE), f32),
        ],
        flops=10 * 4 * 10 * BLK * BLK * PAIR + 2 * ROW_LEN * WIDE * D,
        far=(6, 7, 8, 9, 10, 11),
    )


def spread_kernel(m_ref, w_ref, own_ref, send_ref):
    own_ref[...] = dot_nt(m_ref[0:BLK, :], w_ref[...]).astype(bf16)
    send_ref[...] = dot_nt(m_ref[BLK:HALF, :], w_ref[...]).astype(bf16)


def qkv_back(dmix, weights, after):
    return call(
        spread_kernel,
        (dmix, weights),
        [whole(dmix.shape), pl.BlockSpec((D, 3 * WIDE), lambda *_: (0, 0))],
        [((BLK, D), bf16)] * 2,
        flops=2 * HALF * D * 3 * WIDE,
        after=after,
    )


TILE = 256
TILES = HID // TILE


def gelu_pair(u):
    half = jnp.exp(u * u * -0.5)
    t = 1.0 / (1.0 + (0.3275911 * 0.5 ** 0.5) * jnp.abs(u))
    poly = t * (
        0.5 * 0.254829592
        + t * (0.5 * -0.284496736 + t * (0.5 * 1.421413741 + t * (0.5 * -1.453152027 + t * (0.5 * 1.061405429))))
    )
    tail = poly * half
    phi = jnp.where(u >= 0.0, 1.0 - tail, tail)
    return u * phi, phi + u * half * (1.0 / math.sqrt(2.0 * math.pi))


def mlp_kernel(ho_ref, hs_ref, up_ref, down_ref, zg_ref, own_ref, send_ref):
    for at, (h_ref, p_ref) in enumerate(((ho_ref, own_ref), (hs_ref, send_ref))):
        rows = slice(at * BLK, (at + 1) * BLK)
        value, slope = gelu_pair(dot_nn(h_ref[...], up_ref[...]))
        z = value.astype(bf16)
        zg_ref[rows, 0:HID] = z
        zg_ref[rows, HID:] = slope.astype(bf16)
        p_ref[...] = dot_nt(z, down_ref[...]).astype(bf16)


def mlp(h_own, h_sib, weights, after):
    blk = whole((BLK, D))
    array, first = weights
    return call(
        mlp_kernel,
        (h_own, h_sib, array, array),
        [
            blk, blk,
            pl.BlockSpec((D, HID), lambda *_: (0, first)),
            pl.BlockSpec((D, HID), lambda *_: (0, first + 1)),
        ],
        [((HALF, 2 * HID), bf16), ((BLK, D), bf16), ((BLK, D), bf16)],
        flops=4 * HALF * D * HID,
        keep=(0,),
        after=after,
    )


def mlp_back_kernel(do_ref, ds_ref, g_ref, up_ref, down_ref, du_ref, own_ref, send_ref):
    for at, (d_ref, p_ref) in enumerate(((do_ref, own_ref), (ds_ref, send_ref))):
        rows = slice(at * BLK, (at + 1) * BLK)
        du = (dot_nn(d_ref[...], down_ref[...]) * g_ref[rows, :].astype(f32)).astype(bf16)
        du_ref[rows, :] = du
        p_ref[...] = dot_nt(du, up_ref[...]).astype(bf16)


def mlp_back(d_own, d_sib, zg, weights, after):
    blk = whole((BLK, D))
    array, first = weights
    return call(
        mlp_back_kernel,
        (d_own, d_sib, zg, array, array),
        [
            blk, blk,
            pl.BlockSpec((HALF, HID), lambda *_: (0, 1)),
            pl.BlockSpec((D, HID), lambda *_: (0, first)),
            pl.BlockSpec((D, HID), lambda *_: (0, first + 1)),
        ],
        [((HALF, HID), bf16), ((BLK, D), bf16), ((BLK, D), bf16)],
        flops=4 * HALF * D * HID,
        far=(2,),
        after=after,
    )


def turn_into(t_ref, x_refs):
    for i, x in enumerate(x_refs):
        t_ref[:, i * BLK : (i + 1) * BLK] = x[...].T


def grad_tile(t_ref, y_refs):
    first, second = y_refs
    return (dot_nn(t_ref[:, 0:HALF], first[...]) + dot_nn(t_ref[:, HALF:], second[...])).astype(bf16)


def mlp_grad_kernel(x0, x1, x2, x3, d0, d1, d2, d3, u0, u1, z0, z1, g_ref, t_ref):
    step = pl.program_id(0)

    @pl.when(step == 0)
    def _():
        turn_into(t_ref, (x0, x1, x2, x3))

    @pl.when(step == HID // HALF)
    def _():
        turn_into(t_ref, (d0, d1, d2, d3))

    @pl.when(step < HID // HALF)
    def _():
        g_ref[...] = grad_tile(t_ref, (u0, u1))

    @pl.when(step >= HID // HALF)
    def _():
        g_ref[...] = grad_tile(t_ref, (z0, z1))


def mlp_grads(hidden, dblocks, dus, zs, after):
    blk = whole((BLK, D))
    tiles = HID // HALF
    first = pl.BlockSpec((HALF, HALF), lambda t: (0, jnp.minimum(t, tiles - 1)))
    second = pl.BlockSpec((HALF, HALF), lambda t: (0, jnp.maximum(t - tiles, 0)))
    return call(
        mlp_grad_kernel,
        (*hidden, *dblocks, *dus, *zs),
        [blk] * 8 + [first] * 2 + [second] * 2,
        [((D, 2 * HID), bf16)],
        out_specs=[pl.BlockSpec((D, HALF), lambda t: (0, t))],
        grid=(2 * tiles,),
        scratch=[pltpu.VMEM((D, ROW_LEN), bf16)],
        flops=4 * ROW_LEN * D * HID,
        keep=(0,),
        after=after,
    )[0]


def attn_grad_kernel(with_small, x0, x1, x2, x3, d0, d1, d2, d3, m0, m1, o0, o1, *refs):
    g_ref, t_ref = refs[-2:]
    step = pl.program_id(0)

    @pl.when(step == 0)
    def _():
        turn_into(t_ref, (x0, x1, x2, x3))

    @pl.when(step == 3)
    def _():
        turn_into(t_ref, (d0, d1, d2, d3))

    @pl.when(step < 3)
    def _():
        g_ref[...] = grad_tile(t_ref, (m0, m1))

    @pl.when(step == 3)
    def _():
        g_ref[...] = grad_tile(t_ref, (o0, o1))

    if with_small:

        @pl.when(step == 4)
        def _():
            g_ref[...] = refs[0][...]


def attn_grads(streams, dblocks, dmixes, outs, after, small=None):
    blk = whole((BLK, D))
    first = pl.BlockSpec((HALF, WIDE), lambda t: (0, jnp.minimum(t, 2)))
    args = (*streams, *dblocks, *dmixes, *outs) + (() if small is None else (small,))
    specs = [blk] * 8 + [first] * 2 + [whole((HALF, WIDE))] * 2
    specs += [] if small is None else [whole((D, WIDE))]
    steps = 4 if small is None else 5
    return call(
        functools.partial(attn_grad_kernel, small is not None),
        args,
        specs,
        [((D, steps * WIDE), bf16)],
        out_specs=[pl.BlockSpec((D, WIDE), lambda t: (0, t))],
        grid=(steps,),
        scratch=[pltpu.VMEM((D, ROW_LEN), bf16)],
        flops=2 * ROW_LEN * D * 4 * WIDE,
        after=after,
    )[0]


def loss_kernel(ls_ref, e_ref, seg_ref, segr_ref, len_ref, par_ref, x0_ref, x1_ref, we_ref,
                dx0_ref, dx1_ref, ge_ref, out_ref, sim_ref, b_ref, ll_ref, de_ref):
    tokens = ROW_LEN
    mine = HALF
    width_blk = BLK
    emb = e_ref[...].astype(f32)
    emb_t = emb.T
    lanes = lax.broadcasted_iota(jnp.int32, (tokens, PAIR), 1)
    label_col = lanes.astype(f32)
    member = (seg_ref[...] == label_col).astype(bf16)
    rows16 = lax.broadcasted_iota(jnp.int32, (16, tokens), 0).astype(f32)
    member_t = (jnp.broadcast_to(segr_ref[0:1, :], (16, tokens)) == rows16).astype(bf16)
    scale = jnp.exp(ls_ref[0])
    cls = lax.broadcasted_iota(jnp.int32, (16, PAIR), 0)
    seg = lax.broadcasted_iota(jnp.int32, (16, PAIR), 1)
    real = (cls < SEGS) & (seg < SEGS)
    allowed = (cls != seg) & real
    lengths = len_ref[0:1, :]
    chosen = (cls.astype(f32) == par_ref[0:1, :]) & real
    loss = jnp.zeros((1, PAIR), f32)
    dscale = jnp.zeros((1, PAIR), f32)
    de_ref[...] = jnp.zeros(de_ref.shape, f32)
    for width in (EMB, EMB * 3 // 4, EMB // 2):
        kept = jnp.where(lanes < width, emb, 0.0)
        r_col = lax.rsqrt(jnp.sum(kept * kept, axis=1, keepdims=True) + 1e-06)
        kept_low = kept.astype(bf16)
        row_of = lax.broadcasted_iota(jnp.int32, (PAIR, tokens), 0)
        kept_t = jnp.where(row_of < width, emb_t, 0.0)
        r_row = lax.rsqrt(jnp.sum(kept_t * kept_t, axis=0, keepdims=True) + 1e-06)
        b_ref[16:24, :] = jnp.broadcast_to(r_row, (8, tokens))

        def sims(i, carry):
            at = pl.multiple_of(i * width_blk, width_blk)
            cols = pl.ds(at, width_blk)
            other = jnp.where(lanes[0:width_blk, :] < width, e_ref[cols, :], jnp.zeros((width_blk, PAIR), bf16))
            near = dot_nt(kept_low, other)
            expo = jnp.exp(near * r_col * (b_ref[16:17, cols] * (1.0 / sharpness)) - 1.0 / sharpness)
            sim_ref[:, cols] = expo
            ll_ref[:, cols] = dot_nn(member_t, expo.astype(bf16))
            return carry

        lax.fori_loop(0, tokens // width_blk, sims, 0)
        totals = ll_ref[...]
        sum_rows = lax.broadcasted_iota(jnp.int32, totals.shape, 0)
        totals = jnp.where(sum_rows < SEGS, totals, 1.0)
        soft = sharpness * jnp.log(totals) + 1.0
        score = jnp.dot(soft, member.astype(f32), precision=best, preferred_element_type=f32) / lengths
        logits = jnp.where(allowed, scale * score, -1e30)
        top = jnp.max(logits, axis=0, keepdims=True)
        powers = jnp.exp(logits - top)
        summed = jnp.sum(powers, axis=0, keepdims=True)
        picked = jnp.sum(jnp.where(chosen, logits, 0.0), axis=0, keepdims=True)
        live = seg[0:1, :] < SEGS
        loss = loss + jnp.where(live, top + jnp.log(summed) - picked, 0.0)
        dlogit = jnp.where(allowed, powers / summed - chosen.astype(f32), 0.0)
        dscale = dscale + jnp.sum(dlogit * jnp.where(allowed, logits, 0.0), axis=0, keepdims=True)
        dscore = dlogit * scale / lengths
        dsoft = jnp.dot(dscore, jnp.concatenate([member_t.astype(f32), jnp.zeros((PAIR - 16, tokens), f32)], axis=0),
                        precision=best, preferred_element_type=f32)
        coef = dsoft / totals
        b_ref[0:16, :] = coef
        coef_high, coef_rest = halves(coef)
        left = jnp.concatenate([member_t, member_t, coef_high, coef_rest], axis=0)
        keep_t = kept_t.astype(bf16)

        def pulls(i, carry):
            at = pl.multiple_of(i * width_blk, width_blk)
            cols = pl.ds(at, width_blk)
            here_high, here_rest = halves(b_ref[0:16, cols])
            member_here = (
                jnp.broadcast_to(segr_ref[0:1, cols], (16, width_blk)) == rows16[:, 0:width_blk]
            ).astype(bf16)
            right = jnp.concatenate([here_high, here_rest, member_here, member_here], axis=0)
            pull = dot_tn(left, right) * sim_ref[:, cols] * r_col
            high, rest = halves(pull)
            de = dot_nn(keep_t, high) + dot_nn(keep_t, rest)
            r_here = b_ref[16:17, cols]
            e_here = jnp.where(lanes[0:width_blk, :] < width, e_ref[cols, :].astype(f32), 0.0).T
            along = jnp.sum(e_here * de, axis=0, keepdims=True)
            de_ref[:, cols] += r_here * de - (r_here * r_here * r_here * along) * e_here
            return carry

        lax.fori_loop(0, mine // width_blk, pulls, 0)
    de = de_ref[...].T.astype(bf16)
    dx0_ref[...] = dot_nt(de[0:BLK, :], we_ref[...])
    dx1_ref[...] = dot_nt(de[BLK:HALF, :], we_ref[...])
    ge_ref[...] = dot_tn(x0_ref[...], de[0:BLK, :]) + dot_tn(x1_ref[...], de[BLK:HALF, :])
    out_ref[...] = jnp.concatenate([loss, dscale, jnp.zeros((6, PAIR), f32)], axis=0)


def loss_and_grads(log_scale, emb, seg_col, seg_row, lengths, partner, x0, x1, w_emb):
    blk = whole((BLK, D))
    return call(
        loss_kernel,
        (log_scale, emb, seg_col, seg_row, lengths, partner, x0, x1, w_emb),
        [
            smem(), whole((ROW_LEN, EMB)), whole((ROW_LEN, PAIR)), whole((8, ROW_LEN)),
            whole((8, PAIR)), whole((8, PAIR)), blk, blk, whole((D, EMB)),
        ],
        [((BLK, D), f32), ((BLK, D), f32), ((D, EMB), f32), ((8, PAIR), f32)],
        scratch=[
            pltpu.VMEM((ROW_LEN, ROW_LEN), f32),
            pltpu.VMEM((24, ROW_LEN), f32),
            pltpu.VMEM((16, ROW_LEN), f32),
            pltpu.VMEM((EMB, HALF), f32),
        ],
        flops=20 * ROW_LEN * ROW_LEN * EMB,
    )


def row_layout(lengths):
    ends = jnp.cumsum(lengths)
    places = jnp.arange(ROW_LEN, dtype=jnp.int32)
    after = places[:, None] >= ends[None, :]
    segment = jnp.sum(after.astype(jnp.int32), axis=1)
    starts = jnp.sum(jnp.where(after, lengths[None, :], 0), axis=1)
    return (segment, places - starts)


def adamw_update(master, moments, grad, factor, rate, step_f):
    scaled = grad * factor
    moment_one = 0.9 * moments[0] + 0.1 * scaled
    moment_two = 0.95 * moments[1] + 0.05 * scaled * scaled
    one_hat = moment_one / (1.0 - jnp.power(0.9, step_f))
    two_hat = moment_two / (1.0 - jnp.power(0.95, step_f))
    updated = master - rate * (one_hat / (jnp.sqrt(two_hat) + 1e-08) + 0.01 * master)
    return (updated, moment_one, moment_two)


def adam_kernel(rate, turned, k_ref, w_ref, m_ref, v_ref, g0_ref, g1_ref, wo_ref, mo_ref, vo_ref):
    grad = jnp.where(pl.program_id(0) == 0, g0_ref[...].astype(f32), g1_ref[...].astype(f32))
    if turned:
        grad = grad.T
    grad = (grad * k_ref[0]).reshape(w_ref.shape)
    one = 0.9 * m_ref[...].reshape(w_ref.shape) + 0.1 * grad
    two = 0.95 * v_ref[...].reshape(w_ref.shape) + 0.05 * grad * grad
    w = w_ref[...]
    one_hat = one * (1.0 / (1.0 - 0.9 ** STEP))
    two_hat = two * (1.0 / (1.0 - 0.95 ** STEP))
    wo_ref[...] = w - rate * (one_hat / (jnp.sqrt(two_hat) + 1e-08) + 0.01 * w)
    mo_ref[...] = one
    vo_ref[...] = two


def adam_step(factor, master, moments, grads, tiles, block, where_of, grad_block, grad_at, rate, turned=False):
    spec = pl.BlockSpec((1,) + block, lambda l, t: (l,) + where_of(t))
    first = pl.BlockSpec((1, 1) + block, lambda l, t: (0, l) + where_of(t))
    second = pl.BlockSpec((1, 1) + block, lambda l, t: (1, l) + where_of(t))
    at_zero, at_one = grad_at
    return call(
        functools.partial(adam_kernel, rate, turned),
        (factor, master, moments, moments, *grads),
        [
            smem(), spec, first, second,
            pl.BlockSpec(grad_block, lambda l, t: (0, at_zero + t)),
            pl.BlockSpec(grad_block, lambda l, t: (0, at_one + t)),
        ],
        [(master.shape, f32)] * 3,
        out_specs=[spec] * 3,
        grid=(LAYERS, tiles),
        flops=20 * master.size,
    )


def swap(values, axis, bit):
    count = lax.axis_size(axis)
    return lax.ppermute(values, axis, [(i, i ^ bit) for i in range(count)])


def bit_orders(axis):
    count = lax.axis_size(axis).bit_length() - 1
    return list(range(count)), list(range(1, count)) + [0]


def swap_core(values, pieces=2):
    parts = jnp.split(values, pieces, axis=0)
    return jnp.concatenate([swap(part, "mp", 1) for part in parts], axis=0)


def gather_rows(values, axis, order):
    index = lax.axis_index(axis)
    share = values.shape
    for bit in order:
        other = swap(values, axis, 1 << bit)
        high = ((index >> bit) & 1) == 1
        values = jnp.stack([jnp.where(high, other, values), jnp.where(high, values, other)])
    done = list(reversed(order))
    count = len(order)
    turn = [done.index(bit) for bit in reversed(range(count))]
    values = values.transpose(turn + [count, count + 1])
    return values.reshape((-1,) + share[1:])


def gather_both(values, axis):
    first, second = bit_orders(axis)
    cut = (values.shape[1] // 2 + PAIR - 1) // PAIR * PAIR
    parts = [
        gather_rows(values[:, :cut], axis, first[::-1]),
        gather_rows(values[:, cut:], axis, second[::-1]),
    ]
    return jnp.concatenate(parts, axis=1)


class Scatter:

    def __init__(self, values, axis, cut=None):
        orders = bit_orders(axis)
        count = len(orders[0])
        self.axis, self.index, self.steps = axis, lax.axis_index(axis), count
        cut = values.shape[1] // 2 if cut is None else cut
        parts = (values[:, :cut], values[:, cut:])
        self.parts = [p.reshape((2,) * count + (-1, p.shape[1])) for p in parts]
        self.left = [list(order) for order in orders]

    def send(self):
        self.kept, self.came = [], []
        for values, left in zip(self.parts, self.left):
            bit = left[0]
            high = ((self.index >> bit) & 1) == 1
            at = sum(1 for other in left if other > bit)
            low_part = lax.index_in_dim(values, 0, at, keepdims=False)
            high_part = lax.index_in_dim(values, 1, at, keepdims=False)
            self.kept.append(jnp.where(high, high_part, low_part))
            self.came.append(swap(jnp.where(high, low_part, high_part), self.axis, 1 << bit))

    def wait_with(self, other):
        first, second, other = lax.optimization_barrier((self.came[0], self.came[1], other))
        self.came = [first, second]
        return other

    def add(self):
        self.left = [left[1:] for left in self.left]
        parts = [k.astype(f32) + c.astype(f32) for k, c in zip(self.kept, self.came)]
        self.parts = parts if not self.left[0] else [p.astype(bf16) for p in parts]

    def result(self):
        return jnp.concatenate(self.parts, axis=1)


def sum_all(values):
    for axis in ("mp", "dp"):
        bit = 1
        while bit < lax.axis_size(axis):
            values = values + swap(values, axis, bit)
            bit *= 2
    return values


def body(
    hidden_in,
    seg_lengths,
    partner,
    qkv_weight,
    out_weight,
    up_weight,
    down_weight,
    norm_params,
    emb_weight,
    log_scale,
    qkv_moments,
    out_moments,
    up_moments,
    down_moments,
    norm_moments,
    emb_moments,
    scale_moments,
):
    share = qkv_weight.shape[1]
    mp_count = lax.axis_size("mp")
    place = lax.axis_index("mp")
    core = place & 1
    far_chip = (place >> 1) == 1
    core_arr = core.reshape(1).astype(jnp.int32)

    def mine(first, second):
        return jnp.where(far_chip, second, first)

    def attn_pack(layer_at):
        return [qkv_weight[layer_at].reshape(share, 3 * WIDE), out_weight[layer_at].T]

    def mlp_pack(layer_at):
        return [up_weight[layer_at], down_weight[layer_at].T]

    norm_cols = jnp.pad(norm_params.reshape(4 * LAYERS, share).T, ((0, 0), (0, PAIR - 4 * LAYERS)))

    def packed(parts):
        return jnp.concatenate(parts, axis=1).astype(bf16)

    def gather(values):
        return lax.all_gather(values, "dp", axis=0, tiled=True)

    first_w = gather_both(packed(attn_pack(0) + [norm_cols]), "dp")
    middle_w = gather(packed(attn_pack(1) + mlp_pack(0)))
    last_w = gather(packed(mlp_pack(1) + [emb_weight]))
    attn_w = [first_w, middle_w]
    mlp_w = [(middle_w, 1), (last_w, 0)]
    nrm = first_w[:, 4 * WIDE : 4 * WIDE + 4 * LAYERS].T.astype(f32)
    w_emb = last_w[:, 2 * HID :]

    segment, offset = row_layout(seg_lengths[0])

    def own_order(values):
        blocks = values.reshape(2, 2, BLK)
        return jnp.where(core == 1, blocks[:, ::-1], blocks).reshape(ROW_LEN)

    segment = own_order(segment).astype(f32)
    offset = own_order(offset).astype(f32)
    seg_col = jnp.broadcast_to(segment[:, None], (ROW_LEN, PAIR))
    seg_row = jnp.broadcast_to(segment[None, :], (8, ROW_LEN))
    lane = jnp.arange(PAIR, dtype=jnp.int32)
    frequency = jnp.exp((lane % (HEAD_DIM // 2)).astype(f32) * (-2.0 * math.log(10000.0) / HEAD_DIM))
    angles = offset[:, None] * frequency[None, :]
    cosines = jnp.cos(angles)
    sines = jnp.where((lane % HEAD_DIM) < HEAD_DIM // 2, -1.0, 1.0)[None, :] * jnp.sin(angles)

    other_half = swap(hidden_in, "mp", 2)
    low = [mine(hidden_in, other_half), mine(other_half, hidden_in)]
    stream = [v.astype(f32) for v in low]

    def chip_sum(own, send):
        return (own.astype(f32) + swap_core(send).astype(f32)).astype(bf16)

    def cross(total, earlier=None):
        if earlier is not None:
            total, earlier = lax.optimization_barrier((total, earlier))
        return total, swap(total, "mp", 2), earlier

    kept = []
    sums = None
    for layer_at in range(LAYERS):
        streams, qkvs, norm_prev = [], [], []
        if layer_at > 0:
            stream, low = [], []
        for at in range(2):
            if layer_at > 0:
                h, hb, zz = norm_fwd(4 * layer_at - 2, normed[at], *sums[at], nrm)
                stream.append(h)
                low.append(hb)
                kept[-1][-1].append(zz)
            sib = swap(low[at], "mp", 1)
            streams += [low[at], sib]
            qkvs.append(qkv_project(low[at], sib, attn_w[layer_at], cosines, sines, at))
        o_a, lse_a, own, send = attend(
            0, core_arr, qkvs[0], qkvs[1], seg_col, seg_row, attn_w[layer_at], None
        )
        total_a, came_a, _ = cross(chip_sum(own, send))
        o_b, lse_b, own, send = attend(
            1, core_arr, qkvs[1], qkvs[0], seg_col, seg_row, attn_w[layer_at], total_a
        )
        total_b, came_b, came_a = cross(chip_sum(own, send), came_a)
        h_a, hb_a, z_a = norm_fwd(4 * layer_at, stream[0], total_a, came_a, nrm)
        sib_a = swap(hb_a, "mp", 1)
        zg_a, own, send = mlp(hb_a, sib_a, mlp_w[layer_at], None)
        next_a, next_came_a, came_b = cross(chip_sum(own, send), came_b)
        h_b, hb_b, z_b = norm_fwd(4 * layer_at, stream[1], total_b, came_b, nrm)
        sib_b = swap(hb_b, "mp", 1)
        zg_b, own, send = mlp(hb_b, sib_b, mlp_w[layer_at], None)
        next_b, next_came_b, next_came_a = cross(chip_sum(own, send), next_came_a)
        normed = [h_a, h_b]
        sums = [(next_a, next_came_a), (next_b, next_came_b)]
        kept.append(
            (streams, qkvs, [(o_a, lse_a), (o_b, lse_b)], [z_a, z_b], [hb_a, sib_a, hb_b, sib_b], [zg_a, zg_b], [])
        )
    stream, low = [], []
    for at in range(2):
        h, hb, zz = norm_fwd(4 * LAYERS - 2, normed[at], *sums[at], nrm)
        stream.append(h)
        low.append(hb)
        kept[-1][-1].append(zz)
    hidden_out = mine(stream[0], stream[1])

    emb_own = jnp.concatenate([dot_nn(low[0], w_emb), dot_nn(low[1], w_emb)], axis=0).astype(bf16)
    emb_all = jnp.concatenate([emb_own, swap(emb_own, "mp", 1)], axis=0)

    def loss_order(values):
        return values.reshape(2, 2, BLK).transpose(1, 0, 2).reshape(ROW_LEN)

    loss_seg = loss_order(segment)
    lengths = jnp.broadcast_to(
        jnp.pad(seg_lengths[0].astype(f32), (0, PAIR - SEGS), constant_values=1.0)[None], (8, PAIR)
    )
    partners = jnp.broadcast_to(
        jnp.pad(partner[0].astype(f32), (0, PAIR - SEGS), constant_values=-1.0)[None], (8, PAIR)
    )
    dx0, dx1, g_emb, loss_parts = loss_and_grads(
        log_scale,
        emb_all,
        jnp.broadcast_to(loss_seg[:, None], (ROW_LEN, PAIR)),
        jnp.broadcast_to(loss_seg[None, :], (8, ROW_LEN)),
        lengths,
        partners,
        low[0],
        low[1],
        w_emb,
    )

    grads = [dx0, dx1]
    pending = [(), ()]
    reduced = []
    norm_grads = [None] * LAYERS
    for layer_at in reversed(range(LAYERS)):
        streams, qkvs, attended, norm_a, hiddens, zgs, norm_b = kept[layer_at]
        row = 4 * layer_at + 2
        d_a, db_a, gain_a = norm_bwd(row, grads[0], pending[0], norm_b[0], nrm)
        sib_a = swap(db_a, "mp", 1)
        du_a, own, send = mlp_back(db_a, sib_a, zgs[0], mlp_w[layer_at], None)
        total_a = chip_sum(own, send)
        if pending[1]:
            total_a, came_a, came_b = cross(total_a, pending[1][1])
            if upper.left[0]:
                came_b = upper.wait_with(came_b)
                upper.add()
                upper.send()
            pending[1] = (pending[1][0], came_b)
        else:
            total_a, came_a, _ = cross(total_a)
        d_b, db_b, gain_b = norm_bwd(row, grads[1], pending[1], norm_b[1], nrm)
        sib_b = swap(db_b, "mp", 1)
        du_b, own, send = mlp_back(db_b, sib_b, zgs[1], mlp_w[layer_at], total_a)
        total_b, came_b, came_a = cross(chip_sum(own, send), came_a)
        if layer_at < LAYERS - 1:
            came_a = upper.wait_with(came_a)
            upper.add()
            upper.send()
        gains = [(gain_a + gain_b)[:2]]
        both = mlp_grads(hiddens, [db_a, sib_a, db_b, sib_b], [du_a, du_b], zgs, total_b)
        reduced.append(lax.psum_scatter(both, "dp", scatter_dimension=0, tiled=True))
        row = 4 * layer_at
        grad_a, low_a, gain_a = norm_bwd(row, d_a, (total_a, came_a), norm_a[0], nrm)
        sib_a = swap(low_a, "mp", 1)
        if layer_at < LAYERS - 1:
            came_b = upper.wait_with(came_b)
            upper.add()
            while upper.left[0]:
                upper.send()
                upper.add()
        grad_b, low_b, gain_b = norm_bwd(row, d_b, (total_b, came_b), norm_a[1], nrm)
        dattn = [low_a, sib_a, low_b, swap(low_b, "mp", 1)]
        dmixes = attend_back(
            core_arr, dattn, attn_w[layer_at], *qkvs, attended[0][0], attended[1][0],
            attended[0][1], attended[1][1], seg_col, seg_row, cosines, sines,
        )
        norm_grads[layer_at] = jnp.concatenate([(gain_a + gain_b)[:2]] + gains, axis=0)
        outs = [attended[0][0], attended[1][0]]
        grads = [grad_a, grad_b]
        if layer_at > 0:
            total_a, came_a, _ = cross(chip_sum(*qkv_back(dmixes[0], attn_w[layer_at], None)))
            total_b, came_b, came_a = cross(
                chip_sum(*qkv_back(dmixes[1], attn_w[layer_at], total_a)), came_a
            )
            pending = [(total_a, came_a), (total_b, came_b)]
            upper = Scatter(attn_grads(streams, dattn, dmixes, outs, total_a), "dp")
            upper.send()
        else:
            norm_rows = jnp.concatenate(norm_grads, axis=0)
            small = jnp.concatenate([g_emb, jnp.pad(norm_rows.T, ((0, 0), (0, PAIR - 4 * LAYERS)))], axis=1)
            last = attn_grads(streams, dattn, dmixes, outs, None, small.astype(bf16))
            lower = Scatter(last, "dp")
            fourth = upper.result()
            squares = jnp.sum(jnp.square(reduced[0].astype(f32))) + jnp.sum(jnp.square(fourth))
            while lower.left[0]:
                lower.send()
                if len(lower.left[0]) == lower.steps:
                    squares = lower.wait_with(squares)
                lower.add()
            third = lower.result()
            totals = []
            for at in range(2):
                own, send = qkv_back(dmixes[at], attn_w[layer_at], last)
                totals.append(own.astype(f32) + swap(send, "mp", 1).astype(f32))
            came = swap(mine(totals[1], totals[0]).astype(bf16), "mp", 2)
            hidden_grad = mine(grads[0], grads[1]) + (mine(totals[0], totals[1]) + came.astype(f32))

    first, second = reduced
    third, hidden_grad = lax.optimization_barrier((third, hidden_grad))
    small = third[:, 4 * WIDE :]
    small = small + swap(small, "mp", 1)
    emb_grad = small[:, :EMB]
    norm_grad = small[:, EMB : EMB + 4 * LAYERS].T.reshape(LAYERS, 2, 2, share)
    squares = (
        squares + jnp.sum(jnp.square(second.astype(f32))) + jnp.sum(jnp.square(third[:, : 4 * WIDE]))
        + jnp.sum(small * small) / mp_count
    )
    parts = jnp.concatenate([loss_parts[:2], jnp.zeros((6, PAIR), f32)], axis=0)
    loss_here = jnp.sum(parts[0]) / mp_count
    dscale_here = jnp.sum(parts[1]) / mp_count
    vector = jnp.where(lane == 0, squares, jnp.where(lane == 1, dscale_here, jnp.where(lane == 2, loss_here, 0.0)))
    vector = sum_all(jnp.broadcast_to(vector[None], (8, PAIR)))
    total_squares = vector[0, 0]
    scale_grad = vector[0, 1:2]
    loss_total = vector[0, 2]
    norm_value = jnp.sqrt(total_squares + scale_grad[0] * scale_grad[0] + 1e-06)
    factor = clip_limit / jnp.maximum(norm_value, clip_limit)
    step_f = jnp.asarray(STEP, f32)
    factor_arr = factor.reshape(1)
    qkv_step = adam_step(
        factor_arr, qkv_weight.transpose(0, 2, 1, 3), qkv_moments.transpose(0, 1, 3, 2, 4), (third, fourth),
        3, (1, share, WIDE), lambda t: (t, 0, 0), (share, WIDE), (0, 0), D ** (-0.5),
    )
    qkv_new, qkv_first, qkv_second = [v.transpose(0, 2, 1, 3) for v in qkv_step]
    out_new, out_first, out_second = adam_step(
        factor_arr, out_weight, out_moments, (third, fourth),
        1, (WIDE, share), lambda t: (t, 0), (share, WIDE), (3, 3), (D * SEGS // ROW_LEN) ** (-0.5), True,
    )
    up_new, up_first, up_second = adam_step(
        factor_arr, up_weight, up_moments, (second, first),
        2, (share, HALF), lambda t: (0, t), (share, HALF), (0, 0), D ** (-0.5),
    )
    down_new, down_first, down_second = adam_step(
        factor_arr, down_weight, down_moments, (second, first),
        4, (TILE, share), lambda t: (t, 0), (share, TILE), (4, 4), FF ** (-0.5), True,
    )
    norm_new, norm_first, norm_second = adamw_update(norm_params, norm_moments, norm_grad, factor, 0.5, step_f)
    emb_new, emb_first, emb_second = adamw_update(emb_weight, emb_moments, emb_grad, factor, D ** (-0.5), step_f)
    scale_new, scale_first, scale_second = adamw_update(log_scale, scale_moments, scale_grad, factor, 1.0, step_f)
    return (
        hidden_out,
        hidden_grad,
        loss_total.reshape(1),
        norm_value.reshape(1),
        qkv_new,
        qkv_first,
        qkv_second,
        out_new,
        out_first,
        out_second,
        up_new,
        up_first,
        up_second,
        down_new,
        down_first,
        down_second,
        norm_new,
        norm_first,
        norm_second,
        emb_new,
        emb_first,
        emb_second,
        scale_new,
        scale_first,
        scale_second,
    )


def solution(mesh):
    placed = (
        P(("dp", "mp"), None),
        P("dp", None),
        P("dp", None),
        P(None, "dp", None, "mp"),
        P(None, "mp", "dp"),
        P(None, "dp", "mp"),
        P(None, "mp", "dp"),
        P(None, None, None, "dp"),
        P("dp", None),
        P(),
        P(None, None, "dp", None, "mp"),
        P(None, None, "mp", "dp"),
        P(None, None, "dp", "mp"),
        P(None, None, "mp", "dp"),
        P(None, None, None, None, "dp"),
        P(None, "dp", None),
        P(),
    )
    results = (P(("dp", "mp"), None), P(("dp", "mp"), None), P(), P())
    for at in (3, 4, 5, 6, 7, 8, 9):
        results += (placed[at],) * 3
    return jax.shard_map(body, mesh=mesh, in_specs=placed, out_specs=results, check_vma=False)
```

time: 1650 us -> 592 us (0.36)
  waiting for transfers between devices: 1010 us -> 209 us
  matrix products: 285 us -> 0.57 us
  Pallas kernels: 0 us -> 177 us
  blocking collectives: 96.1 us -> 0 us
  starting transfers between devices: 2.83 us -> 77.6 us
  other arithmetic: 99.9 us -> 45 us
  local copies, waits for them, and re-layouts: 93.8 us -> 45.4 us
    reduce_scatter x13 -> x2, waiting for transfers between devices: 621 us -> 0.02 us  [body(): lax.psum_scatter(both, 'dp', scatter_dimension=0, tiled=True)]
    all_gather x12 -> x2, waiting for transfers between devices: 393 us -> 6.32 us  [gather(): return lax.all_gather(values, 'dp', axis=0, tiled=True)]
    dot_general x76 -> x2, matrix products: 285 us -> 0.57 us  [dot_nn(): lax.dot_general(left, right, (((1,), (0,)), ((), ())), preferred_element_...]
    ppermute x0 -> x87, waiting for transfers between devices: none -> 203 us  [swap(): return lax.ppermute(values, axis, [(i, i ^ bit) for i in range(count)])]
    pallas_call x0 -> x47, Pallas kernels: none -> 177 us  [call(): pl.pallas_call(body_fn, grid=grid, in_specs=in_specs, out_specs=out_specs...]
    ppermute x0 -> x87, starting transfers between devices: none -> 77.2 us  [swap(): return lax.ppermute(values, axis, [(i, i ^ bit) for i in range(count)])]
    all_gather x3 -> x0, blocking collectives: 55.4 us -> none  [the longest x1 30.8 us: body(): lax.all_gather(emb_weight.astype(jnp.bfloat16), 'dp', axis=0, tiled=True)]
    dynamic_update_slice x8 -> x0, local copies, waits for them, and re-layouts: 43.7 us -> none  [attend_forward(): lax.map(one_block, jnp.arange(block_count, dtype=jnp.int32))]
  transfers between devices with their start and end apart: 26 -> 91, of which waited for: 22 -> 59; matrix products, arithmetic and copies ran while one was open for 12% -> 9% of each run, Pallas kernels for 0% -> 24%
where the time goes in v1:
time: 592 us; the launch traced here: 585 us
  waiting for transfers between devices  209 us (35%)
  Pallas kernels  177 us (30%)
  starting transfers between devices  77.6 us (13%)
  local copies, waits for them, and re-layouts  45.4 us (8%)
  other arithmetic  45 us (8%)
  between operations  29.7 us (5%)
    ppermute x87, waiting for transfers between devices, swap(): return lax.ppermute(values, axis, [(i, i ^ bit) for i in range(count)])  203 us
    pallas_call x47, Pallas kernels, call(): pl.pallas_call(body_fn, grid=grid, in_specs=in_specs, out_specs=out_specs...  177 us
    ppermute x87, starting transfers between devices, swap(): return lax.ppermute(values, axis, [(i, i ^ bit) for i in range(count)])  77.2 us
    unnamed x222, local copies, waits for them, and re-layouts  34.2 us
  transfers between devices with their start and end apart: 91, of which 59 were waited for; matrix products, arithmetic and copies ran while one was open for 9% of the time, Pallas kernels for 24%

profile of v1, /device:TPU:0, one launch (start us, length us, event | category | flops | bytes accessed | tf_op | source)
XLA Modules:
  0.0 584.9 jit_solution(4314618985460264557)
XLA Ops:
  25.7 12.3 %collective-permute-start.3 = (bf16[2,128,640]{1,2,0:T(8,128)(2,1)S(1)}, bf16[2,128,640]{1,2,0:T(8,128)(2,1)S(1)}, u32[]{:S(2)}, u32[]{:S(2)}) collective-permute-start(bf16[2,128,640]{1,2,0:T(8,128)(2,1)S(1)} %pad_maximum_fusion.7), channel_id=1, source_target_pairs={{0,8},{4,12},{8,0},{12,4},{16,24},{20,28},{24,16},{28,20},{1,9},{5... | collective-permute-start | bytes 983048 | tf_op jit(solution)/shard_map/ppermute | solution.py:721
  38.0 11.9 %collective-permute-done.6 = bf16[2,128,512]{1,2,0:T(8,128)(2,1)S(1)} collective-permute-done((bf16[2,128,512]{1,2,0:T(8,128)(2,1)S(1)}, bf16[2,128,512]{1,2,0:T(8,128)(2,1)S(1)}, u32[]{:S(2)}, u32[]{:S(2)}) %collective-permute-start.6) | collective-permute-done | bytes 262176 | tf_op jit(solution)/shard_map/ppermute | solution.py:721
  50.0 3.8 collective-permute-start.7
  53.7 13.0 %collective-permute-done.3 = bf16[2,128,640]{1,2,0:T(8,128)(2,1)S(1)} collective-permute-done((bf16[2,128,640]{1,2,0:T(8,128)(2,1)S(1)}, bf16[2,128,640]{1,2,0:T(8,128)(2,1)S(1)}, u32[]{:S(2)}, u32[]{:S(2)}) %collective-permute-start.3) | collective-permute-done | bytes 327712 | tf_op jit(solution)/shard_map/ppermute | solution.py:721
  71.4 8.5 %collective-permute-done.7 = bf16[2,2,128,512]{2,3,1,0:T(8,128)(2,1)S(1)} collective-permute-done((bf16[2,2,128,512]{2,3,1,0:T(8,128)(2,1)S(1)}, bf16[2,2,128,512]{2,3,1,0:T(8,128)(2,1)S(1)}, u32[]{:S(2)}, u32[]{:S(2)}) %collective-permute-start.7) | collective-permute-done | bytes 524320 | tf_op jit(solution)/shard_map/ppermute | solution.py:721
  83.3 8.4 %collective-permute-done.4 = bf16[2,2,128,640]{2,3,1,0:T(8,128)(2,1)} collective-permute-done((bf16[2,2,128,640]{2,3,1,0:T(8,128)(2,1)}, bf16[2,2,128,640]{2,3,1,0:T(8,128)(2,1)}, u32[]{:S(2)}, u32[]{:S(2)}) %collective-permute-start.4) | collective-permute-done | bytes 655392 | tf_op jit(solution)/shard_map/ppermute | solution.py:721
  98.7 3.4 shard_map.360.mo_ref.refs_1_.mix1
  102.1 3.1 shard_map.361.m_ref.refs_2_.mix0
  105.4 5.7 shard_map.362
  113.3 4.1 collective-permute-start.13
  117.4 5.8 shard_map.363
  143.3 4.7 shard_map.365
  155.0 4.3 shard_map.367
  162.3 5.1 collective-permute-done.21.refs_2_
  170.5 10.6 %collective-permute-done.22.refs_2_ = bf16[256,1024]{1,0:T(8,128)(2,1)S(1)} collective-permute-done((bf16[256,1024]{1,0:T(8,128)(2,1)S(1)}, bf16[256,1024]{1,0:T(8,128)(2,1)S(1)}, u32[]{:S(2)}, u32[]{:S(2)}) %collective-permute-start.22) | collective-permute-done | bytes 524320 | tf_op jit(solution)/shard_map/ppermute | solution.py:721
  187.3 5.9 %shard_map.372 = (bf16[512,256]{1,0:T(8,128)(2,1)}, f32[8,512]{1,0:T(8,128)}, bf16[256,1024]{1,0:T(8,128)(2,1)S(1)}, bf16[256,1024]{1,0:T(8,128)(2,1)S(1)}) custom-call(s32[1]{0:T(128)} %bitcast.core_ref.refs_0_, bf16[512,768]{1,0:T(8,128)(2,1)} %shard_map.371.m_ref.refs_2_.mix0, bf16[512,768]{1,0:T(8,128)(2,1)} %shard_map.369.mo_ref.refs_1_.mix1, ...), custom_call_target="tpu_custom_call" | custom-call | flops 939524096 | bytes 3981316 | tf_op jit(solution)/shard_map/pallas_call | solution.py:74
  197.1 5.7 shard_map.373
  205.1 4.7 collective-permute-done.29.refs_2_
  213.6 4.2 all-gather.5.cloned.1.call-done.up_ref.down_ref.refs_3_.refs_4_
  220.1 5.4 shard_map.375
  232.0 4.7 shard_map.377
  239.0 5.5 collective-permute-done.37.refs_2_
  249.2 8.6 %collective-permute-done.38.refs_2_ = bf16[256,1024]{1,0:T(8,128)(2,1)S(1)} collective-permute-done((bf16[256,1024]{1,0:T(8,128)(2,1)S(1)}, bf16[256,1024]{1,0:T(8,128)(2,1)S(1)}, u32[]{:S(2)}, u32[]{:S(2)}) %collective-permute-start.38) | collective-permute-done | bytes 524320 | tf_op jit(solution)/shard_map/ppermute | solution.py:721
  262.1 14.7 %shard_map.380 = (f32[256,1024]{1,0:T(8,128)S(1)}, f32[256,1024]{1,0:T(8,128)S(1)}, f32[1024,128]{1,0:T(8,128)S(1)}, f32[8,128]{1,0:T(8,128)S(1)}) custom-call(f32[1]{0:T(128)S(6)} %copy.245.ls_ref, bf16[1024,128]{1,0:T(8,128)(2,1)S(1)} %pad_maximum_fusion.9.e_ref, f32[1024,128]{1,0:T(8,128)S(1)} %broadcast_in_dim.92.seg_ref, ...), custom_call_target="tpu_custom_call" | custom-call | flops 2684354560 | bytes 4763652 | tf_op jit(solution)/shard_map/pallas_call | solution.py:74
  281.9 3.6 shard_map.382
  289.2 3.7 shard_map.384
  295.2 6.7 %collective-permute-done.46.refs_2_ = bf16[256,1024]{1,0:T(8,128)(2,1)S(1)} collective-permute-done((bf16[256,1024]{1,0:T(8,128)(2,1)S(1)}, bf16[256,1024]{1,0:T(8,128)(2,1)S(1)}, u32[]{:S(2)}, u32[]{:S(2)}) %collective-permute-start.46) | collective-permute-done | bytes 524320 | tf_op jit(solution)/shard_map/ppermute | solution.py:721
  302.7 8.8 %shard_map.399 = bf16[1024,2048]{1,0:T(8,128)(2,1)} custom-call(bf16[256,1024]{1,0:T(8,128)(2,1)S(1)} %get-tuple-element.203.ho_ref.refs_0_, bf16[256,1024]{1,0:T(8,128)(2,1)} %collective-permute-done.30.hs_ref.refs_1_, bf16[256,1024]{1,0:T(8,128)(2,1)S(1)} %get-tuple-element.208.ho_ref.refs_2_, ...), custom_call_target="tpu_custom_call" | custom-call | flops 4294967296 | bytes 14680064 | tf_op jit(solution)/shard_map/pallas_call | solution.py:74
  319.4 6.7 %collective-permute-done.48.refs_2_ = bf16[256,1024]{1,0:T(8,128)(2,1)S(1)} collective-permute-done((bf16[256,1024]{1,0:T(8,128)(2,1)}, bf16[256,1024]{1,0:T(8,128)(2,1)S(1)}, u32[]{:S(2)}, u32[]{:S(2)}) %collective-permute-start.48) | collective-permute-done | bytes 524320 | tf_op jit(solution)/shard_map/ppermute | solution.py:721
  332.7 10.6 %shard_map.387 = (bf16[512,768]{1,0:T(8,128)(2,1)S(1)}, bf16[512,768]{1,0:T(8,128)(2,1)S(1)}) custom-call(s32[1]{0:T(128)} %bitcast.core_ref.refs_0_, bf16[256,1024]{1,0:T(8,128)(2,1)S(1)} %get-tuple-element.235.d0o.refs_4_, bf16[256,1024]{1,0:T(8,128)(2,1)S(1)} %collective-permute-done.47.d0s.refs_5_, bf16[256,1024]{1,0:T(8,128)(2,1)S(1)} %get-tuple-element.239.d1o.refs_6_, ...), custom_call_target="tpu_custom_call" | custom-call | flops 3892314112 | bytes 7405572 | tf_op jit(solution)/shard_map/pallas_call | solution.py:74
  350.3 4.6 shard_map.392
  356.2 4.6 collective-permute-done.54.refs_2_
  365.5 3.6 shard_map.391
  371.3 6.1 %collective-permute-done.58.refs_2_ = bf16[256,1024]{1,0:T(8,128)(2,1)S(1)} collective-permute-done((bf16[256,1024]{1,0:T(8,128)(2,1)S(1)}, bf16[256,1024]{1,0:T(8,128)(2,1)S(1)}, u32[]{:S(2)}, u32[]{:S(2)}) %collective-permute-start.58) | collective-permute-done | bytes 524320 | tf_op jit(solution)/shard_map/ppermute | solution.py:721
  385.1 3.7 shard_map.394
  391.1 5.7 collective-permute-done.66.refs_2_
  397.6 8.0 %shard_map.402 = bf16[1024,2048]{1,0:T(8,128)(2,1)} custom-call(bf16[256,1024]{1,0:T(8,128)(2,1)S(1)} %copy-done.75, bf16[256,1024]{1,0:T(8,128)(2,1)S(1)} %copy-done.78, bf16[256,1024]{1,0:T(8,128)(2,1)S(1)} %copy-done.80, bf16[256,1024]{1,0:T(8,128)(2,1)S(1)} %copy-done.82, bf16[256,1024]{1,0:T(8,128)(2,1)S(1)} %get-tuple-element.253.do_ref.refs_4_, ...), custom_call_target="tpu_custom_call" | custom-call | flops 4294967296 | bytes 14680064 | tf_op jit(solution)/shard_map/pallas_call | solution.py:74
  414.3 11.5 %collective-permute-done.61 = bf16[2,128,512]{2,1,0:T(8,128)(2,1)} collective-permute-done((bf16[2,128,512]{2,1,0:T(8,128)(2,1)}, bf16[2,128,512]{2,1,0:T(8,128)(2,1)}, u32[]{:S(2)}, u32[]{:S(2)}) %collective-permute-start.61) | collective-permute-done | bytes 262176 | tf_op jit(solution)/shard_map/ppermute | solution.py:721
  435.3 7.8 %collective-permute-done.68 = bf16[128,512]{1,0:T(8,128)(2,1)S(1)} collective-permute-done((bf16[128,512]{1,0:T(8,128)(2,1)S(1)}, bf16[128,512]{1,0:T(8,128)(2,1)S(1)}, u32[]{:S(2)}, u32[]{:S(2)}) %collective-permute-start.68) | collective-permute-done | bytes 131104 | tf_op jit(solution)/shard_map/ppermute | solution.py:721
  450.7 11.3 %shard_map.397 = (bf16[512,768]{1,0:T(8,128)(2,1)S(1)}, bf16[512,768]{1,0:T(8,128)(2,1)S(1)}) custom-call(s32[1]{0:T(128)} %bitcast.core_ref.refs_0_, bf16[256,1024]{1,0:T(8,128)(2,1)} %get-tuple-element.272.d0o.d0, bf16[256,1024]{1,0:T(8,128)(2,1)} %collective-permute-done.67.d0s.d1, bf16[256,1024]{1,0:T(8,128)(2,1)} %get-tuple-element.279.d1o.d2, ...), custom_call_target="tpu_custom_call" | custom-call | flops 3892314112 | bytes 9764868 | tf_op jit(solution)/shard_map/pallas_call | solution.py:74
  462.0 6.8 %shard_map.398.refs_2_ = bf16[1024,1280]{1,0:T(8,128)(2,1)S(1)} custom-call(bf16[256,1024]{1,0:T(8,128)(2,1)S(1)} %copy-done.14, bf16[256,1024]{1,0:T(8,128)(2,1)} %collective-permute-done.8.xs_ref.x1, bf16[256,1024]{1,0:T(8,128)(2,1)S(1)} %copy-done.16, bf16[256,1024]{1,0:T(8,128)(2,1)} %collective-permute-done.1.xs_ref.x3, ...), custom_call_target="tpu_custom_call" | custom-call | flops 2147483648 | bytes 9437184 | tf_op jit(solution)/shard_map/pallas_call | solution.py:74
  477.1 10.7 %collective-permute-done.80 = bf16[256,1024]{1,0:T(8,128)(2,1)S(1)} collective-permute-done((bf16[256,1024]{1,0:T(8,128)(2,1)S(1)}, bf16[256,1024]{1,0:T(8,128)(2,1)S(1)}, u32[]{:S(2)}, u32[]{:S(2)}) %collective-permute-start.80) | collective-permute-done | bytes 524320 | tf_op jit(solution)/shard_map/ppermute | solution.py:721
  492.6 4.7 collective-permute-done.72
  498.7 3.2 collective-permute-start.76
  503.5 19.2 %collective-permute-done.76 = bf16[2,128,640]{2,1,0:T(8,128)(2,1)S(1)} collective-permute-done((bf16[2,128,640]{2,1,0:T(8,128)(2,1)S(1)}, bf16[2,128,640]{2,1,0:T(8,128)(2,1)S(1)}, u32[]{:S(2)}, u32[]{:S(2)}) %collective-permute-start.76) | collective-permute-done | bytes 327712 | tf_op jit(solution)/shard_map/ppermute | solution.py:721
  523.9 4.6 collective-permute-done.77
  528.5 3.7 collective-permute-done.75
  566.8 4.0 shard_map.406
  (554 shorter events, 227.3 us)
Async XLA Ops:
  7.2 131.3 %all-gather.3.cloned.1.call-start = ((), (), s32[]{:S(2)}) async-start(), calls=%async_computation.2 | async-start | bytes 7077888 | tf_op jit(solution)/shard_map/all_gather | solution.py:844
  12.3 205.6 %all-gather.5.cloned.1.call-start = ((), (), s32[]{:S(2)}) async-start(), calls=%async_computation.3 | async-start | bytes 5013504 | tf_op jit(solution)/shard_map/all_gather | solution.py:844
  12.5 10.7 %collective-permute-start.5 = (bf16[128,512]{0,1:T(8,128)(2,1)S(1)}, bf16[128,512]{0,1:T(8,128)(2,1)S(1)}, u32[]{:S(2)}, u32[]{:S(2)}) collective-permute-start(bf16[128,512]{0,1:T(8,128)(2,1)S(1)} %fusion.12), channel_id=1, source_target_pairs={{0,4},{4,0},{8,12},{12,8},{16,20},{20,16},{24,28},{28,24},{1,5},{5... | collective-permute-start | bytes 393224 | tf_op jit(solution)/shard_map/ppermute | solution.py:721
  15.5 10.1 %collective-permute-start.2 = (bf16[128,640]{0,1:T(8,128)(2,1)S(1)}, bf16[128,640]{0,1:T(8,128)(2,1)S(1)}, u32[]{:S(2)}, u32[]{:S(2)}) collective-permute-start(bf16[128,640]{0,1:T(8,128)(2,1)S(1)} %slice.253), channel_id=1, source_target_pairs={{0,16},{4,20},{8,24},{12,28},{16,0},{20,4},{24,8},{28,12},{1,17},{... | collective-permute-start | bytes 491528 | tf_op jit(solution)/shard_map/ppermute | solution.py:721
  18.2 50.3 %collective-permute-start = (bf16[256,1024]{1,0:T(8,128)(2,1)}, bf16[256,1024]{1,0:T(8,128)(2,1)}, u32[]{:S(2)}, u32[]{:S(2)}) collective-permute-start(bf16[256,1024]{1,0:T(8,128)(2,1)} %param.17), channel_id=1, source_target_pairs={{0,2},{1,3},{2,0},{3,1},{4,6},{5,7},{6,4},{7,5},{8,10},{9,11},{10,... | collective-permute-start | bytes 1572872 | tf_op jit(solution)/shard_map/ppermute | solution.py:721
  20.6 468.8 %reduce-scatter.3.cloned.1.call-start = ((), (), s32[]{:S(2)}) async-start(), calls=%async_computation.4 | async-start | bytes 4718592 | tf_op jit(solution)/shard_map/reduce_scatter | solution.py:981
  23.2 26.7 %collective-permute-start.6 = (bf16[2,128,512]{1,2,0:T(8,128)(2,1)S(1)}, bf16[2,128,512]{1,2,0:T(8,128)(2,1)S(1)}, u32[]{:S(2)}, u32[]{:S(2)}) collective-permute-start(bf16[2,128,512]{1,2,0:T(8,128)(2,1)S(1)} %pad_maximum_fusion.8), channel_id=1, source_target_pairs={{0,16},{4,20},{8,24},{12,28},{16,0},{20,4},{24,8},{28,12},{1,17},{... | collective-permute-start | bytes 786440 | tf_op jit(solution)/shard_map/ppermute | solution.py:721
  25.7 41.1 %collective-permute-start.3 = (bf16[2,128,640]{1,2,0:T(8,128)(2,1)S(1)}, bf16[2,128,640]{1,2,0:T(8,128)(2,1)S(1)}, u32[]{:S(2)}, u32[]{:S(2)}) collective-permute-start(bf16[2,128,640]{1,2,0:T(8,128)(2,1)S(1)} %pad_maximum_fusion.7), channel_id=1, source_target_pairs={{0,8},{4,12},{8,0},{12,4},{16,24},{20,28},{24,16},{28,20},{1,9},{5... | collective-permute-start | bytes 983048 | tf_op jit(solution)/shard_map/ppermute | solution.py:721
  50.0 29.9 %collective-permute-start.7 = (bf16[2,2,128,512]{2,3,1,0:T(8,128)(2,1)S(1)}, bf16[2,2,128,512]{2,3,1,0:T(8,128)(2,1)S(1)}, u32[]{:S(2)}, u32[]{:S(2)}) collective-permute-start(bf16[2,2,128,512]{2,3,1,0:T(8,128)(2,1)S(1)} %pad_maximum_fusion.5), channel_id=1, source_target_pairs={{0,8},{4,12},{8,0},{12,4},{16,24},{20,28},{24,16},{28,20},{1,9},{5... | collective-permute-start | bytes 1572872 | tf_op jit(solution)/shard_map/ppermute | solution.py:721
  67.8 23.9 %collective-permute-start.4 = (bf16[2,2,128,640]{2,3,1,0:T(8,128)(2,1)}, bf16[2,2,128,640]{2,3,1,0:T(8,128)(2,1)}, u32[]{:S(2)}, u32[]{:S(2)}) collective-permute-start(bf16[2,2,128,640]{2,3,1,0:T(8,128)(2,1)} %pad_maximum_fusion.2), channel_id=1, source_target_pairs={{0,4},{4,0},{8,12},{12,8},{16,20},{20,16},{24,28},{28,24},{1,5},{5... | collective-permute-start | bytes 1966088 | tf_op jit(solution)/shard_map/ppermute | solution.py:721
  70.9 31.2 %collective-permute-start.8 = (bf16[256,1024]{1,0:T(8,128)(2,1)S(1)}, bf16[256,1024]{1,0:T(8,128)(2,1)}, u32[]{:S(2)}, u32[]{:S(2)}) collective-permute-start(bf16[256,1024]{1,0:T(8,128)(2,1)S(1)} %get-tuple-element.338.xo_ref.x0), channel_id=1, source_target_pairs={{0,1},{1,0},{2,3},{3,2},{4,5},{5,4},{6,7},{7,6},{8,9},{9,8},{10,11... | collective-permute-start | bytes 1572872 | tf_op jit(solution)/shard_map/ppermute | solution.py:721
  70.9 27.7 %collective-permute-start.1 = (bf16[256,1024]{1,0:T(8,128)(2,1)S(1)}, bf16[256,1024]{1,0:T(8,128)(2,1)}, u32[]{:S(2)}, u32[]{:S(2)}) collective-permute-start(bf16[256,1024]{1,0:T(8,128)(2,1)S(1)} %get-tuple-element.352.xo_ref.x2), channel_id=1, source_target_pairs={{0,1},{1,0},{2,3},{3,2},{4,5},{5,4},{6,7},{7,6},{8,9},{9,8},{10,11... | collective-permute-start | bytes 1572872 | tf_op jit(solution)/shard_map/ppermute | solution.py:721
  113.3 16.5 %collective-permute-start.13 = (bf16[256,1024]{1,0:T(8,128)(2,1)S(1)}, bf16[256,1024]{1,0:T(8,128)(2,1)}, u32[]{:S(2)}, u32[]{:S(2)}) collective-permute-start(bf16[256,1024]{1,0:T(8,128)(2,1)S(1)} %add_convert_fusion.13.refs_7_.refs_1_), channel_id=1, source_target_pairs={{0,2},{1,3},{2,0},{3,1},{4,6},{5,7},{6,4},{7,5},{8,10},{9,11},{10,... | collective-permute-start | bytes 1572872 | tf_op jit(solution)/shard_map/ppermute | solution.py:721
  133.9 16.3 %collective-permute-start.17 = (bf16[256,1024]{1,0:T(8,128)(2,1)}, bf16[256,1024]{1,0:T(8,128)(2,1)}, u32[]{:S(2)}, u32[]{:S(2)}) collective-permute-start(bf16[256,1024]{1,0:T(8,128)(2,1)} %add_convert_fusion.12.refs_1_), channel_id=1, source_target_pairs={{0,2},{1,3},{2,0},{3,1},{4,6},{5,7},{6,4},{7,5},{8,10},{9,11},{10,... | collective-permute-start | bytes 1572872 | tf_op jit(solution)/shard_map/ppermute | solution.py:721
  152.9 14.5 %collective-permute-start.21 = (bf16[256,1024]{1,0:T(8,128)(2,1)S(1)}, bf16[256,1024]{1,0:T(8,128)(2,1)S(1)}, u32[]{:S(2)}, u32[]{:S(2)}) collective-permute-start(bf16[256,1024]{1,0:T(8,128)(2,1)S(1)} %add_convert_fusion.11.refs_1_), channel_id=1, source_target_pairs={{0,2},{1,3},{2,0},{3,1},{4,6},{5,7},{6,4},{7,5},{8,10},{9,11},{10,... | collective-permute-start | bytes 1572872 | tf_op jit(solution)/shard_map/ppermute | solution.py:721
  167.4 13.7 %collective-permute-start.22 = (bf16[256,1024]{1,0:T(8,128)(2,1)S(1)}, bf16[256,1024]{1,0:T(8,128)(2,1)S(1)}, u32[]{:S(2)}, u32[]{:S(2)}) collective-permute-start(bf16[256,1024]{1,0:T(8,128)(2,1)S(1)} %add_convert_fusion.10.refs_1_), channel_id=1, source_target_pairs={{0,2},{1,3},{2,0},{3,1},{4,6},{5,7},{6,4},{7,5},{8,10},{9,11},{10,... | collective-permute-start | bytes 1572872 | tf_op jit(solution)/shard_map/ppermute | solution.py:721
  170.5 11.9 %collective-permute-start.24 = (bf16[256,1024]{1,0:T(8,128)(2,1)S(1)}, bf16[256,1024]{1,0:T(8,128)(2,1)S(1)}, u32[]{:S(2)}, u32[]{:S(2)}) collective-permute-start(bf16[256,1024]{1,0:T(8,128)(2,1)S(1)} %get-tuple-element.195.xo_ref.refs_0_), channel_id=1, source_target_pairs={{0,1},{1,0},{2,3},{3,2},{4,5},{5,4},{6,7},{7,6},{8,9},{9,8},{10,11... | collective-permute-start | bytes 1572872 | tf_op jit(solution)/shard_map/ppermute | solution.py:721
  195.5 14.3 %collective-permute-start.29 = (bf16[256,1024]{1,0:T(8,128)(2,1)S(1)}, bf16[256,1024]{1,0:T(8,128)(2,1)S(1)}, u32[]{:S(2)}, u32[]{:S(2)}) collective-permute-start(bf16[256,1024]{1,0:T(8,128)(2,1)S(1)} %add_convert_fusion.9.refs_7_.refs_1_), channel_id=1, source_target_pairs={{0,2},{1,3},{2,0},{3,1},{4,6},{5,7},{6,4},{7,5},{8,10},{9,11},{10,... | collective-permute-start | bytes 1572872 | tf_op jit(solution)/shard_map/ppermute | solution.py:721
  212.1 5.8 collective-permute-start.30
  212.1 15.6 %collective-permute-start.33 = (bf16[256,1024]{1,0:T(8,128)(2,1)S(1)}, bf16[256,1024]{1,0:T(8,128)(2,1)}, u32[]{:S(2)}, u32[]{:S(2)}) collective-permute-start(bf16[256,1024]{1,0:T(8,128)(2,1)S(1)} %add_convert_fusion.8.refs_1_), channel_id=1, source_target_pairs={{0,2},{1,3},{2,0},{3,1},{4,6},{5,7},{6,4},{7,5},{8,10},{9,11},{10,... | collective-permute-start | bytes 1572872 | tf_op jit(solution)/shard_map/ppermute | solution.py:721
  230.3 14.2 %collective-permute-start.37 = (bf16[256,1024]{1,0:T(8,128)(2,1)S(1)}, bf16[256,1024]{1,0:T(8,128)(2,1)S(1)}, u32[]{:S(2)}, u32[]{:S(2)}) collective-permute-start(bf16[256,1024]{1,0:T(8,128)(2,1)S(1)} %add_convert_fusion.7.refs_1_), channel_id=1, source_target_pairs={{0,2},{1,3},{2,0},{3,1},{4,6},{5,7},{6,4},{7,5},{8,10},{9,11},{10,... | collective-permute-start | bytes 1572872 | tf_op jit(solution)/shard_map/ppermute | solution.py:721
  244.5 13.4 %collective-permute-start.38 = (bf16[256,1024]{1,0:T(8,128)(2,1)S(1)}, bf16[256,1024]{1,0:T(8,128)(2,1)S(1)}, u32[]{:S(2)}, u32[]{:S(2)}) collective-permute-start(bf16[256,1024]{1,0:T(8,128)(2,1)S(1)} %add_convert_fusion.6.refs_1_), channel_id=1, source_target_pairs={{0,2},{1,3},{2,0},{3,1},{4,6},{5,7},{6,4},{7,5},{8,10},{9,11},{10,... | collective-permute-start | bytes 1572872 | tf_op jit(solution)/shard_map/ppermute | solution.py:721
  281.7 7.6 %collective-permute-start.43 = (bf16[256,1024]{1,0:T(8,128)(2,1)S(1)}, bf16[256,1024]{1,0:T(8,128)(2,1)S(1)}, u32[]{:S(2)}, u32[]{:S(2)}) collective-permute-start(bf16[256,1024]{1,0:T(8,128)(2,1)S(1)} %get-tuple-element.228.refs_0_.refs_6_), channel_id=1, source_target_pairs={{0,1},{1,0},{2,3},{3,2},{4,5},{5,4},{6,7},{7,6},{8,9},{9,8},{10,11... | collective-permute-start | bytes 1572872 | tf_op jit(solution)/shard_map/ppermute | solution.py:721
  287.7 14.2 %collective-permute-start.46 = (bf16[256,1024]{1,0:T(8,128)(2,1)S(1)}, bf16[256,1024]{1,0:T(8,128)(2,1)S(1)}, u32[]{:S(2)}, u32[]{:S(2)}) collective-permute-start(bf16[256,1024]{1,0:T(8,128)(2,1)S(1)} %add_convert_fusion.5.refs_5_.refs_1_), channel_id=1, source_target_pairs={{0,2},{1,3},{2,0},{3,1},{4,6},{5,7},{6,4},{7,5},{8,10},{9,11},{10,... | collective-permute-start | bytes 1572872 | tf_op jit(solution)/shard_map/ppermute | solution.py:721
  312.3 222.8 %reduce-scatter.5.cloned.1.call-start = ((), (), s32[]{:S(2)}) async-start(), calls=%async_computation.5 | async-start | bytes 4718592 | tf_op jit(solution)/shard_map/reduce_scatter | solution.py:981
  312.5 13.6 %collective-permute-start.48 = (bf16[256,1024]{1,0:T(8,128)(2,1)}, bf16[256,1024]{1,0:T(8,128)(2,1)S(1)}, u32[]{:S(2)}, u32[]{:S(2)}) collective-permute-start(bf16[256,1024]{1,0:T(8,128)(2,1)} %copy-done.40), channel_id=1, source_target_pairs={{0,2},{1,3},{2,0},{3,1},{4,6},{5,7},{6,4},{7,5},{8,10},{9,11},{10,... | collective-permute-start | bytes 1572872 | tf_op jit(solution)/shard_map/ppermute | solution.py:721
  319.3 8.6 %collective-permute-start.47 = (bf16[256,1024]{1,0:T(8,128)(2,1)S(1)}, bf16[256,1024]{1,0:T(8,128)(2,1)S(1)}, u32[]{:S(2)}, u32[]{:S(2)}) collective-permute-start(bf16[256,1024]{1,0:T(8,128)(2,1)S(1)} %get-tuple-element.235.d0o.refs_4_), channel_id=1, source_target_pairs={{0,1},{1,0},{2,3},{3,2},{4,5},{5,4},{6,7},{7,6},{8,9},{9,8},{10,11... | collective-permute-start | bytes 1572872 | tf_op jit(solution)/shard_map/ppermute | solution.py:721
  346.7 14.1 %collective-permute-start.54 = (bf16[256,1024]{1,0:T(8,128)(2,1)S(1)}, bf16[256,1024]{1,0:T(8,128)(2,1)S(1)}, u32[]{:S(2)}, u32[]{:S(2)}) collective-permute-start(bf16[256,1024]{1,0:T(8,128)(2,1)S(1)} %add_convert_fusion.3.refs_2_.refs_1_.refs_12_), channel_id=1, source_target_pairs={{0,2},{1,3},{2,0},{3,1},{4,6},{5,7},{6,4},{7,5},{8,10},{9,11},{10,... | collective-permute-start | bytes 1572872 | tf_op jit(solution)/shard_map/ppermute | solution.py:721
  349.7 6.3 %collective-permute-start.52 = (bf16[128,1024]{1,0:T(8,128)(2,1)S(1)}, bf16[128,1024]{1,0:T(8,128)(2,1)S(1)}, u32[]{:S(2)}, u32[]{:S(2)}) collective-permute-start(bf16[128,1024]{1,0:T(8,128)(2,1)S(1)} %get-tuple-element.363), channel_id=1, source_target_pairs={{0,1},{1,0},{2,3},{3,2},{4,5},{5,4},{6,7},{7,6},{8,9},{9,8},{10,11... | collective-permute-start | bytes 786440 | tf_op jit(solution)/shard_map/ppermute | solution.py:721
  349.8 6.2 %collective-permute-start.53 = (bf16[128,1024]{1,0:T(8,128)(2,1)S(1)}, bf16[128,1024]{1,0:T(8,128)(2,1)S(1)}, u32[]{:S(2)}, u32[]{:S(2)}) collective-permute-start(bf16[128,1024]{1,0:T(8,128)(2,1)S(1)} %get-tuple-element.364), channel_id=1, source_target_pairs={{0,1},{1,0},{2,3},{3,2},{4,5},{5,4},{6,7},{7,6},{8,9},{9,8},{10,11... | collective-permute-start | bytes 786440 | tf_op jit(solution)/shard_map/ppermute | solution.py:721
  355.2 22.2 %collective-permute-start.60 = (bf16[2,2,128,512]{3,2,1,0:T(8,128)(2,1)S(1)}, bf16[2,2,128,512]{3,2,1,0:T(8,128)(2,1)S(1)}, u32[]{:S(2)}, u32[]{:S(2)}) collective-permute-start(bf16[2,2,128,512]{3,2,1,0:T(8,128)(2,1)S(1)} %select_bitcast_fusion.4), channel_id=1, source_target_pairs={{0,8},{4,12},{8,0},{12,4},{16,24},{20,28},{24,16},{28,20},{1,9},{5... | collective-permute-start | bytes 1572872 | tf_op jit(solution)/shard_map/ppermute | solution.py:721
  363.5 16.1 %collective-permute-start.59 = (bf16[2,2,128,512]{3,2,0,1:T(8,128)(2,1)S(1)}, bf16[2,2,128,512]{3,2,0,1:T(8,128)(2,1)S(1)}, u32[]{:S(2)}, u32[]{:S(2)}) collective-permute-start(bf16[2,2,128,512]{3,2,0,1:T(8,128)(2,1)S(1)} %select_bitcast_fusion.5), channel_id=1, source_target_pairs={{0,4},{4,0},{8,12},{12,8},{16,20},{20,16},{24,28},{28,24},{1,5},{5... | collective-permute-start | bytes 1572872 | tf_op jit(solution)/shard_map/ppermute | solution.py:721
  364.0 13.4 %collective-permute-start.58 = (bf16[256,1024]{1,0:T(8,128)(2,1)S(1)}, bf16[256,1024]{1,0:T(8,128)(2,1)S(1)}, u32[]{:S(2)}, u32[]{:S(2)}) collective-permute-start(bf16[256,1024]{1,0:T(8,128)(2,1)S(1)} %add_convert_fusion.2.refs_1_), channel_id=1, source_target_pairs={{0,2},{1,3},{2,0},{3,1},{4,6},{5,7},{6,4},{7,5},{8,10},{9,11},{10,... | collective-permute-start | bytes 1572872 | tf_op jit(solution)/shard_map/ppermute | solution.py:721
  382.4 14.3 %collective-permute-start.66 = (bf16[256,1024]{1,0:T(8,128)(2,1)S(1)}, bf16[256,1024]{1,0:T(8,128)(2,1)S(1)}, u32[]{:S(2)}, u32[]{:S(2)}) collective-permute-start(bf16[256,1024]{1,0:T(8,128)(2,1)S(1)} %add_convert_fusion.1.refs_5_.refs_1_), channel_id=1, source_target_pairs={{0,2},{1,3},{2,0},{3,1},{4,6},{5,7},{6,4},{7,5},{8,10},{9,11},{10,... | collective-permute-start | bytes 1572872 | tf_op jit(solution)/shard_map/ppermute | solution.py:721
  406.4 19.4 %collective-permute-start.61 = (bf16[2,128,512]{2,1,0:T(8,128)(2,1)}, bf16[2,128,512]{2,1,0:T(8,128)(2,1)}, u32[]{:S(2)}, u32[]{:S(2)}) collective-permute-start(bf16[2,128,512]{2,1,0:T(8,128)(2,1)} %select_bitcast_fusion.13), channel_id=1, source_target_pairs={{0,8},{4,12},{8,0},{12,4},{16,24},{20,28},{24,16},{28,20},{1,9},{5... | collective-permute-start | bytes 786440 | tf_op jit(solution)/shard_map/ppermute | solution.py:721
  407.5 18.2 %collective-permute-start.62 = (bf16[2,128,512]{2,1,0:T(8,128)(2,1)}, bf16[2,128,512]{2,1,0:T(8,128)(2,1)}, u32[]{:S(2)}, u32[]{:S(2)}) collective-permute-start(bf16[2,128,512]{2,1,0:T(8,128)(2,1)} %select_bitcast_fusion.12), channel_id=1, source_target_pairs={{0,16},{4,20},{8,24},{12,28},{16,0},{20,4},{24,8},{28,12},{1,17},{... | collective-permute-start | bytes 786440 | tf_op jit(solution)/shard_map/ppermute | solution.py:721
  412.6 30.5 %collective-permute-start.70 = (bf16[256,1024]{1,0:T(8,128)(2,1)S(1)}, bf16[256,1024]{1,0:T(8,128)(2,1)S(1)}, u32[]{:S(2)}, u32[]{:S(2)}) collective-permute-start(bf16[256,1024]{1,0:T(8,128)(2,1)S(1)} %add_convert_fusion.refs_1_.refs_12_), channel_id=1, source_target_pairs={{0,2},{1,3},{2,0},{3,1},{4,6},{5,7},{6,4},{7,5},{8,10},{9,11},{10,... | collective-permute-start | bytes 1572872 | tf_op jit(solution)/shard_map/ppermute | solution.py:721
  428.1 7.2 %collective-permute-start.69 = (bf16[128,512]{1,0:T(8,128)(2,1)S(1)}, bf16[128,512]{1,0:T(8,128)(2,1)S(1)}, u32[]{:S(2)}, u32[]{:S(2)}) collective-permute-start(bf16[128,512]{1,0:T(8,128)(2,1)S(1)} %select_bitcast_fusion.20), channel_id=1, source_target_pairs={{0,4},{4,0},{8,12},{12,8},{16,20},{20,16},{24,28},{28,24},{1,5},{5... | collective-permute-start | bytes 393224 | tf_op jit(solution)/shard_map/ppermute | solution.py:721
  429.9 13.1 %collective-permute-start.68 = (bf16[128,512]{1,0:T(8,128)(2,1)S(1)}, bf16[128,512]{1,0:T(8,128)(2,1)S(1)}, u32[]{:S(2)}, u32[]{:S(2)}) collective-permute-start(bf16[128,512]{1,0:T(8,128)(2,1)S(1)} %select_bitcast_fusion.21), channel_id=1, source_target_pairs={{0,16},{4,20},{8,24},{12,28},{16,0},{20,4},{24,8},{28,12},{1,17},{... | collective-permute-start | bytes 393224 | tf_op jit(solution)/shard_map/ppermute | solution.py:721
  435.3 15.4 %collective-permute-start.67 = (bf16[256,1024]{1,0:T(8,128)(2,1)}, bf16[256,1024]{1,0:T(8,128)(2,1)}, u32[]{:S(2)}, u32[]{:S(2)}) collective-permute-start(bf16[256,1024]{1,0:T(8,128)(2,1)} %get-tuple-element.272.d0o.d0), channel_id=1, source_target_pairs={{0,1},{1,0},{2,3},{3,2},{4,5},{5,4},{6,7},{7,6},{8,9},{9,8},{10,11... | collective-permute-start | bytes 1572872 | tf_op jit(solution)/shard_map/ppermute | solution.py:721
  472.6 20.0 %collective-permute-start.73 = (bf16[2,2,128,640]{3,2,1,0:T(8,128)(2,1)}, bf16[2,2,128,640]{3,2,1,0:T(8,128)(2,1)}, u32[]{:S(2)}, u32[]{:S(2)}) collective-permute-start(bf16[2,2,128,640]{3,2,1,0:T(8,128)(2,1)} %select_bitcast_fusion), channel_id=1, source_target_pairs={{0,8},{4,12},{8,0},{12,4},{16,24},{20,28},{24,16},{28,20},{1,9},{5... | collective-permute-start | bytes 1966088 | tf_op jit(solution)/shard_map/ppermute | solution.py:721
  473.7 14.0 %collective-permute-start.80 = (bf16[256,1024]{1,0:T(8,128)(2,1)S(1)}, bf16[256,1024]{1,0:T(8,128)(2,1)S(1)}, u32[]{:S(2)}, u32[]{:S(2)}) collective-permute-start(bf16[256,1024]{1,0:T(8,128)(2,1)S(1)} %select_convert_fusion), channel_id=1, source_target_pairs={{0,2},{1,3},{2,0},{3,1},{4,6},{5,7},{6,4},{7,5},{8,10},{9,11},{10,... | collective-permute-start | bytes 1572872 | tf_op jit(solution)/shard_map/ppermute | solution.py:721
  476.0 21.3 %collective-permute-start.72 = (bf16[2,2,128,640]{3,2,0,1:T(8,128)(2,1)}, bf16[2,2,128,640]{3,2,0,1:T(8,128)(2,1)}, u32[]{:S(2)}, u32[]{:S(2)}) collective-permute-start(bf16[2,2,128,640]{3,2,0,1:T(8,128)(2,1)} %select_bitcast_fusion.1), channel_id=1, source_target_pairs={{0,4},{4,0},{8,12},{12,8},{16,20},{20,16},{24,28},{28,24},{1,5},{5... | collective-permute-start | bytes 1966088 | tf_op jit(solution)/shard_map/ppermute | solution.py:721
  498.7 24.0 %collective-permute-start.76 = (bf16[2,128,640]{2,1,0:T(8,128)(2,1)S(1)}, bf16[2,128,640]{2,1,0:T(8,128)(2,1)S(1)}, u32[]{:S(2)}, u32[]{:S(2)}) collective-permute-start(bf16[2,128,640]{2,1,0:T(8,128)(2,1)S(1)} %select_bitcast_fusion.8), channel_id=1, source_target_pairs={{0,16},{4,20},{8,24},{12,28},{16,0},{20,4},{24,8},{28,12},{1,17},{... | collective-permute-start | bytes 983048 | tf_op jit(solution)/shard_map/ppermute | solution.py:721
  503.4 20.2 %collective-permute-start.74 = (bf16[2,128,640]{2,1,0:T(8,128)(2,1)S(1)}, bf16[2,128,640]{2,1,0:T(8,128)(2,1)S(1)}, u32[]{:S(2)}, u32[]{:S(2)}) collective-permute-start(bf16[2,128,640]{2,1,0:T(8,128)(2,1)S(1)} %select_bitcast_fusion.9), channel_id=1, source_target_pairs={{0,8},{4,12},{8,0},{12,4},{16,24},{20,28},{24,16},{28,20},{1,9},{5... | collective-permute-start | bytes 983048 | tf_op jit(solution)/shard_map/ppermute | solution.py:721
  522.8 5.6 collective-permute-start.77
  523.8 8.4 %collective-permute-start.75 = (bf16[128,640]{1,0:T(8,128)(2,1)S(1)}, bf16[128,640]{1,0:T(8,128)(2,1)S(1)}, u32[]{:S(2)}, u32[]{:S(2)}) collective-permute-start(bf16[128,640]{1,0:T(8,128)(2,1)S(1)} %select_bitcast_fusion.17), channel_id=1, source_target_pairs={{0,16},{4,20},{8,24},{12,28},{16,0},{20,4},{24,8},{28,12},{1,17},{... | collective-permute-start | bytes 491528 | tf_op jit(solution)/shard_map/ppermute | solution.py:721
  550.4 4.5 collective-permute-start.86
  (151 other events, 1014.3 us)
Sparse Core Ops, SparseCore 0:
  12.4 126.0 all-gather.2
  141.2 76.5 all-gather.4
  312.4 91.1 reduce-scatter.2
  407.5 113.3 reduce-scatter.4

commit v2 on v1

--- a/solution.py
+++ b/solution.py
@@ -685,7 +685,9 @@
     grad = jnp.where(pl.program_id(0) == 0, g0_ref[...].astype(f32), g1_ref[...].astype(f32))
     if turned:
         grad = grad.T
-    grad = (grad * k_ref[0]).reshape(w_ref.shape)
+    scale_grad = k_ref[0:1, 1:2]
+    norm = jnp.sqrt(k_ref[0:1, 0:1] + scale_grad * scale_grad + 1e-06)
+    grad = (grad * (clip_limit / jnp.maximum(norm, clip_limit))).reshape(w_ref.shape)
     one = 0.9 * m_ref[...].reshape(w_ref.shape) + 0.1 * grad
     two = 0.95 * v_ref[...].reshape(w_ref.shape) + 0.05 * grad * grad
     w = w_ref[...]
@@ -705,7 +707,7 @@
         functools.partial(adam_kernel, rate, turned),
         (factor, master, moments, moments, *grads),
         [
-            smem(), spec, first, second,
+            whole((8, PAIR)), spec, first, second,
             pl.BlockSpec(grad_block, lambda l, t: (0, at_zero + t)),
             pl.BlockSpec(grad_block, lambda l, t: (0, at_one + t)),
         ],
@@ -891,7 +893,7 @@
                 stream.append(h)
                 low.append(hb)
                 kept[-1][-1].append(zz)
-            sib = swap(low[at], "mp", 1)
+            sib = swap_core(low[at])
             streams += [low[at], sib]
             qkvs.append(qkv_project(low[at], sib, attn_w[layer_at], cosines, sines, at))
         o_a, lse_a, own, send = attend(
@@ -903,11 +905,11 @@
         )
         total_b, came_b, came_a = cross(chip_sum(own, send), came_a)
         h_a, hb_a, z_a = norm_fwd(4 * layer_at, stream[0], total_a, came_a, nrm)
-        sib_a = swap(hb_a, "mp", 1)
+        sib_a = swap_core(hb_a)
         zg_a, own, send = mlp(hb_a, sib_a, mlp_w[layer_at], None)
         next_a, next_came_a, came_b = cross(chip_sum(own, send), came_b)
         h_b, hb_b, z_b = norm_fwd(4 * layer_at, stream[1], total_b, came_b, nrm)
-        sib_b = swap(hb_b, "mp", 1)
+        sib_b = swap_core(hb_b)
         zg_b, own, send = mlp(hb_b, sib_b, mlp_w[layer_at], None)
         next_b, next_came_b, next_came_a = cross(chip_sum(own, send), next_came_a)
         normed = [h_a, h_b]
@@ -956,7 +958,7 @@
         streams, qkvs, attended, norm_a, hiddens, zgs, norm_b = kept[layer_at]
         row = 4 * layer_at + 2
         d_a, db_a, gain_a = norm_bwd(row, grads[0], pending[0], norm_b[0], nrm)
-        sib_a = swap(db_a, "mp", 1)
+        sib_a = swap_core(db_a)
         du_a, own, send = mlp_back(db_a, sib_a, zgs[0], mlp_w[layer_at], None)
         total_a = chip_sum(own, send)
         if pending[1]:
@@ -969,27 +971,22 @@
         else:
             total_a, came_a, _ = cross(total_a)
         d_b, db_b, gain_b = norm_bwd(row, grads[1], pending[1], norm_b[1], nrm)
-        sib_b = swap(db_b, "mp", 1)
+        sib_b = swap_core(db_b)
         du_b, own, send = mlp_back(db_b, sib_b, zgs[1], mlp_w[layer_at], total_a)
         total_b, came_b, came_a = cross(chip_sum(own, send), came_a)
-        if layer_at < LAYERS - 1:
-            came_a = upper.wait_with(came_a)
-            upper.add()
-            upper.send()
         gains = [(gain_a + gain_b)[:2]]
         both = mlp_grads(hiddens, [db_a, sib_a, db_b, sib_b], [du_a, du_b], zgs, total_b)
+        both, came_b = lax.optimization_barrier((both, came_b))
         reduced.append(lax.psum_scatter(both, "dp", scatter_dimension=0, tiled=True))
         row = 4 * layer_at
         grad_a, low_a, gain_a = norm_bwd(row, d_a, (total_a, came_a), norm_a[0], nrm)
-        sib_a = swap(low_a, "mp", 1)
+        sib_a = swap_core(low_a)
         if layer_at < LAYERS - 1:
             came_b = upper.wait_with(came_b)
             upper.add()
-            while upper.left[0]:
-                upper.send()
-                upper.add()
+            upper.send()
         grad_b, low_b, gain_b = norm_bwd(row, d_b, (total_b, came_b), norm_a[1], nrm)
-        dattn = [low_a, sib_a, low_b, swap(low_b, "mp", 1)]
+        dattn = [low_a, sib_a, low_b, swap_core(low_b)]
         dmixes = attend_back(
             core_arr, dattn, attn_w[layer_at], *qkvs, attended[0][0], attended[1][0],
             attended[0][1], attended[1][1], seg_col, seg_row, cosines, sines,
@@ -999,23 +996,30 @@
         grads = [grad_a, grad_b]
         if layer_at > 0:
             total_a, came_a, _ = cross(chip_sum(*qkv_back(dmixes[0], attn_w[layer_at], None)))
+            above = attn_grads(streams, dattn, dmixes, outs, total_a)
+            above, came_a = lax.optimization_barrier((above, came_a))
+            upper = Scatter(above, "dp")
+            upper.send()
             total_b, came_b, came_a = cross(
                 chip_sum(*qkv_back(dmixes[1], attn_w[layer_at], total_a)), came_a
             )
             pending = [(total_a, came_a), (total_b, came_b)]
-            upper = Scatter(attn_grads(streams, dattn, dmixes, outs, total_a), "dp")
-            upper.send()
         else:
             norm_rows = jnp.concatenate(norm_grads, axis=0)
             small = jnp.concatenate([g_emb, jnp.pad(norm_rows.T, ((0, 0), (0, PAIR - 4 * LAYERS)))], axis=1)
             last = attn_grads(streams, dattn, dmixes, outs, None, small.astype(bf16))
             lower = Scatter(last, "dp")
-            fourth = upper.result()
-            squares = jnp.sum(jnp.square(reduced[0].astype(f32))) + jnp.sum(jnp.square(fourth))
+            squares = jnp.sum(jnp.square(reduced[0].astype(f32)))
             while lower.left[0]:
                 lower.send()
                 if len(lower.left[0]) == lower.steps:
-                    squares = lower.wait_with(squares)
+                    squares = upper.wait_with(lower.wait_with(squares))
+                    while upper.left[0]:
+                        upper.add()
+                        if upper.left[0]:
+                            upper.send()
+                    fourth = upper.result()
+                    squares = squares + jnp.sum(jnp.square(fourth))
                 lower.add()
             third = lower.result()
             totals = []
@@ -1046,22 +1050,21 @@
     norm_value = jnp.sqrt(total_squares + scale_grad[0] * scale_grad[0] + 1e-06)
     factor = clip_limit / jnp.maximum(norm_value, clip_limit)
     step_f = jnp.asarray(STEP, f32)
-    factor_arr = factor.reshape(1)
     qkv_step = adam_step(
-        factor_arr, qkv_weight.transpose(0, 2, 1, 3), qkv_moments.transpose(0, 1, 3, 2, 4), (third, fourth),
+        vector, qkv_weight.transpose(0, 2, 1, 3), qkv_moments.transpose(0, 1, 3, 2, 4), (third, fourth),
         3, (1, share, WIDE), lambda t: (t, 0, 0), (share, WIDE), (0, 0), D ** (-0.5),
     )
     qkv_new, qkv_first, qkv_second = [v.transpose(0, 2, 1, 3) for v in qkv_step]
     out_new, out_first, out_second = adam_step(
-        factor_arr, out_weight, out_moments, (third, fourth),
+        vector, out_weight, out_moments, (third, fourth),
         1, (WIDE, share), lambda t: (t, 0), (share, WIDE), (3, 3), (D * SEGS // ROW_LEN) ** (-0.5), True,
     )
     up_new, up_first, up_second = adam_step(
-        factor_arr, up_weight, up_moments, (second, first),
+        vector, up_weight, up_moments, (second, first),
         2, (share, HALF), lambda t: (0, t), (share, HALF), (0, 0), D ** (-0.5),
     )
     down_new, down_first, down_second = adam_step(
-        factor_arr, down_weight, down_moments, (second, first),
+        vector, down_weight, down_moments, (second, first),
         4, (TILE, share), lambda t: (t, 0), (share, TILE), (4, 4), FF ** (-0.5), True,
     )
     norm_new, norm_first, norm_second = adamw_update(norm_params, norm_moments, norm_grad, factor, 0.5, step_f)

time: 592 us -> 592 us (level)
  waiting for transfers between devices: 209 us -> 192 us
  other arithmetic: 45 us -> 53.8 us
  Pallas kernels: 177 us -> 170 us
  local copies, waits for them, and re-layouts: 45.4 us -> 51.4 us
    ppermute x87 -> x103, waiting for transfers between devices: 203 us -> 183 us  [swap(): return lax.ppermute(values, axis, [(i, i ^ bit) for i in range(count)])]
    pallas_call x47, Pallas kernels: 177 us -> 170 us  [call(): pl.pallas_call(body_fn, grid=grid, in_specs=in_specs, out_specs=out_specs...]
    ppermute x87 -> x103, starting transfers between devices: 77.2 us -> 82 us  [swap(): return lax.ppermute(values, axis, [(i, i ^ bit) for i in range(count)])]
    unnamed x222 -> x290, local copies, waits for them, and re-layouts: 34.2 us -> 33 us
  transfers between devices with their start and end apart: 91 -> 107, of which waited for: 59 -> 54; matrix products, arithmetic and copies ran while one was open for 9% -> 11% of each run, Pallas kernels for 24% -> 24%
where the time goes in v2:
time: 592 us; the launch traced here: 581 us
  waiting for transfers between devices  192 us (32%)
  Pallas kernels  170 us (29%)
  starting transfers between devices  82.9 us (14%)
  other arithmetic  53.8 us (9%)
  local copies, waits for them, and re-layouts  51.4 us (9%)
  between operations  30.7 us (5%)
    ppermute x103, waiting for transfers between devices, swap(): return lax.ppermute(values, axis, [(i, i ^ bit) for i in range(count)])  183 us
    pallas_call x47, Pallas kernels, call(): pl.pallas_call(body_fn, grid=grid, in_specs=in_specs, out_specs=out_specs...  170 us
    ppermute x103, starting transfers between devices, swap(): return lax.ppermute(values, axis, [(i, i ^ bit) for i in range(count)])  82 us
    unnamed x290, local copies, waits for them, and re-layouts  33 us
  transfers between devices with their start and end apart: 107, of which 54 were waited for; matrix products, arithmetic and copies ran while one was open for 11% of the time, Pallas kernels for 24%

profile of v2, /device:TPU:0, one launch (start us, length us, event | category | flops | bytes accessed | tf_op | source)
XLA Modules:
  0.0 581.5 jit_solution(6722667142528302165)
XLA Ops:
  13.2 3.0 collective-permute-start.6
  23.4 9.0 %collective-permute-done.3 = bf16[128,640]{0,1:T(8,128)(2,1)S(1)} collective-permute-done((bf16[128,640]{0,1:T(8,128)(2,1)S(1)}, bf16[128,640]{0,1:T(8,128)(2,1)S(1)}, u32[]{:S(2)}, u32[]{:S(2)}) %collective-permute-start.3) | collective-permute-done | bytes 163872 | tf_op jit(solution)/shard_map/ppermute | solution.py:723
  32.5 8.6 %collective-permute-start.4 = (bf16[2,128,640]{1,2,0:T(8,128)(2,1)S(1)}, bf16[2,128,640]{1,2,0:T(8,128)(2,1)S(1)}, u32[]{:S(2)}, u32[]{:S(2)}) collective-permute-start(bf16[2,128,640]{1,2,0:T(8,128)(2,1)S(1)} %pad_maximum_fusion.7), channel_id=1, source_target_pairs={{0,8},{4,12},{8,0},{12,4},{16,24},{20,28},{24,16},{28,20},{1,9},{5... | collective-permute-start | bytes 983048 | tf_op jit(solution)/shard_map/ppermute | solution.py:723
  41.1 11.0 %collective-permute-done.7 = bf16[2,128,512]{1,2,0:T(8,128)(2,1)S(1)} collective-permute-done((bf16[2,128,512]{1,2,0:T(8,128)(2,1)S(1)}, bf16[2,128,512]{1,2,0:T(8,128)(2,1)S(1)}, u32[]{:S(2)}, u32[]{:S(2)}) %collective-permute-start.7) | collective-permute-done | bytes 262176 | tf_op jit(solution)/shard_map/ppermute | solution.py:723
  52.2 4.4 collective-permute-start.8
  58.9 8.7 %collective-permute-done.4 = bf16[2,128,640]{1,2,0:T(8,128)(2,1)S(1)} collective-permute-done((bf16[2,128,640]{1,2,0:T(8,128)(2,1)S(1)}, bf16[2,128,640]{1,2,0:T(8,128)(2,1)S(1)}, u32[]{:S(2)}, u32[]{:S(2)}) %collective-permute-start.4) | collective-permute-done | bytes 327712 | tf_op jit(solution)/shard_map/ppermute | solution.py:723
  71.7 15.8 %collective-permute-done.8 = bf16[2,2,128,512]{2,3,1,0:T(8,128)(2,1)S(1)} collective-permute-done((bf16[2,2,128,512]{2,3,1,0:T(8,128)(2,1)S(1)}, bf16[2,2,128,512]{2,3,1,0:T(8,128)(2,1)S(1)}, u32[]{:S(2)}, u32[]{:S(2)}) %collective-permute-start.8) | collective-permute-done | bytes 524320 | tf_op jit(solution)/shard_map/ppermute | solution.py:723
  89.0 8.1 %collective-permute-done.5 = bf16[2,2,128,640]{2,3,1,0:T(8,128)(2,1)} collective-permute-done((bf16[2,2,128,640]{2,3,1,0:T(8,128)(2,1)}, bf16[2,2,128,640]{2,3,1,0:T(8,128)(2,1)}, u32[]{:S(2)}, u32[]{:S(2)}) %collective-permute-start.5) | collective-permute-done | bytes 655392 | tf_op jit(solution)/shard_map/ppermute | solution.py:723
  106.2 5.8 shard_map.362
  119.7 5.7 shard_map.363
  137.2 2.9 all-gather.3.cloned.1.call-done.up_ref.down_ref.w_ref.refs_6_.refs_1_.refs_3_.refs_4_
  140.1 2.8 copy-done
  142.9 4.3 shard_map.365
  154.2 4.5 shard_map.367
  161.0 5.5 collective-permute-done.25.refs_2_
  170.0 9.7 %collective-permute-done.26.refs_2_ = bf16[256,1024]{1,0:T(8,128)(2,1)S(1)} collective-permute-done((bf16[256,1024]{1,0:T(8,128)(2,1)S(1)}, bf16[256,1024]{1,0:T(8,128)(2,1)S(1)}, u32[]{:S(2)}, u32[]{:S(2)}) %collective-permute-start.26) | collective-permute-done | bytes 524320 | tf_op jit(solution)/shard_map/ppermute | solution.py:723
  187.3 5.7 shard_map.372
  196.9 5.8 shard_map.373
  205.2 4.1 collective-permute-done.35.refs_2_
  212.9 6.0 %all-gather.5.cloned.1.call-done.up_ref.down_ref.refs_3_.refs_4_ = bf16[1024,2176]{1,0:T(8,128)(2,1)} async-done(((bf16[128,2176]{1,0:T(8,128)(2,1)}), bf16[1024,2176]{1,0:T(8,128)(2,1)}) %all-gather.5.cloned.1.call-update) | async-done | bytes 4456464 | tf_op jit(solution)/shard_map/all_gather | solution.py:846
  221.2 4.6 shard_map.375
  232.6 4.5 shard_map.377
  239.4 5.7 collective-permute-done.45.refs_2_
  249.8 8.4 %collective-permute-done.46.refs_2_ = bf16[256,1024]{1,0:T(8,128)(2,1)S(1)} collective-permute-done((bf16[256,1024]{1,0:T(8,128)(2,1)S(1)}, bf16[256,1024]{1,0:T(8,128)(2,1)S(1)}, u32[]{:S(2)}, u32[]{:S(2)}) %collective-permute-start.46) | collective-permute-done | bytes 524320 | tf_op jit(solution)/shard_map/ppermute | solution.py:723
  262.4 14.4 %shard_map.380 = (f32[256,1024]{1,0:T(8,128)S(1)}, f32[256,1024]{1,0:T(8,128)S(1)}, f32[1024,128]{1,0:T(8,128)S(1)}, f32[8,128]{1,0:T(8,128)S(1)}) custom-call(f32[1]{0:T(128)S(6)} %copy.261.ls_ref, bf16[1024,128]{1,0:T(8,128)(2,1)S(1)} %pad_maximum_fusion.9.e_ref, f32[1024,128]{1,0:T(8,128)S(1)} %broadcast_in_dim.92.seg_ref, ...), custom_call_target="tpu_custom_call" | custom-call | flops 2684354560 | bytes 4763652 | tf_op jit(solution)/shard_map/pallas_call | solution.py:74
  281.7 3.6 shard_map.382
  289.1 3.6 shard_map.384
  295.7 5.9 %collective-permute-done.56.refs_2_ = bf16[256,1024]{1,0:T(8,128)(2,1)S(1)} collective-permute-done((bf16[256,1024]{1,0:T(8,128)(2,1)S(1)}, bf16[256,1024]{1,0:T(8,128)(2,1)S(1)}, u32[]{:S(2)}, u32[]{:S(2)}) %collective-permute-start.56) | collective-permute-done | bytes 524320 | tf_op jit(solution)/shard_map/ppermute | solution.py:723
  307.4 7.8 %shard_map.386 = bf16[1024,2048]{1,0:T(8,128)(2,1)} custom-call(bf16[256,1024]{1,0:T(8,128)(2,1)S(1)} %get-tuple-element.209.ho_ref.refs_0_, bf16[256,1024]{1,0:T(8,128)(2,1)S(1)} %copy-done.63, bf16[256,1024]{1,0:T(8,128)(2,1)S(1)} %get-tuple-element.214.ho_ref.refs_2_, bf16[256,1024]{1,0:T(8,128)(2,1)S(1)} %constant_dynamic-update-slice_fusion.14.hs_ref.refs_3_, ...), custom_call_target="tpu_custom_call" | custom-call | flops 4294967296 | bytes 14680064 | tf_op jit(solution)/shard_map/pallas_call | solution.py:74
  324.9 10.7 %shard_map.388 = (bf16[512,768]{1,0:T(8,128)(2,1)S(1)}, bf16[512,768]{1,0:T(8,128)(2,1)S(1)}) custom-call(s32[1]{0:T(128)} %bitcast.core_ref.refs_0_, bf16[256,1024]{1,0:T(8,128)(2,1)S(1)} %copy-done.49, bf16[256,1024]{1,0:T(8,128)(2,1)S(1)} %constant_dynamic-update-slice_fusion.20.d0s.refs_5_, bf16[256,1024]{1,0:T(8,128)(2,1)S(1)} %get-tuple-element.248.d1o.refs_6_, ...), custom_call_target="tpu_custom_call" | custom-call | flops 3892314112 | bytes 7405572 | tf_op jit(solution)/shard_map/pallas_call | solution.py:74
  342.1 4.6 shard_map.391
  347.8 5.2 collective-permute-done.66.refs_2_
  360.3 3.8 shard_map.393
  371.8 6.8 %collective-permute-done.72 = bf16[2,2,128,512]{3,2,0,1:T(8,128)(2,1)} collective-permute-done((bf16[2,2,128,512]{3,2,0,1:T(8,128)(2,1)}, bf16[2,2,128,512]{3,2,0,1:T(8,128)(2,1)}, u32[]{:S(2)}, u32[]{:S(2)}) %collective-permute-start.72) | collective-permute-done | bytes 524320 | tf_op jit(solution)/shard_map/ppermute | solution.py:723
  385.8 3.1 copy-done.3
  389.0 3.7 shard_map.395
  402.3 8.1 %shard_map.397 = bf16[1024,2048]{1,0:T(8,128)(2,1)} custom-call(bf16[256,1024]{1,0:T(8,128)(2,1)S(1)} %copy-done.59, bf16[256,1024]{1,0:T(8,128)(2,1)S(1)} %copy-done.70, bf16[256,1024]{1,0:T(8,128)(2,1)S(1)} %copy-done.61, bf16[256,1024]{1,0:T(8,128)(2,1)S(1)} %copy-done.72, bf16[256,1024]{1,0:T(8,128)(2,1)S(1)} %copy-done.47, ...), custom_call_target="tpu_custom_call" | custom-call | flops 4294967296 | bytes 14680064 | tf_op jit(solution)/shard_map/pallas_call | solution.py:74
  413.5 4.5 collective-permute-done.82
  433.9 10.7 %shard_map.399 = (bf16[512,768]{1,0:T(8,128)(2,1)S(1)}, bf16[512,768]{1,0:T(8,128)(2,1)S(1)}) custom-call(s32[1]{0:T(128)} %bitcast.core_ref.refs_0_, bf16[256,1024]{1,0:T(8,128)(2,1)S(1)} %copy-done.51, bf16[256,1024]{1,0:T(8,128)(2,1)S(1)} %copy-done.67, bf16[256,1024]{1,0:T(8,128)(2,1)S(1)} %copy-done.53, ...), custom_call_target="tpu_custom_call" | custom-call | flops 3892314112 | bytes 9764868 | tf_op jit(solution)/shard_map/pallas_call | solution.py:74
  444.7 4.9 shard_map.400.refs_2_
  459.6 8.9 %collective-permute-done.94 = bf16[256,1024]{1,0:T(8,128)(2,1)S(1)} collective-permute-done((bf16[256,1024]{1,0:T(8,128)(2,1)S(1)}, bf16[256,1024]{1,0:T(8,128)(2,1)S(1)}, u32[]{:S(2)}, u32[]{:S(2)}) %collective-permute-start.94) | collective-permute-done | bytes 524320 | tf_op jit(solution)/shard_map/ppermute | solution.py:723
  472.0 9.0 %collective-permute-done.87 = bf16[2,2,128,640]{3,2,1,0:T(8,128)(2,1)} collective-permute-done((bf16[2,2,128,640]{3,2,1,0:T(8,128)(2,1)S(1)}, bf16[2,2,128,640]{3,2,1,0:T(8,128)(2,1)}, u32[]{:S(2)}, u32[]{:S(2)}) %collective-permute-start.87) | collective-permute-done | bytes 655392 | tf_op jit(solution)/shard_map/ppermute | solution.py:723
  490.6 10.4 %collective-permute-done.90 = bf16[2,128,640]{2,1,0:T(8,128)(2,1)} collective-permute-done((bf16[2,128,640]{2,1,0:T(8,128)(2,1)}, bf16[2,128,640]{2,1,0:T(8,128)(2,1)}, u32[]{:S(2)}, u32[]{:S(2)}) %collective-permute-start.90) | collective-permute-done | bytes 327712 | tf_op jit(solution)/shard_map/ppermute | solution.py:723
  503.8 6.1 %collective-permute-start.89 = (bf16[128,640]{1,0:T(8,128)(2,1)S(1)}, bf16[128,640]{1,0:T(8,128)(2,1)S(1)}, u32[]{:S(2)}, u32[]{:S(2)}) collective-permute-start(bf16[128,640]{1,0:T(8,128)(2,1)S(1)} %select_bitcast_fusion.17), channel_id=1, source_target_pairs={{0,16},{4,20},{8,24},{12,28},{16,0},{20,4},{24,8},{28,12},{1,17},{... | collective-permute-start | bytes 491528 | tf_op jit(solution)/shard_map/ppermute | solution.py:723
  510.3 14.4 %collective-permute-done.89 = bf16[128,640]{1,0:T(8,128)(2,1)S(1)} collective-permute-done((bf16[128,640]{1,0:T(8,128)(2,1)S(1)}, bf16[128,640]{1,0:T(8,128)(2,1)S(1)}, u32[]{:S(2)}, u32[]{:S(2)}) %collective-permute-start.89) | collective-permute-done | bytes 163872 | tf_op jit(solution)/shard_map/ppermute | solution.py:723
  559.4 3.2 shard_map.403
  562.7 4.1 shard_map.406
  566.8 3.2 shard_map.405
  (686 shorter events, 235.2 us)
Async XLA Ops:
  7.2 132.9 %all-gather.3.cloned.1.call-start = ((), (), s32[]{:S(2)}) async-start(), calls=%async_computation.2 | async-start | bytes 7077888 | tf_op jit(solution)/shard_map/all_gather | solution.py:846
  13.0 205.9 %all-gather.5.cloned.1.call-start = ((), (), s32[]{:S(2)}) async-start(), calls=%async_computation.3 | async-start | bytes 5013504 | tf_op jit(solution)/shard_map/all_gather | solution.py:846
  13.2 9.7 %collective-permute-start.6 = (bf16[128,512]{0,1:T(8,128)(2,1)S(1)}, bf16[128,512]{0,1:T(8,128)(2,1)S(1)}, u32[]{:S(2)}, u32[]{:S(2)}) collective-permute-start(bf16[128,512]{0,1:T(8,128)(2,1)S(1)} %fusion.12), channel_id=1, source_target_pairs={{0,4},{4,0},{8,12},{12,8},{16,20},{20,16},{24,28},{28,24},{1,5},{5... | collective-permute-start | bytes 393224 | tf_op jit(solution)/shard_map/ppermute | solution.py:723
  16.2 16.1 %collective-permute-start.3 = (bf16[128,640]{0,1:T(8,128)(2,1)S(1)}, bf16[128,640]{0,1:T(8,128)(2,1)S(1)}, u32[]{:S(2)}, u32[]{:S(2)}) collective-permute-start(bf16[128,640]{0,1:T(8,128)(2,1)S(1)} %slice.253), channel_id=1, source_target_pairs={{0,16},{4,20},{8,24},{12,28},{16,0},{20,4},{24,8},{28,12},{1,17},{... | collective-permute-start | bytes 491528 | tf_op jit(solution)/shard_map/ppermute | solution.py:723
  18.9 37.7 %collective-permute-start = (bf16[256,1024]{1,0:T(8,128)(2,1)S(1)}, bf16[256,1024]{1,0:T(8,128)(2,1)S(1)}, u32[]{:S(2)}, u32[]{:S(2)}) collective-permute-start(bf16[256,1024]{1,0:T(8,128)(2,1)S(1)} %copy-done.125), channel_id=1, source_target_pairs={{0,2},{1,3},{2,0},{3,1},{4,6},{5,7},{6,4},{7,5},{8,10},{9,11},{10,... | collective-permute-start | bytes 1572872 | tf_op jit(solution)/shard_map/ppermute | solution.py:723
  23.0 29.1 %collective-permute-start.7 = (bf16[2,128,512]{1,2,0:T(8,128)(2,1)S(1)}, bf16[2,128,512]{1,2,0:T(8,128)(2,1)S(1)}, u32[]{:S(2)}, u32[]{:S(2)}) collective-permute-start(bf16[2,128,512]{1,2,0:T(8,128)(2,1)S(1)} %pad_maximum_fusion.8), channel_id=1, source_target_pairs={{0,16},{4,20},{8,24},{12,28},{16,0},{20,4},{24,8},{28,12},{1,17},{... | collective-permute-start | bytes 786440 | tf_op jit(solution)/shard_map/ppermute | solution.py:723
  32.5 35.1 %collective-permute-start.4 = (bf16[2,128,640]{1,2,0:T(8,128)(2,1)S(1)}, bf16[2,128,640]{1,2,0:T(8,128)(2,1)S(1)}, u32[]{:S(2)}, u32[]{:S(2)}) collective-permute-start(bf16[2,128,640]{1,2,0:T(8,128)(2,1)S(1)} %pad_maximum_fusion.7), channel_id=1, source_target_pairs={{0,8},{4,12},{8,0},{12,4},{16,24},{20,28},{24,16},{28,20},{1,9},{5... | collective-permute-start | bytes 983048 | tf_op jit(solution)/shard_map/ppermute | solution.py:723
  52.2 35.3 %collective-permute-start.8 = (bf16[2,2,128,512]{2,3,1,0:T(8,128)(2,1)S(1)}, bf16[2,2,128,512]{2,3,1,0:T(8,128)(2,1)S(1)}, u32[]{:S(2)}, u32[]{:S(2)}) collective-permute-start(bf16[2,2,128,512]{2,3,1,0:T(8,128)(2,1)S(1)} %pad_maximum_fusion.5), channel_id=1, source_target_pairs={{0,8},{4,12},{8,0},{12,4},{16,24},{20,28},{24,16},{28,20},{1,9},{5... | collective-permute-start | bytes 1572872 | tf_op jit(solution)/shard_map/ppermute | solution.py:723
  58.2 11.1 %collective-permute-start.9 = (bf16[128,1024]{1,0:T(8,128)(2,1)S(1)}, bf16[128,1024]{1,0:T(8,128)(2,1)S(1)}, u32[]{:S(2)}, u32[]{:S(2)}) collective-permute-start(bf16[128,1024]{1,0:T(8,128)(2,1)S(1)} %get-tuple-element.432), channel_id=1, source_target_pairs={{0,1},{1,0},{2,3},{3,2},{4,5},{5,4},{6,7},{7,6},{8,9},{9,8},{10,11... | collective-permute-start | bytes 786440 | tf_op jit(solution)/shard_map/ppermute | solution.py:723
  58.3 11.2 %collective-permute-start.1 = (bf16[128,1024]{1,0:T(8,128)(2,1)S(1)}, bf16[128,1024]{1,0:T(8,128)(2,1)S(1)}, u32[]{:S(2)}, u32[]{:S(2)}) collective-permute-start(bf16[128,1024]{1,0:T(8,128)(2,1)S(1)} %get-tuple-element.436), channel_id=1, source_target_pairs={{0,1},{1,0},{2,3},{3,2},{4,5},{5,4},{6,7},{7,6},{8,9},{9,8},{10,11... | collective-permute-start | bytes 786440 | tf_op jit(solution)/shard_map/ppermute | solution.py:723
  68.6 28.5 %collective-permute-start.5 = (bf16[2,2,128,640]{2,3,1,0:T(8,128)(2,1)}, bf16[2,2,128,640]{2,3,1,0:T(8,128)(2,1)}, u32[]{:S(2)}, u32[]{:S(2)}) collective-permute-start(bf16[2,2,128,640]{2,3,1,0:T(8,128)(2,1)} %pad_maximum_fusion.2), channel_id=1, source_target_pairs={{0,4},{4,0},{8,12},{12,8},{16,20},{20,16},{24,28},{28,24},{1,5},{5... | collective-permute-start | bytes 1966088 | tf_op jit(solution)/shard_map/ppermute | solution.py:723
  115.0 355.1 %reduce-scatter.3.cloned.1.call-start = ((), (), s32[]{:S(2)}) async-start(), calls=%async_computation.4 | async-start | bytes 4718592 | tf_op jit(solution)/shard_map/reduce_scatter | solution.py:980
  118.0 14.3 %collective-permute-start.15 = (bf16[256,1024]{1,0:T(8,128)(2,1)}, bf16[256,1024]{1,0:T(8,128)(2,1)}, u32[]{:S(2)}, u32[]{:S(2)}) collective-permute-start(bf16[256,1024]{1,0:T(8,128)(2,1)} %add_convert_fusion.13.refs_7_.refs_1_), channel_id=1, source_target_pairs={{0,2},{1,3},{2,0},{3,1},{4,6},{5,7},{6,4},{7,5},{8,10},{9,11},{10,... | collective-permute-start | bytes 1572872 | tf_op jit(solution)/shard_map/ppermute | solution.py:723
  135.4 14.0 %collective-permute-start.20 = (bf16[256,1024]{1,0:T(8,128)(2,1)S(1)}, bf16[256,1024]{1,0:T(8,128)(2,1)}, u32[]{:S(2)}, u32[]{:S(2)}) collective-permute-start(bf16[256,1024]{1,0:T(8,128)(2,1)S(1)} %add_convert_fusion.12.refs_1_), channel_id=1, source_target_pairs={{0,2},{1,3},{2,0},{3,1},{4,6},{5,7},{6,4},{7,5},{8,10},{9,11},{10,... | collective-permute-start | bytes 1572872 | tf_op jit(solution)/shard_map/ppermute | solution.py:723
  152.5 14.0 %collective-permute-start.25 = (bf16[256,1024]{1,0:T(8,128)(2,1)S(1)}, bf16[256,1024]{1,0:T(8,128)(2,1)S(1)}, u32[]{:S(2)}, u32[]{:S(2)}) collective-permute-start(bf16[256,1024]{1,0:T(8,128)(2,1)S(1)} %add_convert_fusion.11.refs_1_), channel_id=1, source_target_pairs={{0,2},{1,3},{2,0},{3,1},{4,6},{5,7},{6,4},{7,5},{8,10},{9,11},{10,... | collective-permute-start | bytes 1572872 | tf_op jit(solution)/shard_map/ppermute | solution.py:723
  166.4 13.2 %collective-permute-start.26 = (bf16[256,1024]{1,0:T(8,128)(2,1)S(1)}, bf16[256,1024]{1,0:T(8,128)(2,1)S(1)}, u32[]{:S(2)}, u32[]{:S(2)}) collective-permute-start(bf16[256,1024]{1,0:T(8,128)(2,1)S(1)} %add_convert_fusion.10.refs_1_), channel_id=1, source_target_pairs={{0,2},{1,3},{2,0},{3,1},{4,6},{5,7},{6,4},{7,5},{8,10},{9,11},{10,... | collective-permute-start | bytes 1572872 | tf_op jit(solution)/shard_map/ppermute | solution.py:723
  169.4 11.7 %collective-permute-start.29 = (bf16[128,1024]{1,0:T(8,128)(2,1)S(1)}, bf16[128,1024]{1,0:T(8,128)(2,1)S(1)}, u32[]{:S(2)}, u32[]{:S(2)}) collective-permute-start(bf16[128,1024]{1,0:T(8,128)(2,1)S(1)} %get-tuple-element.416), channel_id=1, source_target_pairs={{0,1},{1,0},{2,3},{3,2},{4,5},{5,4},{6,7},{7,6},{8,9},{9,8},{10,11... | collective-permute-start | bytes 786440 | tf_op jit(solution)/shard_map/ppermute | solution.py:723
  169.5 12.2 %collective-permute-start.30 = (bf16[128,1024]{1,0:T(8,128)(2,1)S(1)}, bf16[128,1024]{1,0:T(8,128)(2,1)S(1)}, u32[]{:S(2)}, u32[]{:S(2)}) collective-permute-start(bf16[128,1024]{1,0:T(8,128)(2,1)S(1)} %get-tuple-element.415), channel_id=1, source_target_pairs={{0,1},{1,0},{2,3},{3,2},{4,5},{5,4},{6,7},{7,6},{8,9},{9,8},{10,11... | collective-permute-start | bytes 786440 | tf_op jit(solution)/shard_map/ppermute | solution.py:723
  195.3 14.0 %collective-permute-start.35 = (bf16[256,1024]{1,0:T(8,128)(2,1)S(1)}, bf16[256,1024]{1,0:T(8,128)(2,1)S(1)}, u32[]{:S(2)}, u32[]{:S(2)}) collective-permute-start(bf16[256,1024]{1,0:T(8,128)(2,1)S(1)} %add_convert_fusion.9.refs_7_.refs_1_), channel_id=1, source_target_pairs={{0,2},{1,3},{2,0},{3,1},{4,6},{5,7},{6,4},{7,5},{8,10},{9,11},{10,... | collective-permute-start | bytes 1572872 | tf_op jit(solution)/shard_map/ppermute | solution.py:723
  211.3 16.7 %collective-permute-start.40 = (bf16[256,1024]{1,0:T(8,128)(2,1)S(1)}, bf16[256,1024]{1,0:T(8,128)(2,1)}, u32[]{:S(2)}, u32[]{:S(2)}) collective-permute-start(bf16[256,1024]{1,0:T(8,128)(2,1)S(1)} %add_convert_fusion.8.refs_1_), channel_id=1, source_target_pairs={{0,2},{1,3},{2,0},{3,1},{4,6},{5,7},{6,4},{7,5},{8,10},{9,11},{10,... | collective-permute-start | bytes 1572872 | tf_op jit(solution)/shard_map/ppermute | solution.py:723
  231.1 14.0 %collective-permute-start.45 = (bf16[256,1024]{1,0:T(8,128)(2,1)S(1)}, bf16[256,1024]{1,0:T(8,128)(2,1)S(1)}, u32[]{:S(2)}, u32[]{:S(2)}) collective-permute-start(bf16[256,1024]{1,0:T(8,128)(2,1)S(1)} %add_convert_fusion.7.refs_1_), channel_id=1, source_target_pairs={{0,2},{1,3},{2,0},{3,1},{4,6},{5,7},{6,4},{7,5},{8,10},{9,11},{10,... | collective-permute-start | bytes 1572872 | tf_op jit(solution)/shard_map/ppermute | solution.py:723
  245.0 13.1 %collective-permute-start.46 = (bf16[256,1024]{1,0:T(8,128)(2,1)S(1)}, bf16[256,1024]{1,0:T(8,128)(2,1)S(1)}, u32[]{:S(2)}, u32[]{:S(2)}) collective-permute-start(bf16[256,1024]{1,0:T(8,128)(2,1)S(1)} %add_convert_fusion.6.refs_1_), channel_id=1, source_target_pairs={{0,2},{1,3},{2,0},{3,1},{4,6},{5,7},{6,4},{7,5},{8,10},{9,11},{10,... | collective-permute-start | bytes 1572872 | tf_op jit(solution)/shard_map/ppermute | solution.py:723
  287.6 14.0 %collective-permute-start.56 = (bf16[256,1024]{1,0:T(8,128)(2,1)S(1)}, bf16[256,1024]{1,0:T(8,128)(2,1)S(1)}, u32[]{:S(2)}, u32[]{:S(2)}) collective-permute-start(bf16[256,1024]{1,0:T(8,128)(2,1)S(1)} %add_convert_fusion.5.refs_5_.refs_1_), channel_id=1, source_target_pairs={{0,2},{1,3},{2,0},{3,1},{4,6},{5,7},{6,4},{7,5},{8,10},{9,11},{10,... | collective-permute-start | bytes 1572872 | tf_op jit(solution)/shard_map/ppermute | solution.py:723
  301.6 13.6 %collective-permute-start.59 = (bf16[256,1024]{1,0:T(8,128)(2,1)}, bf16[256,1024]{1,0:T(8,128)(2,1)}, u32[]{:S(2)}, u32[]{:S(2)}) collective-permute-start(bf16[256,1024]{1,0:T(8,128)(2,1)} %add_convert_fusion.4.refs_12_.refs_1_), channel_id=1, source_target_pairs={{0,2},{1,3},{2,0},{3,1},{4,6},{5,7},{6,4},{7,5},{8,10},{9,11},{10,... | collective-permute-start | bytes 1572872 | tf_op jit(solution)/shard_map/ppermute | solution.py:723
  306.9 14.1 %collective-permute-start.58 = (bf16[128,1024]{1,0:T(8,128)(2,1)}, bf16[128,1024]{1,0:T(8,128)(2,1)}, u32[]{:S(2)}, u32[]{:S(2)}) collective-permute-start(bf16[128,1024]{1,0:T(8,128)(2,1)} %get-tuple-element.389), channel_id=1, source_target_pairs={{0,1},{1,0},{2,3},{3,2},{4,5},{5,4},{6,7},{7,6},{8,9},{9,8},{10,11... | collective-permute-start | bytes 786440 | tf_op jit(solution)/shard_map/ppermute | solution.py:723
  306.9 12.9 %collective-permute-start.57 = (bf16[128,1024]{1,0:T(8,128)(2,1)}, bf16[128,1024]{1,0:T(8,128)(2,1)}, u32[]{:S(2)}, u32[]{:S(2)}) collective-permute-start(bf16[128,1024]{1,0:T(8,128)(2,1)} %get-tuple-element.390), channel_id=1, source_target_pairs={{0,1},{1,0},{2,3},{3,2},{4,5},{5,4},{6,7},{7,6},{8,9},{9,8},{10,11... | collective-permute-start | bytes 786440 | tf_op jit(solution)/shard_map/ppermute | solution.py:723
  315.3 213.0 %reduce-scatter.5.cloned.1.call-start = ((), (), s32[]{:S(2)}) async-start(), calls=%async_computation.5 | async-start | bytes 4718592 | tf_op jit(solution)/shard_map/reduce_scatter | solution.py:980
  339.0 14.0 %collective-permute-start.66 = (bf16[256,1024]{1,0:T(8,128)(2,1)S(1)}, bf16[256,1024]{1,0:T(8,128)(2,1)S(1)}, u32[]{:S(2)}, u32[]{:S(2)}) collective-permute-start(bf16[256,1024]{1,0:T(8,128)(2,1)S(1)} %add_convert_fusion.3.refs_2_.refs_12_.refs_1_), channel_id=1, source_target_pairs={{0,2},{1,3},{2,0},{3,1},{4,6},{5,7},{6,4},{7,5},{8,10},{9,11},{10,... | collective-permute-start | bytes 1572872 | tf_op jit(solution)/shard_map/ppermute | solution.py:723
  341.2 5.5 collective-permute-start.64
  355.4 15.6 %collective-permute-start.71 = (bf16[256,1024]{1,0:T(8,128)(2,1)}, bf16[256,1024]{1,0:T(8,128)(2,1)}, u32[]{:S(2)}, u32[]{:S(2)}) collective-permute-start(bf16[256,1024]{1,0:T(8,128)(2,1)} %add_convert_fusion.2.refs_1_), channel_id=1, source_target_pairs={{0,2},{1,3},{2,0},{3,1},{4,6},{5,7},{6,4},{7,5},{8,10},{9,11},{10,... | collective-permute-start | bytes 1572872 | tf_op jit(solution)/shard_map/ppermute | solution.py:723
  357.6 14.2 %collective-permute-start.73 = (bf16[2,2,128,512]{3,2,1,0:T(8,128)(2,1)}, bf16[2,2,128,512]{3,2,1,0:T(8,128)(2,1)}, u32[]{:S(2)}, u32[]{:S(2)}) collective-permute-start(bf16[2,2,128,512]{3,2,1,0:T(8,128)(2,1)} %select_bitcast_fusion.4), channel_id=1, source_target_pairs={{0,8},{4,12},{8,0},{12,4},{16,24},{20,28},{24,16},{28,20},{1,9},{5... | collective-permute-start | bytes 1572872 | tf_op jit(solution)/shard_map/ppermute | solution.py:723
  359.4 19.3 %collective-permute-start.72 = (bf16[2,2,128,512]{3,2,0,1:T(8,128)(2,1)}, bf16[2,2,128,512]{3,2,0,1:T(8,128)(2,1)}, u32[]{:S(2)}, u32[]{:S(2)}) collective-permute-start(bf16[2,2,128,512]{3,2,0,1:T(8,128)(2,1)} %select_bitcast_fusion.5), channel_id=1, source_target_pairs={{0,4},{4,0},{8,12},{12,8},{16,20},{20,16},{24,28},{28,24},{1,5},{5... | collective-permute-start | bytes 1572872 | tf_op jit(solution)/shard_map/ppermute | solution.py:723
  371.1 26.1 %collective-permute-start.78 = (bf16[256,1024]{1,0:T(8,128)(2,1)S(1)}, bf16[256,1024]{1,0:T(8,128)(2,1)S(1)}, u32[]{:S(2)}, u32[]{:S(2)}) collective-permute-start(bf16[256,1024]{1,0:T(8,128)(2,1)S(1)} %add_convert_fusion.1.refs_5_.refs_1_), channel_id=1, source_target_pairs={{0,2},{1,3},{2,0},{3,1},{4,6},{5,7},{6,4},{7,5},{8,10},{9,11},{10,... | collective-permute-start | bytes 1572872 | tf_op jit(solution)/shard_map/ppermute | solution.py:723
  394.1 23.9 %collective-permute-start.82 = (bf16[2,128,512]{2,1,0:T(8,128)(2,1)}, bf16[2,128,512]{2,1,0:T(8,128)(2,1)}, u32[]{:S(2)}, u32[]{:S(2)}) collective-permute-start(bf16[2,128,512]{2,1,0:T(8,128)(2,1)} %select_bitcast_fusion.12), channel_id=1, source_target_pairs={{0,16},{4,20},{8,24},{12,28},{16,0},{20,4},{24,8},{28,12},{1,17},{... | collective-permute-start | bytes 786440 | tf_op jit(solution)/shard_map/ppermute | solution.py:723
  395.8 22.2 %collective-permute-start.81 = (bf16[2,128,512]{2,1,0:T(8,128)(2,1)}, bf16[2,128,512]{2,1,0:T(8,128)(2,1)}, u32[]{:S(2)}, u32[]{:S(2)}) collective-permute-start(bf16[2,128,512]{2,1,0:T(8,128)(2,1)} %select_bitcast_fusion.13), channel_id=1, source_target_pairs={{0,8},{4,12},{8,0},{12,4},{16,24},{20,28},{24,16},{28,20},{1,9},{5... | collective-permute-start | bytes 786440 | tf_op jit(solution)/shard_map/ppermute | solution.py:723
  397.1 13.4 %collective-permute-start.83 = (bf16[256,1024]{1,0:T(8,128)(2,1)S(1)}, bf16[256,1024]{1,0:T(8,128)(2,1)S(1)}, u32[]{:S(2)}, u32[]{:S(2)}) collective-permute-start(bf16[256,1024]{1,0:T(8,128)(2,1)S(1)} %add_convert_fusion.refs_12_.refs_1_), channel_id=1, source_target_pairs={{0,2},{1,3},{2,0},{3,1},{4,6},{5,7},{6,4},{7,5},{8,10},{9,11},{10,... | collective-permute-start | bytes 1572872 | tf_op jit(solution)/shard_map/ppermute | solution.py:723
  401.8 10.7 %collective-permute-start.80 = (bf16[128,1024]{1,0:T(8,128)(2,1)}, bf16[128,1024]{1,0:T(8,128)(2,1)}, u32[]{:S(2)}, u32[]{:S(2)}) collective-permute-start(bf16[128,1024]{1,0:T(8,128)(2,1)} %get-tuple-element.373), channel_id=1, source_target_pairs={{0,1},{1,0},{2,3},{3,2},{4,5},{5,4},{6,7},{7,6},{8,9},{9,8},{10,11... | collective-permute-start | bytes 786440 | tf_op jit(solution)/shard_map/ppermute | solution.py:723
  401.8 9.6 %collective-permute-start.79 = (bf16[128,1024]{1,0:T(8,128)(2,1)}, bf16[128,1024]{1,0:T(8,128)(2,1)}, u32[]{:S(2)}, u32[]{:S(2)}) collective-permute-start(bf16[128,1024]{1,0:T(8,128)(2,1)} %get-tuple-element.374), channel_id=1, source_target_pairs={{0,1},{1,0},{2,3},{3,2},{4,5},{5,4},{6,7},{7,6},{8,9},{9,8},{10,11... | collective-permute-start | bytes 786440 | tf_op jit(solution)/shard_map/ppermute | solution.py:723
  420.0 61.1 %collective-permute-start.96 = (bf16[128,512]{1,0:T(8,128)(2,1)}, bf16[128,512]{1,0:T(8,128)(2,1)}, u32[]{:S(2)}, u32[]{:S(2)}) collective-permute-start(bf16[128,512]{1,0:T(8,128)(2,1)} %select_bitcast_fusion.20), channel_id=1, source_target_pairs={{0,4},{4,0},{8,12},{12,8},{16,20},{20,16},{24,28},{28,24},{1,5},{5... | collective-permute-start | bytes 393224 | tf_op jit(solution)/shard_map/ppermute | solution.py:723
  425.2 5.6 collective-permute-start.85
  454.2 14.3 %collective-permute-start.94 = (bf16[256,1024]{1,0:T(8,128)(2,1)S(1)}, bf16[256,1024]{1,0:T(8,128)(2,1)S(1)}, u32[]{:S(2)}, u32[]{:S(2)}) collective-permute-start(bf16[256,1024]{1,0:T(8,128)(2,1)S(1)} %select_convert_fusion), channel_id=1, source_target_pairs={{0,2},{1,3},{2,0},{3,1},{4,6},{5,7},{6,4},{7,5},{8,10},{9,11},{10,... | collective-permute-start | bytes 1572872 | tf_op jit(solution)/shard_map/ppermute | solution.py:723
  455.9 25.1 %collective-permute-start.87 = (bf16[2,2,128,640]{3,2,1,0:T(8,128)(2,1)S(1)}, bf16[2,2,128,640]{3,2,1,0:T(8,128)(2,1)}, u32[]{:S(2)}, u32[]{:S(2)}) collective-permute-start(bf16[2,2,128,640]{3,2,1,0:T(8,128)(2,1)S(1)} %select_bitcast_fusion), channel_id=1, source_target_pairs={{0,8},{4,12},{8,0},{12,4},{16,24},{20,28},{24,16},{28,20},{1,9},{5... | collective-permute-start | bytes 1966088 | tf_op jit(solution)/shard_map/ppermute | solution.py:723
  456.9 24.1 %collective-permute-start.86 = (bf16[2,2,128,640]{3,2,0,1:T(8,128)(2,1)}, bf16[2,2,128,640]{3,2,0,1:T(8,128)(2,1)}, u32[]{:S(2)}, u32[]{:S(2)}) collective-permute-start(bf16[2,2,128,640]{3,2,0,1:T(8,128)(2,1)} %select_bitcast_fusion.1), channel_id=1, source_target_pairs={{0,4},{4,0},{8,12},{12,8},{16,20},{20,16},{24,28},{28,24},{1,5},{5... | collective-permute-start | bytes 1966088 | tf_op jit(solution)/shard_map/ppermute | solution.py:723
  457.5 23.5 %collective-permute-start.95 = (bf16[128,512]{1,0:T(8,128)(2,1)S(1)}, bf16[128,512]{1,0:T(8,128)(2,1)S(1)}, u32[]{:S(2)}, u32[]{:S(2)}) collective-permute-start(bf16[128,512]{1,0:T(8,128)(2,1)S(1)} %select_bitcast_fusion.21), channel_id=1, source_target_pairs={{0,16},{4,20},{8,24},{12,28},{16,0},{20,4},{24,8},{28,12},{1,17},{... | collective-permute-start | bytes 393224 | tf_op jit(solution)/shard_map/ppermute | solution.py:723
  483.1 17.9 %collective-permute-start.90 = (bf16[2,128,640]{2,1,0:T(8,128)(2,1)}, bf16[2,128,640]{2,1,0:T(8,128)(2,1)}, u32[]{:S(2)}, u32[]{:S(2)}) collective-permute-start(bf16[2,128,640]{2,1,0:T(8,128)(2,1)} %select_bitcast_fusion.8), channel_id=1, source_target_pairs={{0,16},{4,20},{8,24},{12,28},{16,0},{20,4},{24,8},{28,12},{1,17},{... | collective-permute-start | bytes 983048 | tf_op jit(solution)/shard_map/ppermute | solution.py:723
  485.6 18.1 %collective-permute-start.88 = (bf16[2,128,640]{2,1,0:T(8,128)(2,1)S(1)}, bf16[2,128,640]{2,1,0:T(8,128)(2,1)S(1)}, u32[]{:S(2)}, u32[]{:S(2)}) collective-permute-start(bf16[2,128,640]{2,1,0:T(8,128)(2,1)S(1)} %select_bitcast_fusion.9), channel_id=1, source_target_pairs={{0,8},{4,12},{8,0},{12,4},{16,24},{20,28},{24,16},{28,20},{1,9},{5... | collective-permute-start | bytes 983048 | tf_op jit(solution)/shard_map/ppermute | solution.py:723
  502.1 8.1 %collective-permute-start.91 = (bf16[128,640]{1,0:T(8,128)(2,1)S(1)}, bf16[128,640]{1,0:T(8,128)(2,1)S(1)}, u32[]{:S(2)}, u32[]{:S(2)}) collective-permute-start(bf16[128,640]{1,0:T(8,128)(2,1)S(1)} %select_bitcast_fusion.16), channel_id=1, source_target_pairs={{0,4},{4,0},{8,12},{12,8},{16,20},{20,16},{24,28},{28,24},{1,5},{5... | collective-permute-start | bytes 491528 | tf_op jit(solution)/shard_map/ppermute | solution.py:723
  503.8 20.9 %collective-permute-start.89 = (bf16[128,640]{1,0:T(8,128)(2,1)S(1)}, bf16[128,640]{1,0:T(8,128)(2,1)S(1)}, u32[]{:S(2)}, u32[]{:S(2)}) collective-permute-start(bf16[128,640]{1,0:T(8,128)(2,1)S(1)} %select_bitcast_fusion.17), channel_id=1, source_target_pairs={{0,16},{4,20},{8,24},{12,28},{16,0},{20,4},{24,8},{28,12},{1,17},{... | collective-permute-start | bytes 491528 | tf_op jit(solution)/shard_map/ppermute | solution.py:723
  (193 other events, 964.0 us)
Sparse Core Ops, SparseCore 0:
  13.1 126.9 all-gather.2
  142.9 75.9 all-gather.4
  315.4 101.9 reduce-scatter.2
  421.3 105.7 reduce-scatter.4

commit v3 on v2

--- a/solution.py
+++ b/solution.py
@@ -797,8 +797,13 @@
     for axis in ("mp", "dp"):
         bit = 1
         while bit < lax.axis_size(axis):
-            values = values + swap(values, axis, bit)
-            bit *= 2
+            if 2 * bit < lax.axis_size(axis):
+                first, second, both = [swap(values, axis, at) for at in (bit, 2 * bit, 3 * bit)]
+                values = (values + first) + (second + both)
+                bit *= 4
+            else:
+                values = values + swap(values, axis, bit)
+                bit *= 2
     return values
 
 

time: 592 us -> 587 us (level)
    ppermute x103 -> x105, waiting for transfers between devices: 183 us -> 175 us  [swap(): return lax.ppermute(values, axis, [(i, i ^ bit) for i in range(count)])]
    ppermute x103 -> x105, starting transfers between devices: 82 us -> 87.8 us  [swap(): return lax.ppermute(values, axis, [(i, i ^ bit) for i in range(count)])]
    unnamed x290 -> x288, local copies, waits for them, and re-layouts: 33 us -> 34.4 us
  transfers between devices with their start and end apart: 107 -> 109, of which waited for: 54 -> 54; matrix products, arithmetic and copies ran while one was open for 11% -> 11% of each run, Pallas kernels for 24% -> 24%
where the time goes in v3:
time: 587 us; the launch traced here: 577 us
  waiting for transfers between devices  187 us (32%)
  Pallas kernels  167 us (28%)
  starting transfers between devices  88.7 us (15%)
  other arithmetic  52.6 us (9%)
  local copies, waits for them, and re-layouts  50.2 us (9%)
  between operations  30.6 us (5%)
    ppermute x105, waiting for transfers between devices, swap(): return lax.ppermute(values, axis, [(i, i ^ bit) for i in range(count)])  175 us
    pallas_call x47, Pallas kernels, call(): pl.pallas_call(body_fn, grid=grid, in_specs=in_specs, out_specs=out_specs...  167 us
    ppermute x105, starting transfers between devices, swap(): return lax.ppermute(values, axis, [(i, i ^ bit) for i in range(count)])  87.8 us
    unnamed x288, local copies, waits for them, and re-layouts  34.4 us
    all_gather x2, waiting for transfers between devices, gather(): return lax.all_gather(values, 'dp', axis=0, tiled=True)  12 us
  transfers between devices with their start and end apart: 109, of which 54 were waited for; matrix products, arithmetic and copies ran while one was open for 11% of the time, Pallas kernels for 24%

profile of v3, /device:TPU:0, one launch (start us, length us, event | category | flops | bytes accessed | tf_op | source)
XLA Modules:
  0.0 576.5 jit_solution(18266360076220623108)
XLA Ops:
  13.2 3.0 collective-permute-start.6
  23.4 9.0 %collective-permute-done.3 = bf16[128,640]{0,1:T(8,128)(2,1)S(1)} collective-permute-done((bf16[128,640]{0,1:T(8,128)(2,1)S(1)}, bf16[128,640]{0,1:T(8,128)(2,1)S(1)}, u32[]{:S(2)}, u32[]{:S(2)}) %collective-permute-start.3) | collective-permute-done | bytes 163872 | tf_op jit(solution)/shard_map/ppermute | solution.py:723
  32.5 8.6 %collective-permute-start.4 = (bf16[2,128,640]{1,2,0:T(8,128)(2,1)S(1)}, bf16[2,128,640]{1,2,0:T(8,128)(2,1)S(1)}, u32[]{:S(2)}, u32[]{:S(2)}) collective-permute-start(bf16[2,128,640]{1,2,0:T(8,128)(2,1)S(1)} %pad_maximum_fusion.7), channel_id=1, source_target_pairs={{0,8},{4,12},{8,0},{12,4},{16,24},{20,28},{24,16},{28,20},{1,9},{5... | collective-permute-start | bytes 983048 | tf_op jit(solution)/shard_map/ppermute | solution.py:723
  41.1 11.0 %collective-permute-done.7 = bf16[2,128,512]{1,2,0:T(8,128)(2,1)S(1)} collective-permute-done((bf16[2,128,512]{1,2,0:T(8,128)(2,1)S(1)}, bf16[2,128,512]{1,2,0:T(8,128)(2,1)S(1)}, u32[]{:S(2)}, u32[]{:S(2)}) %collective-permute-start.7) | collective-permute-done | bytes 262176 | tf_op jit(solution)/shard_map/ppermute | solution.py:723
  52.2 4.4 collective-permute-start.8
  58.9 8.7 %collective-permute-done.4 = bf16[2,128,640]{1,2,0:T(8,128)(2,1)S(1)} collective-permute-done((bf16[2,128,640]{1,2,0:T(8,128)(2,1)S(1)}, bf16[2,128,640]{1,2,0:T(8,128)(2,1)S(1)}, u32[]{:S(2)}, u32[]{:S(2)}) %collective-permute-start.4) | collective-permute-done | bytes 327712 | tf_op jit(solution)/shard_map/ppermute | solution.py:723
  70.9 16.6 %collective-permute-done.8 = bf16[2,2,128,512]{2,3,1,0:T(8,128)(2,1)S(1)} collective-permute-done((bf16[2,2,128,512]{2,3,1,0:T(8,128)(2,1)S(1)}, bf16[2,2,128,512]{2,3,1,0:T(8,128)(2,1)S(1)}, u32[]{:S(2)}, u32[]{:S(2)}) %collective-permute-start.8) | collective-permute-done | bytes 524320 | tf_op jit(solution)/shard_map/ppermute | solution.py:723
  89.0 6.2 %collective-permute-done.5 = bf16[2,2,128,640]{2,3,1,0:T(8,128)(2,1)} collective-permute-done((bf16[2,2,128,640]{2,3,1,0:T(8,128)(2,1)S(1)}, bf16[2,2,128,640]{2,3,1,0:T(8,128)(2,1)}, u32[]{:S(2)}, u32[]{:S(2)}) %collective-permute-start.5) | collective-permute-done | bytes 655392 | tf_op jit(solution)/shard_map/ppermute | solution.py:723
  104.2 5.8 %shard_map.362 = (bf16[512,256]{1,0:T(8,128)(2,1)}, f32[8,512]{1,0:T(8,128)}, bf16[256,1024]{1,0:T(8,128)(2,1)S(1)}, bf16[256,1024]{1,0:T(8,128)(2,1)S(1)}) custom-call(s32[1]{0:T(128)} %bitcast.core_ref.refs_0_, bf16[512,768]{1,0:T(8,128)(2,1)} %shard_map.361.m_ref.refs_2_.mix0, bf16[512,768]{1,0:T(8,128)(2,1)} %shard_map.360.mo_ref.refs_1_.mix1, ...), custom_call_target="tpu_custom_call" | custom-call | flops 939524096 | bytes 6340612 | tf_op jit(solution)/shard_map/pallas_call | solution.py:74
  117.7 5.7 shard_map.363
  126.9 3.4 collective-permute-done.15.refs_2_
  135.2 4.0 all-gather.3.cloned.1.call-done.up_ref.down_ref.w_ref.refs_6_.refs_1_.refs_3_.refs_4_
  141.9 4.2 shard_map.365
  151.9 4.5 shard_map.367
  158.6 5.8 collective-permute-done.25.refs_2_
  167.7 9.9 %collective-permute-done.26.refs_2_ = bf16[256,1024]{1,0:T(8,128)(2,1)S(1)} collective-permute-done((bf16[256,1024]{1,0:T(8,128)(2,1)S(1)}, bf16[256,1024]{1,0:T(8,128)(2,1)S(1)}, u32[]{:S(2)}, u32[]{:S(2)}) %collective-permute-start.26) | collective-permute-done | bytes 524320 | tf_op jit(solution)/shard_map/ppermute | solution.py:723
  184.4 5.7 shard_map.372
  193.8 5.7 shard_map.373
  202.2 4.2 collective-permute-done.35.refs_2_
  209.9 8.0 %all-gather.5.cloned.1.call-done.up_ref.down_ref.refs_3_.refs_4_ = bf16[1024,2176]{1,0:T(8,128)(2,1)} async-done(((bf16[128,2176]{1,0:T(8,128)(2,1)}), bf16[1024,2176]{1,0:T(8,128)(2,1)}) %all-gather.5.cloned.1.call-update) | async-done | bytes 4456464 | tf_op jit(solution)/shard_map/all_gather | solution.py:851
  220.2 4.6 shard_map.375
  230.5 4.7 shard_map.377
  237.4 5.5 collective-permute-done.45.refs_2_
  246.7 9.3 %collective-permute-done.46.refs_2_ = bf16[256,1024]{1,0:T(8,128)(2,1)S(1)} collective-permute-done((bf16[256,1024]{1,0:T(8,128)(2,1)S(1)}, bf16[256,1024]{1,0:T(8,128)(2,1)S(1)}, u32[]{:S(2)}, u32[]{:S(2)}) %collective-permute-start.46) | collective-permute-done | bytes 524320 | tf_op jit(solution)/shard_map/ppermute | solution.py:723
  260.0 14.5 %shard_map.380 = (f32[256,1024]{1,0:T(8,128)S(1)}, f32[256,1024]{1,0:T(8,128)S(1)}, f32[1024,128]{1,0:T(8,128)S(1)}, f32[8,128]{1,0:T(8,128)S(1)}) custom-call(f32[1]{0:T(128)S(6)} %copy.261.ls_ref, bf16[1024,128]{1,0:T(8,128)(2,1)S(1)} %pad_maximum_fusion.9.e_ref, f32[1024,128]{1,0:T(8,128)S(1)} %broadcast_in_dim.92.seg_ref, ...), custom_call_target="tpu_custom_call" | custom-call | flops 2684354560 | bytes 4763652 | tf_op jit(solution)/shard_map/pallas_call | solution.py:74
  280.1 3.6 shard_map.382
  287.4 3.6 shard_map.384
  293.2 6.7 %collective-permute-done.56.refs_2_ = bf16[256,1024]{1,0:T(8,128)(2,1)S(1)} collective-permute-done((bf16[256,1024]{1,0:T(8,128)(2,1)S(1)}, bf16[256,1024]{1,0:T(8,128)(2,1)S(1)}, u32[]{:S(2)}, u32[]{:S(2)}) %collective-permute-start.56) | collective-permute-done | bytes 524320 | tf_op jit(solution)/shard_map/ppermute | solution.py:723
  305.8 7.8 %shard_map.386 = bf16[1024,2048]{1,0:T(8,128)(2,1)} custom-call(bf16[256,1024]{1,0:T(8,128)(2,1)S(1)} %get-tuple-element.209.ho_ref.refs_0_, bf16[256,1024]{1,0:T(8,128)(2,1)S(1)} %constant_dynamic-update-slice_fusion.12.hs_ref.refs_1_, bf16[256,1024]{1,0:T(8,128)(2,1)S(1)} %get-tuple-element.214.ho_ref.refs_2_, ...), custom_call_target="tpu_custom_call" | custom-call | flops 4294967296 | bytes 14680064 | tf_op jit(solution)/shard_map/pallas_call | solution.py:74
  325.7 10.6 %shard_map.388 = (bf16[512,768]{1,0:T(8,128)(2,1)S(1)}, bf16[512,768]{1,0:T(8,128)(2,1)S(1)}) custom-call(s32[1]{0:T(128)} %bitcast.core_ref.refs_0_, bf16[256,1024]{1,0:T(8,128)(2,1)S(1)} %copy-done.49, bf16[256,1024]{1,0:T(8,128)(2,1)S(1)} %constant_dynamic-update-slice_fusion.20.d0s.refs_5_, bf16[256,1024]{1,0:T(8,128)(2,1)S(1)} %get-tuple-element.248.d1o.refs_6_, ...), custom_call_target="tpu_custom_call" | custom-call | flops 3892314112 | bytes 7405572 | tf_op jit(solution)/shard_map/pallas_call | solution.py:74
  342.5 4.6 shard_map.391
  348.2 5.5 collective-permute-done.66.refs_2_
  360.4 3.8 shard_map.393
  372.5 6.6 %collective-permute-done.72 = bf16[2,2,128,512]{3,2,0,1:T(8,128)(2,1)} collective-permute-done((bf16[2,2,128,512]{3,2,0,1:T(8,128)(2,1)}, bf16[2,2,128,512]{3,2,0,1:T(8,128)(2,1)}, u32[]{:S(2)}, u32[]{:S(2)}) %collective-permute-start.72) | collective-permute-done | bytes 524320 | tf_op jit(solution)/shard_map/ppermute | solution.py:723
  386.0 2.8 copy-done.3
  388.8 3.7 shard_map.395
  402.9 8.0 %shard_map.397 = bf16[1024,2048]{1,0:T(8,128)(2,1)} custom-call(bf16[256,1024]{1,0:T(8,128)(2,1)S(1)} %copy-done.60, bf16[256,1024]{1,0:T(8,128)(2,1)S(1)} %copy-done.68, bf16[256,1024]{1,0:T(8,128)(2,1)S(1)} %copy-done.62, bf16[256,1024]{1,0:T(8,128)(2,1)S(1)} %copy-done.70, bf16[256,1024]{1,0:T(8,128)(2,1)S(1)} %copy-done.47, ...), custom_call_target="tpu_custom_call" | custom-call | flops 4294967296 | bytes 14680064 | tf_op jit(solution)/shard_map/pallas_call | solution.py:74
  413.0 4.2 collective-permute-done.82
  433.0 10.6 %shard_map.399 = (bf16[512,768]{1,0:T(8,128)(2,1)S(1)}, bf16[512,768]{1,0:T(8,128)(2,1)S(1)}) custom-call(s32[1]{0:T(128)} %bitcast.core_ref.refs_0_, bf16[256,1024]{1,0:T(8,128)(2,1)S(1)} %copy-done.51, bf16[256,1024]{1,0:T(8,128)(2,1)S(1)} %copy-done.66, bf16[256,1024]{1,0:T(8,128)(2,1)S(1)} %copy-done.53, ...), custom_call_target="tpu_custom_call" | custom-call | flops 3892314112 | bytes 9764868 | tf_op jit(solution)/shard_map/pallas_call | solution.py:74
  443.7 4.9 shard_map.400.refs_2_
  459.3 8.2 %collective-permute-done.94 = bf16[256,1024]{1,0:T(8,128)(2,1)S(1)} collective-permute-done((bf16[256,1024]{1,0:T(8,128)(2,1)S(1)}, bf16[256,1024]{1,0:T(8,128)(2,1)S(1)}, u32[]{:S(2)}, u32[]{:S(2)}) %collective-permute-start.94) | collective-permute-done | bytes 524320 | tf_op jit(solution)/shard_map/ppermute | solution.py:723
  471.0 8.4 %collective-permute-done.87 = bf16[2,2,128,640]{3,2,1,0:T(8,128)(2,1)} collective-permute-done((bf16[2,2,128,640]{3,2,1,0:T(8,128)(2,1)}, bf16[2,2,128,640]{3,2,1,0:T(8,128)(2,1)}, u32[]{:S(2)}, u32[]{:S(2)}) %collective-permute-start.87) | collective-permute-done | bytes 655392 | tf_op jit(solution)/shard_map/ppermute | solution.py:723
  491.9 7.6 %collective-permute-done.90 = bf16[2,128,640]{2,1,0:T(8,128)(2,1)} collective-permute-done((bf16[2,128,640]{2,1,0:T(8,128)(2,1)}, bf16[2,128,640]{2,1,0:T(8,128)(2,1)}, u32[]{:S(2)}, u32[]{:S(2)}) %collective-permute-start.90) | collective-permute-done | bytes 327712 | tf_op jit(solution)/shard_map/ppermute | solution.py:723
  503.4 8.5 %collective-permute-start.89 = (bf16[128,640]{1,0:T(8,128)(2,1)S(1)}, bf16[128,640]{1,0:T(8,128)(2,1)S(1)}, u32[]{:S(2)}, u32[]{:S(2)}) collective-permute-start(bf16[128,640]{1,0:T(8,128)(2,1)S(1)} %select_bitcast_fusion.17), channel_id=1, source_target_pairs={{0,16},{4,20},{8,24},{12,28},{16,0},{20,4},{24,8},{28,12},{1,17},{... | collective-permute-start | bytes 491528 | tf_op jit(solution)/shard_map/ppermute | solution.py:723
  511.9 11.9 %collective-permute-done.89 = bf16[128,640]{1,0:T(8,128)(2,1)S(1)} collective-permute-done((bf16[128,640]{1,0:T(8,128)(2,1)S(1)}, bf16[128,640]{1,0:T(8,128)(2,1)S(1)}, u32[]{:S(2)}, u32[]{:S(2)}) %collective-permute-start.89) | collective-permute-done | bytes 163872 | tf_op jit(solution)/shard_map/ppermute | solution.py:723
  554.4 3.2 shard_map.403
  557.7 4.1 shard_map.406
  561.9 3.2 shard_map.405
  (686 shorter events, 230.6 us)
Async XLA Ops:
  7.2 131.9 %all-gather.3.cloned.1.call-start = ((), (), s32[]{:S(2)}) async-start(), calls=%async_computation.2 | async-start | bytes 7077888 | tf_op jit(solution)/shard_map/all_gather | solution.py:851
  13.0 204.9 %all-gather.5.cloned.1.call-start = ((), (), s32[]{:S(2)}) async-start(), calls=%async_computation.3 | async-start | bytes 5013504 | tf_op jit(solution)/shard_map/all_gather | solution.py:851
  13.2 9.7 %collective-permute-start.6 = (bf16[128,512]{0,1:T(8,128)(2,1)S(1)}, bf16[128,512]{0,1:T(8,128)(2,1)S(1)}, u32[]{:S(2)}, u32[]{:S(2)}) collective-permute-start(bf16[128,512]{0,1:T(8,128)(2,1)S(1)} %fusion.12), channel_id=1, source_target_pairs={{0,4},{4,0},{8,12},{12,8},{16,20},{20,16},{24,28},{28,24},{1,5},{5... | collective-permute-start | bytes 393224 | tf_op jit(solution)/shard_map/ppermute | solution.py:723
  16.2 16.1 %collective-permute-start.3 = (bf16[128,640]{0,1:T(8,128)(2,1)S(1)}, bf16[128,640]{0,1:T(8,128)(2,1)S(1)}, u32[]{:S(2)}, u32[]{:S(2)}) collective-permute-start(bf16[128,640]{0,1:T(8,128)(2,1)S(1)} %slice.253), channel_id=1, source_target_pairs={{0,16},{4,20},{8,24},{12,28},{16,0},{20,4},{24,8},{28,12},{1,17},{... | collective-permute-start | bytes 491528 | tf_op jit(solution)/shard_map/ppermute | solution.py:723
  18.9 37.7 %collective-permute-start = (bf16[256,1024]{1,0:T(8,128)(2,1)S(1)}, bf16[256,1024]{1,0:T(8,128)(2,1)S(1)}, u32[]{:S(2)}, u32[]{:S(2)}) collective-permute-start(bf16[256,1024]{1,0:T(8,128)(2,1)S(1)} %copy-done.124), channel_id=1, source_target_pairs={{0,2},{1,3},{2,0},{3,1},{4,6},{5,7},{6,4},{7,5},{8,10},{9,11},{10,... | collective-permute-start | bytes 1572872 | tf_op jit(solution)/shard_map/ppermute | solution.py:723
  23.0 29.1 %collective-permute-start.7 = (bf16[2,128,512]{1,2,0:T(8,128)(2,1)S(1)}, bf16[2,128,512]{1,2,0:T(8,128)(2,1)S(1)}, u32[]{:S(2)}, u32[]{:S(2)}) collective-permute-start(bf16[2,128,512]{1,2,0:T(8,128)(2,1)S(1)} %pad_maximum_fusion.8), channel_id=1, source_target_pairs={{0,16},{4,20},{8,24},{12,28},{16,0},{20,4},{24,8},{28,12},{1,17},{... | collective-permute-start | bytes 786440 | tf_op jit(solution)/shard_map/ppermute | solution.py:723
  32.5 35.1 %collective-permute-start.4 = (bf16[2,128,640]{1,2,0:T(8,128)(2,1)S(1)}, bf16[2,128,640]{1,2,0:T(8,128)(2,1)S(1)}, u32[]{:S(2)}, u32[]{:S(2)}) collective-permute-start(bf16[2,128,640]{1,2,0:T(8,128)(2,1)S(1)} %pad_maximum_fusion.7), channel_id=1, source_target_pairs={{0,8},{4,12},{8,0},{12,4},{16,24},{20,28},{24,16},{28,20},{1,9},{5... | collective-permute-start | bytes 983048 | tf_op jit(solution)/shard_map/ppermute | solution.py:723
  52.2 35.3 %collective-permute-start.8 = (bf16[2,2,128,512]{2,3,1,0:T(8,128)(2,1)S(1)}, bf16[2,2,128,512]{2,3,1,0:T(8,128)(2,1)S(1)}, u32[]{:S(2)}, u32[]{:S(2)}) collective-permute-start(bf16[2,2,128,512]{2,3,1,0:T(8,128)(2,1)S(1)} %pad_maximum_fusion.5), channel_id=1, source_target_pairs={{0,8},{4,12},{8,0},{12,4},{16,24},{20,28},{24,16},{28,20},{1,9},{5... | collective-permute-start | bytes 1572872 | tf_op jit(solution)/shard_map/ppermute | solution.py:723
  58.2 10.4 %collective-permute-start.9 = (bf16[128,1024]{1,0:T(8,128)(2,1)S(1)}, bf16[128,1024]{1,0:T(8,128)(2,1)S(1)}, u32[]{:S(2)}, u32[]{:S(2)}) collective-permute-start(bf16[128,1024]{1,0:T(8,128)(2,1)S(1)} %get-tuple-element.432), channel_id=1, source_target_pairs={{0,1},{1,0},{2,3},{3,2},{4,5},{5,4},{6,7},{7,6},{8,9},{9,8},{10,11... | collective-permute-start | bytes 786440 | tf_op jit(solution)/shard_map/ppermute | solution.py:723
  58.3 10.5 %collective-permute-start.1 = (bf16[128,1024]{1,0:T(8,128)(2,1)S(1)}, bf16[128,1024]{1,0:T(8,128)(2,1)S(1)}, u32[]{:S(2)}, u32[]{:S(2)}) collective-permute-start(bf16[128,1024]{1,0:T(8,128)(2,1)S(1)} %get-tuple-element.436), channel_id=1, source_target_pairs={{0,1},{1,0},{2,3},{3,2},{4,5},{5,4},{6,7},{7,6},{8,9},{9,8},{10,11... | collective-permute-start | bytes 786440 | tf_op jit(solution)/shard_map/ppermute | solution.py:723
  67.8 27.4 %collective-permute-start.5 = (bf16[2,2,128,640]{2,3,1,0:T(8,128)(2,1)S(1)}, bf16[2,2,128,640]{2,3,1,0:T(8,128)(2,1)}, u32[]{:S(2)}, u32[]{:S(2)}) collective-permute-start(bf16[2,2,128,640]{2,3,1,0:T(8,128)(2,1)S(1)} %pad_maximum_fusion.2), channel_id=1, source_target_pairs={{0,4},{4,0},{8,12},{12,8},{16,20},{20,16},{24,28},{28,24},{1,5},{5... | collective-permute-start | bytes 1966088 | tf_op jit(solution)/shard_map/ppermute | solution.py:723
  112.9 356.2 %reduce-scatter.3.cloned.1.call-start = ((), (), s32[]{:S(2)}) async-start(), calls=%async_computation.4 | async-start | bytes 4718592 | tf_op jit(solution)/shard_map/reduce_scatter | solution.py:985
  116.0 14.3 %collective-permute-start.15 = (bf16[256,1024]{1,0:T(8,128)(2,1)}, bf16[256,1024]{1,0:T(8,128)(2,1)}, u32[]{:S(2)}, u32[]{:S(2)}) collective-permute-start(bf16[256,1024]{1,0:T(8,128)(2,1)} %add_convert_fusion.13.refs_7_.refs_1_), channel_id=1, source_target_pairs={{0,2},{1,3},{2,0},{3,1},{4,6},{5,7},{6,4},{7,5},{8,10},{9,11},{10,... | collective-permute-start | bytes 1572872 | tf_op jit(solution)/shard_map/ppermute | solution.py:723
  133.4 15.0 %collective-permute-start.20 = (bf16[256,1024]{1,0:T(8,128)(2,1)S(1)}, bf16[256,1024]{1,0:T(8,128)(2,1)S(1)}, u32[]{:S(2)}, u32[]{:S(2)}) collective-permute-start(bf16[256,1024]{1,0:T(8,128)(2,1)S(1)} %add_convert_fusion.12.refs_1_), channel_id=1, source_target_pairs={{0,2},{1,3},{2,0},{3,1},{4,6},{5,7},{6,4},{7,5},{8,10},{9,11},{10,... | collective-permute-start | bytes 1572872 | tf_op jit(solution)/shard_map/ppermute | solution.py:723
  150.4 14.0 %collective-permute-start.25 = (bf16[256,1024]{1,0:T(8,128)(2,1)S(1)}, bf16[256,1024]{1,0:T(8,128)(2,1)S(1)}, u32[]{:S(2)}, u32[]{:S(2)}) collective-permute-start(bf16[256,1024]{1,0:T(8,128)(2,1)S(1)} %add_convert_fusion.11.refs_1_), channel_id=1, source_target_pairs={{0,2},{1,3},{2,0},{3,1},{4,6},{5,7},{6,4},{7,5},{8,10},{9,11},{10,... | collective-permute-start | bytes 1572872 | tf_op jit(solution)/shard_map/ppermute | solution.py:723
  164.3 13.2 %collective-permute-start.26 = (bf16[256,1024]{1,0:T(8,128)(2,1)S(1)}, bf16[256,1024]{1,0:T(8,128)(2,1)S(1)}, u32[]{:S(2)}, u32[]{:S(2)}) collective-permute-start(bf16[256,1024]{1,0:T(8,128)(2,1)S(1)} %add_convert_fusion.10.refs_1_), channel_id=1, source_target_pairs={{0,2},{1,3},{2,0},{3,1},{4,6},{5,7},{6,4},{7,5},{8,10},{9,11},{10,... | collective-permute-start | bytes 1572872 | tf_op jit(solution)/shard_map/ppermute | solution.py:723
  167.1 11.9 %collective-permute-start.29 = (bf16[128,1024]{1,0:T(8,128)(2,1)S(1)}, bf16[128,1024]{1,0:T(8,128)(2,1)S(1)}, u32[]{:S(2)}, u32[]{:S(2)}) collective-permute-start(bf16[128,1024]{1,0:T(8,128)(2,1)S(1)} %get-tuple-element.416), channel_id=1, source_target_pairs={{0,1},{1,0},{2,3},{3,2},{4,5},{5,4},{6,7},{7,6},{8,9},{9,8},{10,11... | collective-permute-start | bytes 786440 | tf_op jit(solution)/shard_map/ppermute | solution.py:723
  167.2 12.4 %collective-permute-start.30 = (bf16[128,1024]{1,0:T(8,128)(2,1)S(1)}, bf16[128,1024]{1,0:T(8,128)(2,1)S(1)}, u32[]{:S(2)}, u32[]{:S(2)}) collective-permute-start(bf16[128,1024]{1,0:T(8,128)(2,1)S(1)} %get-tuple-element.415), channel_id=1, source_target_pairs={{0,1},{1,0},{2,3},{3,2},{4,5},{5,4},{6,7},{7,6},{8,9},{9,8},{10,11... | collective-permute-start | bytes 786440 | tf_op jit(solution)/shard_map/ppermute | solution.py:723
  192.3 14.0 %collective-permute-start.35 = (bf16[256,1024]{1,0:T(8,128)(2,1)S(1)}, bf16[256,1024]{1,0:T(8,128)(2,1)S(1)}, u32[]{:S(2)}, u32[]{:S(2)}) collective-permute-start(bf16[256,1024]{1,0:T(8,128)(2,1)S(1)} %add_convert_fusion.9.refs_7_.refs_1_), channel_id=1, source_target_pairs={{0,2},{1,3},{2,0},{3,1},{4,6},{5,7},{6,4},{7,5},{8,10},{9,11},{10,... | collective-permute-start | bytes 1572872 | tf_op jit(solution)/shard_map/ppermute | solution.py:723
  208.4 18.6 %collective-permute-start.40 = (bf16[256,1024]{1,0:T(8,128)(2,1)S(1)}, bf16[256,1024]{1,0:T(8,128)(2,1)S(1)}, u32[]{:S(2)}, u32[]{:S(2)}) collective-permute-start(bf16[256,1024]{1,0:T(8,128)(2,1)S(1)} %add_convert_fusion.8.refs_1_), channel_id=1, source_target_pairs={{0,2},{1,3},{2,0},{3,1},{4,6},{5,7},{6,4},{7,5},{8,10},{9,11},{10,... | collective-permute-start | bytes 1572872 | tf_op jit(solution)/shard_map/ppermute | solution.py:723
  229.0 14.0 %collective-permute-start.45 = (bf16[256,1024]{1,0:T(8,128)(2,1)S(1)}, bf16[256,1024]{1,0:T(8,128)(2,1)S(1)}, u32[]{:S(2)}, u32[]{:S(2)}) collective-permute-start(bf16[256,1024]{1,0:T(8,128)(2,1)S(1)} %add_convert_fusion.7.refs_1_), channel_id=1, source_target_pairs={{0,2},{1,3},{2,0},{3,1},{4,6},{5,7},{6,4},{7,5},{8,10},{9,11},{10,... | collective-permute-start | bytes 1572872 | tf_op jit(solution)/shard_map/ppermute | solution.py:723
  242.9 13.1 %collective-permute-start.46 = (bf16[256,1024]{1,0:T(8,128)(2,1)S(1)}, bf16[256,1024]{1,0:T(8,128)(2,1)S(1)}, u32[]{:S(2)}, u32[]{:S(2)}) collective-permute-start(bf16[256,1024]{1,0:T(8,128)(2,1)S(1)} %add_convert_fusion.6.refs_1_), channel_id=1, source_target_pairs={{0,2},{1,3},{2,0},{3,1},{4,6},{5,7},{6,4},{7,5},{8,10},{9,11},{10,... | collective-permute-start | bytes 1572872 | tf_op jit(solution)/shard_map/ppermute | solution.py:723
  285.9 14.0 %collective-permute-start.56 = (bf16[256,1024]{1,0:T(8,128)(2,1)S(1)}, bf16[256,1024]{1,0:T(8,128)(2,1)S(1)}, u32[]{:S(2)}, u32[]{:S(2)}) collective-permute-start(bf16[256,1024]{1,0:T(8,128)(2,1)S(1)} %add_convert_fusion.5.refs_5_.refs_1_), channel_id=1, source_target_pairs={{0,2},{1,3},{2,0},{3,1},{4,6},{5,7},{6,4},{7,5},{8,10},{9,11},{10,... | collective-permute-start | bytes 1572872 | tf_op jit(solution)/shard_map/ppermute | solution.py:723
  299.9 13.7 %collective-permute-start.59 = (bf16[256,1024]{1,0:T(8,128)(2,1)S(1)}, bf16[256,1024]{1,0:T(8,128)(2,1)S(1)}, u32[]{:S(2)}, u32[]{:S(2)}) collective-permute-start(bf16[256,1024]{1,0:T(8,128)(2,1)S(1)} %add_convert_fusion.4.refs_12_.refs_1_), channel_id=1, source_target_pairs={{0,2},{1,3},{2,0},{3,1},{4,6},{5,7},{6,4},{7,5},{8,10},{9,11},{10,... | collective-permute-start | bytes 1572872 | tf_op jit(solution)/shard_map/ppermute | solution.py:723
  305.3 16.6 %collective-permute-start.58 = (bf16[128,1024]{1,0:T(8,128)(2,1)}, bf16[128,1024]{1,0:T(8,128)(2,1)}, u32[]{:S(2)}, u32[]{:S(2)}) collective-permute-start(bf16[128,1024]{1,0:T(8,128)(2,1)} %get-tuple-element.389), channel_id=1, source_target_pairs={{0,1},{1,0},{2,3},{3,2},{4,5},{5,4},{6,7},{7,6},{8,9},{9,8},{10,11... | collective-permute-start | bytes 786440 | tf_op jit(solution)/shard_map/ppermute | solution.py:723
  305.3 15.5 %collective-permute-start.57 = (bf16[128,1024]{1,0:T(8,128)(2,1)}, bf16[128,1024]{1,0:T(8,128)(2,1)}, u32[]{:S(2)}, u32[]{:S(2)}) collective-permute-start(bf16[128,1024]{1,0:T(8,128)(2,1)} %get-tuple-element.390), channel_id=1, source_target_pairs={{0,1},{1,0},{2,3},{3,2},{4,5},{5,4},{6,7},{7,6},{8,9},{9,8},{10,11... | collective-permute-start | bytes 786440 | tf_op jit(solution)/shard_map/ppermute | solution.py:723
  314.4 212.2 %reduce-scatter.5.cloned.1.call-start = ((), (), s32[]{:S(2)}) async-start(), calls=%async_computation.5 | async-start | bytes 4718592 | tf_op jit(solution)/shard_map/reduce_scatter | solution.py:985
  339.6 14.0 %collective-permute-start.66 = (bf16[256,1024]{1,0:T(8,128)(2,1)S(1)}, bf16[256,1024]{1,0:T(8,128)(2,1)S(1)}, u32[]{:S(2)}, u32[]{:S(2)}) collective-permute-start(bf16[256,1024]{1,0:T(8,128)(2,1)S(1)} %add_convert_fusion.3.refs_2_.refs_12_.refs_1_), channel_id=1, source_target_pairs={{0,2},{1,3},{2,0},{3,1},{4,6},{5,7},{6,4},{7,5},{8,10},{9,11},{10,... | collective-permute-start | bytes 1572872 | tf_op jit(solution)/shard_map/ppermute | solution.py:723
  341.7 5.5 collective-permute-start.64
  356.1 15.1 %collective-permute-start.71 = (bf16[256,1024]{1,0:T(8,128)(2,1)}, bf16[256,1024]{1,0:T(8,128)(2,1)}, u32[]{:S(2)}, u32[]{:S(2)}) collective-permute-start(bf16[256,1024]{1,0:T(8,128)(2,1)} %add_convert_fusion.2.refs_1_), channel_id=1, source_target_pairs={{0,2},{1,3},{2,0},{3,1},{4,6},{5,7},{6,4},{7,5},{8,10},{9,11},{10,... | collective-permute-start | bytes 1572872 | tf_op jit(solution)/shard_map/ppermute | solution.py:723
  358.1 14.5 %collective-permute-start.73 = (bf16[2,2,128,512]{3,2,1,0:T(8,128)(2,1)}, bf16[2,2,128,512]{3,2,1,0:T(8,128)(2,1)}, u32[]{:S(2)}, u32[]{:S(2)}) collective-permute-start(bf16[2,2,128,512]{3,2,1,0:T(8,128)(2,1)} %select_bitcast_fusion.4), channel_id=1, source_target_pairs={{0,8},{4,12},{8,0},{12,4},{16,24},{20,28},{24,16},{28,20},{1,9},{5... | collective-permute-start | bytes 1572872 | tf_op jit(solution)/shard_map/ppermute | solution.py:723
  359.9 19.3 %collective-permute-start.72 = (bf16[2,2,128,512]{3,2,0,1:T(8,128)(2,1)}, bf16[2,2,128,512]{3,2,0,1:T(8,128)(2,1)}, u32[]{:S(2)}, u32[]{:S(2)}) collective-permute-start(bf16[2,2,128,512]{3,2,0,1:T(8,128)(2,1)} %select_bitcast_fusion.5), channel_id=1, source_target_pairs={{0,4},{4,0},{8,12},{12,8},{16,20},{20,16},{24,28},{28,24},{1,5},{5... | collective-permute-start | bytes 1572872 | tf_op jit(solution)/shard_map/ppermute | solution.py:723
  371.2 26.3 %collective-permute-start.78 = (bf16[256,1024]{1,0:T(8,128)(2,1)S(1)}, bf16[256,1024]{1,0:T(8,128)(2,1)S(1)}, u32[]{:S(2)}, u32[]{:S(2)}) collective-permute-start(bf16[256,1024]{1,0:T(8,128)(2,1)S(1)} %add_convert_fusion.1.refs_5_.refs_1_), channel_id=1, source_target_pairs={{0,2},{1,3},{2,0},{3,1},{4,6},{5,7},{6,4},{7,5},{8,10},{9,11},{10,... | collective-permute-start | bytes 1572872 | tf_op jit(solution)/shard_map/ppermute | solution.py:723
  393.9 23.3 %collective-permute-start.82 = (bf16[2,128,512]{2,1,0:T(8,128)(2,1)}, bf16[2,128,512]{2,1,0:T(8,128)(2,1)}, u32[]{:S(2)}, u32[]{:S(2)}) collective-permute-start(bf16[2,128,512]{2,1,0:T(8,128)(2,1)} %select_bitcast_fusion.12), channel_id=1, source_target_pairs={{0,16},{4,20},{8,24},{12,28},{16,0},{20,4},{24,8},{28,12},{1,17},{... | collective-permute-start | bytes 786440 | tf_op jit(solution)/shard_map/ppermute | solution.py:723
  395.6 21.6 %collective-permute-start.81 = (bf16[2,128,512]{2,1,0:T(8,128)(2,1)}, bf16[2,128,512]{2,1,0:T(8,128)(2,1)}, u32[]{:S(2)}, u32[]{:S(2)}) collective-permute-start(bf16[2,128,512]{2,1,0:T(8,128)(2,1)} %select_bitcast_fusion.13), channel_id=1, source_target_pairs={{0,8},{4,12},{8,0},{12,4},{16,24},{20,28},{24,16},{28,20},{1,9},{5... | collective-permute-start | bytes 786440 | tf_op jit(solution)/shard_map/ppermute | solution.py:723
  397.4 13.7 %collective-permute-start.83 = (bf16[256,1024]{1,0:T(8,128)(2,1)S(1)}, bf16[256,1024]{1,0:T(8,128)(2,1)S(1)}, u32[]{:S(2)}, u32[]{:S(2)}) collective-permute-start(bf16[256,1024]{1,0:T(8,128)(2,1)S(1)} %add_convert_fusion.refs_12_.refs_1_), channel_id=1, source_target_pairs={{0,2},{1,3},{2,0},{3,1},{4,6},{5,7},{6,4},{7,5},{8,10},{9,11},{10,... | collective-permute-start | bytes 1572872 | tf_op jit(solution)/shard_map/ppermute | solution.py:723
  402.3 9.8 %collective-permute-start.80 = (bf16[128,1024]{1,0:T(8,128)(2,1)}, bf16[128,1024]{1,0:T(8,128)(2,1)S(1)}, u32[]{:S(2)}, u32[]{:S(2)}) collective-permute-start(bf16[128,1024]{1,0:T(8,128)(2,1)} %get-tuple-element.373), channel_id=1, source_target_pairs={{0,1},{1,0},{2,3},{3,2},{4,5},{5,4},{6,7},{7,6},{8,9},{9,8},{10,11... | collective-permute-start | bytes 786440 | tf_op jit(solution)/shard_map/ppermute | solution.py:723
  402.3 8.8 %collective-permute-start.79 = (bf16[128,1024]{1,0:T(8,128)(2,1)}, bf16[128,1024]{1,0:T(8,128)(2,1)}, u32[]{:S(2)}, u32[]{:S(2)}) collective-permute-start(bf16[128,1024]{1,0:T(8,128)(2,1)} %get-tuple-element.374), channel_id=1, source_target_pairs={{0,1},{1,0},{2,3},{3,2},{4,5},{5,4},{6,7},{7,6},{8,9},{9,8},{10,11... | collective-permute-start | bytes 786440 | tf_op jit(solution)/shard_map/ppermute | solution.py:723
  419.2 62.1 %collective-permute-start.96 = (bf16[128,512]{1,0:T(8,128)(2,1)}, bf16[128,512]{1,0:T(8,128)(2,1)}, u32[]{:S(2)}, u32[]{:S(2)}) collective-permute-start(bf16[128,512]{1,0:T(8,128)(2,1)} %select_bitcast_fusion.20), channel_id=1, source_target_pairs={{0,4},{4,0},{8,12},{12,8},{16,20},{20,16},{24,28},{28,24},{1,5},{5... | collective-permute-start | bytes 393224 | tf_op jit(solution)/shard_map/ppermute | solution.py:723
  424.3 5.6 collective-permute-start.85
  453.2 14.3 %collective-permute-start.94 = (bf16[256,1024]{1,0:T(8,128)(2,1)S(1)}, bf16[256,1024]{1,0:T(8,128)(2,1)S(1)}, u32[]{:S(2)}, u32[]{:S(2)}) collective-permute-start(bf16[256,1024]{1,0:T(8,128)(2,1)S(1)} %select_convert_fusion), channel_id=1, source_target_pairs={{0,2},{1,3},{2,0},{3,1},{4,6},{5,7},{6,4},{7,5},{8,10},{9,11},{10,... | collective-permute-start | bytes 1572872 | tf_op jit(solution)/shard_map/ppermute | solution.py:723
  455.7 23.7 %collective-permute-start.87 = (bf16[2,2,128,640]{3,2,1,0:T(8,128)(2,1)}, bf16[2,2,128,640]{3,2,1,0:T(8,128)(2,1)}, u32[]{:S(2)}, u32[]{:S(2)}) collective-permute-start(bf16[2,2,128,640]{3,2,1,0:T(8,128)(2,1)} %select_bitcast_fusion), channel_id=1, source_target_pairs={{0,8},{4,12},{8,0},{12,4},{16,24},{20,28},{24,16},{28,20},{1,9},{5... | collective-permute-start | bytes 1966088 | tf_op jit(solution)/shard_map/ppermute | solution.py:723
  456.6 24.7 %collective-permute-start.86 = (bf16[2,2,128,640]{3,2,0,1:T(8,128)(2,1)}, bf16[2,2,128,640]{3,2,0,1:T(8,128)(2,1)}, u32[]{:S(2)}, u32[]{:S(2)}) collective-permute-start(bf16[2,2,128,640]{3,2,0,1:T(8,128)(2,1)} %select_bitcast_fusion.1), channel_id=1, source_target_pairs={{0,4},{4,0},{8,12},{12,8},{16,20},{20,16},{24,28},{28,24},{1,5},{5... | collective-permute-start | bytes 1966088 | tf_op jit(solution)/shard_map/ppermute | solution.py:723
  457.2 24.1 %collective-permute-start.95 = (bf16[128,512]{1,0:T(8,128)(2,1)S(1)}, bf16[128,512]{1,0:T(8,128)(2,1)}, u32[]{:S(2)}, u32[]{:S(2)}) collective-permute-start(bf16[128,512]{1,0:T(8,128)(2,1)S(1)} %select_bitcast_fusion.21), channel_id=1, source_target_pairs={{0,16},{4,20},{8,24},{12,28},{16,0},{20,4},{24,8},{28,12},{1,17},{... | collective-permute-start | bytes 393224 | tf_op jit(solution)/shard_map/ppermute | solution.py:723
  483.5 16.0 %collective-permute-start.90 = (bf16[2,128,640]{2,1,0:T(8,128)(2,1)}, bf16[2,128,640]{2,1,0:T(8,128)(2,1)}, u32[]{:S(2)}, u32[]{:S(2)}) collective-permute-start(bf16[2,128,640]{2,1,0:T(8,128)(2,1)} %select_bitcast_fusion.8), channel_id=1, source_target_pairs={{0,16},{4,20},{8,24},{12,28},{16,0},{20,4},{24,8},{28,12},{1,17},{... | collective-permute-start | bytes 983048 | tf_op jit(solution)/shard_map/ppermute | solution.py:723
  486.7 15.5 %collective-permute-start.88 = (bf16[2,128,640]{2,1,0:T(8,128)(2,1)S(1)}, bf16[2,128,640]{2,1,0:T(8,128)(2,1)}, u32[]{:S(2)}, u32[]{:S(2)}) collective-permute-start(bf16[2,128,640]{2,1,0:T(8,128)(2,1)S(1)} %select_bitcast_fusion.9), channel_id=1, source_target_pairs={{0,8},{4,12},{8,0},{12,4},{16,24},{20,28},{24,16},{28,20},{1,9},{5... | collective-permute-start | bytes 983048 | tf_op jit(solution)/shard_map/ppermute | solution.py:723
  500.6 11.2 %collective-permute-start.91 = (bf16[128,640]{1,0:T(8,128)(2,1)S(1)}, bf16[128,640]{1,0:T(8,128)(2,1)S(1)}, u32[]{:S(2)}, u32[]{:S(2)}) collective-permute-start(bf16[128,640]{1,0:T(8,128)(2,1)S(1)} %select_bitcast_fusion.16), channel_id=1, source_target_pairs={{0,4},{4,0},{8,12},{12,8},{16,20},{20,16},{24,28},{28,24},{1,5},{5... | collective-permute-start | bytes 491528 | tf_op jit(solution)/shard_map/ppermute | solution.py:723
  503.4 20.4 %collective-permute-start.89 = (bf16[128,640]{1,0:T(8,128)(2,1)S(1)}, bf16[128,640]{1,0:T(8,128)(2,1)S(1)}, u32[]{:S(2)}, u32[]{:S(2)}) collective-permute-start(bf16[128,640]{1,0:T(8,128)(2,1)S(1)} %select_bitcast_fusion.17), channel_id=1, source_target_pairs={{0,16},{4,20},{8,24},{12,28},{16,0},{20,4},{24,8},{28,12},{1,17},{... | collective-permute-start | bytes 491528 | tf_op jit(solution)/shard_map/ppermute | solution.py:723
  (194 other events, 954.4 us)
Sparse Core Ops, SparseCore 0:
  13.1 125.9 all-gather.2
  141.9 75.9 all-gather.4
  314.5 101.5 reduce-scatter.2
  420.1 104.8 reduce-scatter.4
